TPU v7x, 32 devices: a whole 2x2x4 slice. The times are simulated.
32 devices in a mesh: gx: 4 (over x, core), gy: 8 (over z, y).
Axes of the slice: x: 2, y: 2, z: 4, core: 2. Of those that a mesh axis runs over, the one named last changes fastest.
Arguments:
- air_state: float32 [3, 16, 512, 1024], P(None, None, 'gx', 'gy'), may hold values from -6 to 6
- level_set: float32 [64, 256, 256], P(('gx', 'gy')), may hold values from -3 to 5
- fuel_left: float32 [64, 256, 256], P(('gx', 'gy')), may hold values from 0.2 to 1
- fuel_class: int32 [64, 256, 256], P(('gx', 'gy')), may hold values from 0 to 12
- fuel_props: float32 [5, 13], replicated, may hold values from 0.5 to 2
- blocks: int32 [64, 2], replicated, may hold values from 0 to 31, as said below
- adjacency: int32 [64, 4], replicated, may hold values from -1 to 63, as said below
Outputs:
- air_next: float32 [3, 16, 512, 1024], P(None, None, 'gx', 'gy')
- level_next: float32 [64, 256, 256], P(('gx', 'gy'))
- fuel_next: float32 [64, 256, 256], P(('gx', 'gy'))
- totals: float32 [2], replicated
Inputs may be any that keep to these rules, and one draw needn't show every extreme that they name: Rows are distinct; entry [i, 0] is below 16 and entry [i, 1] below 32; block i's fire cells lie on device i // 2 of gx+gy; at most 4 blocks lie on the 128 x 128 atmosphere columns of one device, and in every draw some device's columns hold exactly that many. `adjacency`: entry [i, s] is the list index of the burning block one block row above (s = 0), below (1), one block column left (2) or right (3) of block i, and -1 where that block is not in the list.
All inputs are finite; a program needn't handle non-finite values.
Results may differ from a plain program's by a relative error of at most 0.00005.
Values sent between devices are 32-bit elements; how exact they have to be, the bound alone decides.
No kernel may reach another device: no remote copies, remote signals or barrier semaphores. Data moves between devices by JAX's collectives and lax.ppermute only.
A program may use at most 128 MiB of HBM per device.

v0:
```python
import jax
import jax.numpy as jnp
from jax import lax
from jax.sharding import PartitionSpec as P

REF = 8
BA = 32
SUB = 10


step_time = 0.25
smoothing = 0.15
floor_square = 0.25
viscosity = 0.1
courant = 0.25
mixing = 0.1
heating = 2.0


def with_halo(block, sides, width):
    for axis, dim in sides:
        count = lax.axis_size(axis)
        forward = [(i, i + 1) for i in range(count - 1)]
        backward = [(target, source) for source, target in forward]
        low = lax.ppermute(
            lax.slice_in_dim(block, block.shape[dim] - width, None, axis=dim), axis, forward
        )
        high = lax.ppermute(lax.slice_in_dim(block, 0, width, axis=dim), axis, backward)
        block = jnp.concatenate([low, block, high], axis=dim)
    return block


def edges_of(current):
    return jnp.stack(
        [current[:, 0, :], current[:, -1, :], current[:, :, 0], current[:, :, -1]], axis=1
    )


def cell_table(fuel_class, fuel_props):
    scales = (0.3, 0.3, 4.0, 1.0, 3.0)
    values = [jnp.zeros(fuel_class.shape, jnp.float32) for entry in range(5)]
    for kind in range(fuel_props.shape[1]):
        match = fuel_class == kind
        values = [jnp.where(match, fuel_props[entry, kind], values[entry]) for entry in range(5)]
    return tuple((scales[entry] * values[entry] for entry in range(5)))


def advance(current, remaining, released, emitted, ghosts, wind_rows, wind_cols, table):
    base_rate, wind_factor, burn_time, heat_content, emission = table
    north = jnp.concatenate([ghosts[:, 0, None, :], current[:, :-1, :]], axis=1)
    south = jnp.concatenate([current[:, 1:, :], ghosts[:, 1, None, :]], axis=1)
    west = jnp.concatenate([ghosts[:, 2, :, None], current[:, :, :-1]], axis=2)
    east = jnp.concatenate([current[:, :, 1:], ghosts[:, 3, :, None]], axis=2)
    grad_rows = 0.5 * (south - north)
    grad_cols = 0.5 * (east - west)
    laplace = north + south + west + east - 4.0 * current
    length = jnp.sqrt(grad_rows * grad_rows + grad_cols * grad_cols + floor_square)
    along = (wind_rows * grad_rows + wind_cols * grad_cols) / length
    soft = jax.nn.softplus(along)
    spread = base_rate * (1.0 + wind_factor * soft * jnp.sqrt(soft))
    updated = current - step_time * spread * length + smoothing * laplace
    burning = 0.5 * (1.0 - jnp.tanh(updated))
    new_fuel = remaining * jnp.exp(-step_time * burning / burn_time)
    spent = remaining - new_fuel
    return (updated, new_fuel, released + heat_content * spent, emitted + emission * spent)


def air_update(air_state):
    padded = with_halo(air_state, (("gx", 2), ("gy", 3)), 1)
    north = padded[:, :, :-2, 1:-1]
    south = padded[:, :, 2:, 1:-1]
    west = padded[:, :, 1:-1, :-2]
    east = padded[:, :, 1:-1, 2:]
    upper = jnp.concatenate([air_state[:, 1:], jnp.zeros_like(air_state[:, :1])], axis=1)
    lower = jnp.concatenate([jnp.zeros_like(air_state[:, :1]), air_state[:, :-1]], axis=1)
    wind_rows = air_state[0][None]
    wind_cols = air_state[1][None]
    laplace = north + south + west + east - 4.0 * air_state
    advect = wind_rows * (0.5 * (south - north)) + wind_cols * (0.5 * (east - west))
    return (
        air_state
        + viscosity * laplace
        - courant * advect
        + mixing * (upper + lower - 2.0 * air_state)
    )


def local(air_state, level_set, fuel_left, fuel_class, fuel_props, blocks, adjacency):
    local_count = level_set.shape[0]
    edge_cells = level_set.shape[1]
    total_blocks = blocks.shape[0]
    across = lax.axis_size("gy")
    device_rank = lax.axis_index("gx") * across + lax.axis_index("gy")
    rows_here = air_state.shape[2]
    cols_here = air_state.shape[3]
    tile_rows = rows_here // BA
    tile_cols = cols_here // BA
    block_row = blocks[:, 0] - lax.axis_index("gx") * tile_rows
    block_col = blocks[:, 1] - lax.axis_index("gy") * tile_cols
    inside = (block_row >= 0) & (block_row < tile_rows) & (block_col >= 0) & (block_col < tile_cols)
    position = block_row * tile_cols + block_col
    slots = jnp.arange(tile_rows * tile_cols, dtype=jnp.int32)
    placing = jnp.where(inside[:, None] & (position[:, None] == slots[None, :]), 1.0, 0.0).astype(
        jnp.float32
    )
    own_start = device_rank * local_count
    capacity = 2 * local_count
    listed = jnp.arange(total_blocks, dtype=jnp.int32)
    tile_of = blocks[:, 0] // tile_rows * across + blocks[:, 1] // tile_cols
    same_tile = (tile_of[:, None] == tile_of[None, :]) & (listed[:, None] > listed[None, :])
    slot_of = jnp.sum(same_tile.astype(jnp.int32), axis=1)
    capacity_ids = jnp.arange(capacity, dtype=jnp.int32)
    selecting = jnp.where(
        inside[None, :] & (slot_of[None, :] == capacity_ids[:, None]), 1.0, 0.0
    ).astype(jnp.float32)
    packing = jnp.dot(
        selecting, placing, precision=lax.Precision.HIGHEST, preferred_element_type=jnp.float32
    )
    surface = (
        air_state[0:2, 0]
        .reshape(2, tile_rows, BA, tile_cols, BA)
        .transpose(1, 3, 0, 2, 4)
        .reshape(tile_rows * tile_cols, 2 * BA * BA)
    )
    packed = jnp.dot(
        packing, surface, precision=lax.Precision.HIGHEST, preferred_element_type=jnp.float32
    )
    every_wind = lax.all_gather(packed, ("gx", "gy"), axis=0, tiled=True)
    own_tiles = lax.dynamic_slice_in_dim(tile_of, own_start, local_count, 0)
    own_slots = lax.dynamic_slice_in_dim(slot_of, own_start, local_count, 0)
    wanted = own_tiles * capacity + own_slots
    block_wind = jnp.take(every_wind, wanted, axis=0)
    block_wind = block_wind.reshape(local_count, 2, BA, 1, BA, 1)
    fine_wind = jnp.broadcast_to(block_wind, (local_count, 2, BA, REF, BA, REF)).reshape(
        local_count, 2, edge_cells, edge_cells
    )
    wind_rows = fine_wind[:, 0]
    wind_cols = fine_wind[:, 1]
    air_next = air_update(air_state)
    table = cell_table(fuel_class, fuel_props)
    neighbours = lax.dynamic_slice_in_dim(adjacency, own_start, local_count, 0)
    facing = jnp.array([1, 0, 3, 2], dtype=jnp.int32)
    picked_rows = jnp.maximum(neighbours, 0) * 4 + facing[None, :]

    def substep(index, carry):
        current, remaining, released, emitted = carry
        own_edges = edges_of(current)
        along_cols = lax.all_gather(own_edges, "gy", axis=0, tiled=True)
        every_edge = lax.all_gather(along_cols, "gx", axis=0, tiled=True)
        edge_rows = every_edge.reshape(total_blocks * 4, edge_cells)
        ghosts = jnp.where(
            neighbours[:, :, None] >= 0, jnp.take(edge_rows, picked_rows, axis=0), own_edges
        )
        return advance(current, remaining, released, emitted, ghosts, wind_rows, wind_cols, table)

    blank = jnp.zeros(level_set.shape, jnp.float32)
    final_set, final_fuel, released, emitted = lax.fori_loop(
        0, SUB, substep, (level_set, fuel_left, blank, blank)
    )
    burning = 0.5 * (1.0 - jnp.tanh(final_set))
    column_heat = heating * released.reshape(local_count, BA, REF, BA, REF).mean(axis=(2, 4))
    every_heat = lax.all_gather(
        column_heat.reshape(local_count, BA * BA), ("gx", "gy"), axis=0, tiled=True
    )
    tile_heat = jnp.dot(
        placing.T, every_heat, precision=lax.Precision.HIGHEST, preferred_element_type=jnp.float32
    )
    tile_heat = (
        tile_heat.reshape(tile_rows, tile_cols, BA, BA)
        .transpose(0, 2, 1, 3)
        .reshape(rows_here, cols_here)
    )
    air_next = air_next.at[2, 0].add(tile_heat)
    burned_sum, emitted_sum = lax.psum((jnp.sum(burning), jnp.sum(emitted)), ("gx", "gy"))
    cells = total_blocks * edge_cells * edge_cells
    totals = jnp.stack([burned_sum / cells, emitted_sum / cells])
    return (air_next, final_set, final_fuel, totals)


def solution(mesh):
    in_specs = (
        P(None, None, "gx", "gy"),
        P(("gx", "gy"), None, None),
        P(("gx", "gy"), None, None),
        P(("gx", "gy"), None, None),
        P(),
        P(),
        P(),
    )
    out_specs = (
        P(None, None, "gx", "gy"),
        P(("gx", "gy"), None, None),
        P(("gx", "gy"), None, None),
        P(),
    )
    return jax.shard_map(local, mesh=mesh, in_specs=in_specs, out_specs=out_specs, check_vma=False)
```

profile of v0, /device:TPU:0, one launch (start us, length us, event | category | flops | bytes accessed | tf_op | source)
XLA Modules:
  0.0 727.6 jit_solution(16149101431209257403)
XLA Ops:
  12.4 1.9 copy.168
  14.3 1.3 reshape.198
  17.9 2.4 collective-permute-start
  20.3 1.3 collective-permute-start.1
  21.6 2.1 fusion.36
  23.7 1.7 fusion.39
  25.3 2.1 fusion.37
  27.5 2.1 fusion.38
  29.6 3.3 fusion.35
  32.9 1.5 multiply_bitcast_fusion.1
  34.4 2.0 copy.144
  36.6 11.0 %select_multiply_fusion = (f32[2,256,256]{1,2,0:T(8,128)}, pred[2,256,256]{1,2,0:T(8,128)(4,1)S(1)}, pred[2,256,256]{1,2,0:T(8,128)(4,1)S(1)}, pred[2,256,256]{1...) fusion(f32[]{:T(128)} %bitcast.75, f32[]{:T(128)} %bitcast.74, ...), kind=kLoop, calls=%fused_computation.39 | loop fusion | flops 3538944 | bytes 2752564 | tf_op jit(solution)/shard_map/mul | solution.py:45
  47.6 9.6 %select_multiply_fusion.1 = f32[2,256,256]{1,2,0:T(8,128)} fusion(pred[2,256,256]{1,2,0:T(8,128)(4,1)S(1)} %get-tuple-element.377, pred[2,256,256]{1,2,0:T(8,128)(4,1)S(1)} %get-tuple-element.376, pred[2,256,256]{1,2,0:T(8,128)(4,1)S(1)} %get-tuple-element.375, pred[2,256,256]{1,2,0:T(8,128)(4,1)S(1)} %get-tuple-element.374, ...), kind=kLoop, calls=%fused_computation.41 | loop fusion | flops 1835008 | bytes 2228276 | tf_op jit(solution)/shard_map/mul | solution.py:45
  57.2 9.6 %select_multiply_fusion.2 = f32[2,256,256]{1,2,0:T(8,128)} fusion(pred[2,256,256]{1,2,0:T(8,128)(4,1)S(1)} %get-tuple-element.377, pred[2,256,256]{1,2,0:T(8,128)(4,1)S(1)} %get-tuple-element.376, pred[2,256,256]{1,2,0:T(8,128)(4,1)S(1)} %get-tuple-element.375, pred[2,256,256]{1,2,0:T(8,128)(4,1)S(1)} %get-tuple-element.374, ...), kind=kLoop, calls=%fused_computation.42 | loop fusion | flops 1835008 | bytes 2228276 | tf_op jit(solution)/shard_map/mul | solution.py:45
  66.8 9.7 %select_select_fusion.1 = f32[2,256,256]{1,2,0:T(8,128)} fusion(pred[2,256,256]{1,2,0:T(8,128)(4,1)S(1)} %get-tuple-element.377, pred[2,256,256]{1,2,0:T(8,128)(4,1)S(1)} %get-tuple-element.376, pred[2,256,256]{1,2,0:T(8,128)(4,1)S(1)} %get-tuple-element.375, pred[2,256,256]{1,2,0:T(8,128)(4,1)S(1)} %get-tuple-element.374, ...), kind=kLoop, calls=%fused_computation.40 | loop fusion | flops 1703936 | bytes 2228276 | tf_op jit(solution)/shard_map/jit(_where)/select_n | solution.py:44
  76.4 9.6 %select_multiply_fusion.3 = f32[2,256,256]{1,2,0:T(8,128)} fusion(pred[2,256,256]{1,2,0:T(8,128)(4,1)S(1)} %get-tuple-element.377, pred[2,256,256]{1,2,0:T(8,128)(4,1)S(1)} %get-tuple-element.376, pred[2,256,256]{1,2,0:T(8,128)(4,1)S(1)} %get-tuple-element.375, pred[2,256,256]{1,2,0:T(8,128)(4,1)S(1)} %get-tuple-element.374, ...), kind=kLoop, calls=%fused_computation.43 | loop fusion | flops 1835008 | bytes 2228276 | tf_op jit(solution)/shard_map/mul | solution.py:45
  86.6 2.8 fusion.33
  89.4 3.2 copy.138
  92.6 4.2 collective-permute-start.2
  96.9 2.6 copy.140
  99.5 1.5 collective-permute-start.3
  103.5 2.4 copy.139
  105.9 2.4 copy.141
  108.3 14.0 %multiply_add_fusion.1 = f32[3,16,128,128]{3,2,1,0:T(8,128)} fusion(f32[3,16,128,128]{3,2,1,0:T(8,128)} %param.12, f32[3,15,128,128]{3,2,1,0:T(8,128)} %get-tuple-element.401, f32[3,15,128,128]{3,2,1,0:T(8,128)} %get-tuple-element.400, f32[3,16,130,1]{3,2,1,0:T(8,128)} %copy.141, f32[3,16,1,128]{3,2,1,0:T(1,128)S(1)} %collective-permute-done.1, ...), kind=kLoop, calls=%fused_computation.31 | loop fusion | flops 21233664 | bytes 14385920 | tf_op jit(solution)/shard_map/add | solution.py:81
  122.3 1.6 reshape.222
  124.6 7.9 %broadcast_in_dim.276 = f32[2,2,32,8,32,8]{5,4,3,2,1,0:T(8,128)} broadcast(f32[2,2,32,32]{3,2,1,0:T(8,128)S(1)} %broadcast_select_fusion), dimensions={0,1,2,4} | broadcast | bytes 1064960 | tf_op jit(solution)/shard_map/broadcast_in_dim | solution.py:134
  132.6 12.7 %reshape.199 = f32[2,2,256,256]{3,2,1,0:T(8,128)S(1)} reshape(f32[2,2,32,8,32,8]{5,4,3,2,1,0:T(8,128)} %broadcast_in_dim.276) | data formatting | bytes 2097152 | tf_op jit(solution)/shard_map/reshape | solution.py:134
  147.3 446.6 %while.20 = (s32[]{:T(128)}, f32[2,256,256]{1,2,0:T(8,128)S(1)}, f32[2,256,256]{1,2,0:T(8,128)S(1)}, f32[2,256,256]{1,2,0:T(8,128)}, f32[2,256,256]{1,2,0:T(8,12...) while((s32[]{:T(128)}, f32[2,256,256]{1,2,0:T(8,128)S(1)}, ...), condition=%wide.region_2.3_spmd.clone, body=%wide.region_1.2_spmd.clone.sunk | while | flops 6308947 | bytes 24621588 | solution.py:157
  147.6 32.9 %all_gather.24 = f32[16,4,256]{2,1,0:T(4,128)S(1)} all-gather(f32[2,4,256]{2,1,0:T(4,128)S(1)} %pad_maximum_fusion.16), channel_id=1, replica_groups=mesh['gx'=4,'gy'=8] {'gy'}, dimensions={0}, use_global_device_ids=true | all-gather | bytes 73728 | tf_op jit(solution)/shard_map/while/body/eval_jaxpr/all_gather | solution.py:148
  180.5 8.2 %all_gather.25 = f32[64,4,256]{2,1,0:T(4,128)S(1)} all-gather(f32[16,4,256]{2,1,0:T(4,128)S(1)} %all_gather.24), channel_id=1, replica_groups=mesh['gx'=4,'gy'=8] {'gx'}, dimensions={0}, use_global_device_ids=true | all-gather | bytes 327680 | tf_op jit(solution)/shard_map/while/body/eval_jaxpr/all_gather | solution.py:149
  191.0 4.2 select_add_fusion.4
  196.5 30.5 %all_gather.24 = f32[16,4,256]{2,1,0:T(4,128)S(1)} all-gather(f32[2,4,256]{2,1,0:T(4,128)S(1)} %pad_maximum_fusion.16), channel_id=1, replica_groups=mesh['gx'=4,'gy'=8] {'gy'}, dimensions={0}, use_global_device_ids=true | all-gather | bytes 73728 | tf_op jit(solution)/shard_map/while/body/eval_jaxpr/all_gather | solution.py:148
  227.0 5.8 all_gather.25
  235.0 4.4 select_add_fusion.4
  240.7 30.5 %all_gather.24 = f32[16,4,256]{2,1,0:T(4,128)S(1)} all-gather(f32[2,4,256]{2,1,0:T(4,128)S(1)} %pad_maximum_fusion.16), channel_id=1, replica_groups=mesh['gx'=4,'gy'=8] {'gy'}, dimensions={0}, use_global_device_ids=true | all-gather | bytes 73728 | tf_op jit(solution)/shard_map/while/body/eval_jaxpr/all_gather | solution.py:148
  271.2 5.8 all_gather.25
  279.2 4.4 select_add_fusion.4
  284.9 30.5 %all_gather.24 = f32[16,4,256]{2,1,0:T(4,128)S(1)} all-gather(f32[2,4,256]{2,1,0:T(4,128)S(1)} %pad_maximum_fusion.16), channel_id=1, replica_groups=mesh['gx'=4,'gy'=8] {'gy'}, dimensions={0}, use_global_device_ids=true | all-gather | bytes 73728 | tf_op jit(solution)/shard_map/while/body/eval_jaxpr/all_gather | solution.py:148
  315.4 5.8 all_gather.25
  323.4 4.4 select_add_fusion.4
  329.1 30.5 %all_gather.24 = f32[16,4,256]{2,1,0:T(4,128)S(1)} all-gather(f32[2,4,256]{2,1,0:T(4,128)S(1)} %pad_maximum_fusion.16), channel_id=1, replica_groups=mesh['gx'=4,'gy'=8] {'gy'}, dimensions={0}, use_global_device_ids=true | all-gather | bytes 73728 | tf_op jit(solution)/shard_map/while/body/eval_jaxpr/all_gather | solution.py:148
  359.6 5.8 all_gather.25
  367.6 4.4 select_add_fusion.4
  373.2 30.5 %all_gather.24 = f32[16,4,256]{2,1,0:T(4,128)S(1)} all-gather(f32[2,4,256]{2,1,0:T(4,128)S(1)} %pad_maximum_fusion.16), channel_id=1, replica_groups=mesh['gx'=4,'gy'=8] {'gy'}, dimensions={0}, use_global_device_ids=true | all-gather | bytes 73728 | tf_op jit(solution)/shard_map/while/body/eval_jaxpr/all_gather | solution.py:148
  403.8 5.8 all_gather.25
  411.8 4.4 select_add_fusion.4
  417.4 30.5 %all_gather.24 = f32[16,4,256]{2,1,0:T(4,128)S(1)} all-gather(f32[2,4,256]{2,1,0:T(4,128)S(1)} %pad_maximum_fusion.16), channel_id=1, replica_groups=mesh['gx'=4,'gy'=8] {'gy'}, dimensions={0}, use_global_device_ids=true | all-gather | bytes 73728 | tf_op jit(solution)/shard_map/while/body/eval_jaxpr/all_gather | solution.py:148
  448.0 5.8 all_gather.25
  456.0 4.4 select_add_fusion.4
  461.6 30.5 %all_gather.24 = f32[16,4,256]{2,1,0:T(4,128)S(1)} all-gather(f32[2,4,256]{2,1,0:T(4,128)S(1)} %pad_maximum_fusion.16), channel_id=1, replica_groups=mesh['gx'=4,'gy'=8] {'gy'}, dimensions={0}, use_global_device_ids=true | all-gather | bytes 73728 | tf_op jit(solution)/shard_map/while/body/eval_jaxpr/all_gather | solution.py:148
  492.2 5.8 all_gather.25
  500.1 4.4 select_add_fusion.4
  505.8 30.5 %all_gather.24 = f32[16,4,256]{2,1,0:T(4,128)S(1)} all-gather(f32[2,4,256]{2,1,0:T(4,128)S(1)} %pad_maximum_fusion.16), channel_id=1, replica_groups=mesh['gx'=4,'gy'=8] {'gy'}, dimensions={0}, use_global_device_ids=true | all-gather | bytes 73728 | tf_op jit(solution)/shard_map/while/body/eval_jaxpr/all_gather | solution.py:148
  536.4 5.8 all_gather.25
  544.3 4.4 select_add_fusion.4
  550.0 30.5 %all_gather.24 = f32[16,4,256]{2,1,0:T(4,128)S(1)} all-gather(f32[2,4,256]{2,1,0:T(4,128)S(1)} %pad_maximum_fusion.16), channel_id=1, replica_groups=mesh['gx'=4,'gy'=8] {'gy'}, dimensions={0}, use_global_device_ids=true | all-gather | bytes 73728 | tf_op jit(solution)/shard_map/while/body/eval_jaxpr/all_gather | solution.py:148
  580.6 5.8 all_gather.25
  588.5 4.4 select_add_fusion.4
  594.7 1.8 reduce_sum.39
  597.5 39.1 %all-reduce.2 = (f32[]{:T(128)}, f32[]{:T(128)}) all-reduce(f32[]{:T(128)} %reduce_sum.39, f32[]{:T(128)} %multiply_reduce_fusion), channel_id=1, replica_groups=mesh['gx'=4,'gy'=8] {'gx','gy'}, use_global_device_ids=true, to_apply=%region_7.8 | all-reduce | flops 2 | bytes 16 | tf_op jit(solution)/shard_map/psum | solution.py:174
  639.1 6.1 reshape.200
  645.3 4.0 reduce_sum.37
  649.4 67.3 %all-gather.1 = f32[32,2,1024]{2,1,0:T(2,128)S(1)} all-gather(f32[1,2,1024]{2,1,0:T(2,128)S(1)} %reshape.223), channel_id=1, replica_groups=mesh['gx'=4,'gy'=8] {'gx','gy'}, dimensions={0}, use_global_device_ids=true | all-gather | bytes 270336 | tf_op jit(solution)/shard_map/all_gather | solution.py:162
  719.3 1.5 fusion
  (307 shorter events, 52.9 us)
Async XLA Ops:
  7.2 29.2 %copy-start = (s32[64,4]{0,1:T(4,128)S(1)}, s32[64,4]{0,1:T(4,128)}, u32[]{:S(2)}) copy-start(s32[64,4]{0,1:T(4,128)} %param.18) | copy-start | bytes 3076
  7.2 22.4 %copy-start.2 = (f32[3,16,128,128]{3,2,1,0:T(8,128)S(1)}, f32[3,16,128,128]{3,2,1,0:T(8,128)}, u32[]{:S(2)}) copy-start(f32[3,16,128,128]{3,2,1,0:T(8,128)} %param.12) | copy-start | bytes 9437188
  7.2 115.1 %all-gather.4.cloned.1.call-start = ((), (), s32[]{:S(2)}) async-start(), calls=%async_computation | async-start | bytes 1081344 | tf_op jit(solution)/shard_map/all_gather | solution.py:128
  17.9 68.3 %collective-permute-start = (f32[3,16,1,128]{3,2,1,0:T(1,128)S(1)}, f32[3,16,1,128]{3,2,1,0:T(1,128)S(1)}, u32[]{:S(2)}, u32[]{:S(2)}) collective-permute-start(f32[3,16,1,128]{3,2,1,0:T(1,128)S(1)} %get-tuple-element.398), channel_id=1, source_target_pairs={{0,8},{8,16},{16,24},{1,9},{9,17},{17,25},{2,10},{10,18},{18,26},{... | collective-permute-start | bytes 73736 | tf_op jit(solution)/shard_map/ppermute | solution.py:25
  20.3 65.9 %collective-permute-start.1 = (f32[3,16,1,128]{3,2,1,0:T(1,128)S(1)}, f32[3,16,1,128]{3,2,1,0:T(1,128)S(1)}, u32[]{:S(2)}, u32[]{:S(2)}) collective-permute-start(f32[3,16,1,128]{3,2,1,0:T(1,128)S(1)} %get-tuple-element.399), channel_id=1, source_target_pairs={{8,0},{16,8},{24,16},{9,1},{17,9},{25,17},{10,2},{18,10},{26,18},{... | collective-permute-start | bytes 73736 | tf_op jit(solution)/shard_map/ppermute | solution.py:28
  57.2 28.9 %copy-start.8 = (s32[4]{0:T(128)S(1)}, s32[4]{0:T(128)}, u32[]{:S(2)}) copy-start(s32[4]{0:T(128)} %constant.220.clone) | copy-start | bytes 52
  92.6 10.9 %collective-permute-start.2 = (f32[3,16,130,1]{2,1,3,0:T(8,128)S(1)}, f32[3,16,130,1]{2,1,3,0:T(8,128)S(1)}, u32[]{:S(2)}, u32[]{:S(2)}) collective-permute-start(f32[3,16,130,1]{2,1,3,0:T(8,128)S(1)} %copy.138), channel_id=1, source_target_pairs={{0,1},{1,2},{2,3},{3,4},{4,5},{5,6},{6,7},{8,9},{9,10},{10,11},{11... | collective-permute-start | bytes 74888 | tf_op jit(solution)/shard_map/ppermute | solution.py:25
  99.5 6.4 collective-permute-start.3
  103.5 4.8 copy-start.6
  103.5 4.8 copy-start.7
  190.9 4.3 copy-start.3
  190.9 4.3 copy-start.4
  195.4 0.8 copy-start.5
  235.0 4.4 copy-start.3
  235.0 4.4 copy-start.4
  239.6 0.8 copy-start.5
  279.2 4.4 copy-start.3
  279.2 4.4 copy-start.4
  283.8 0.8 copy-start.5
  323.4 4.4 copy-start.3
  323.4 4.4 copy-start.4
  328.0 0.8 copy-start.5
  367.5 4.4 copy-start.3
  367.6 4.4 copy-start.4
  372.2 0.8 copy-start.5
  411.7 4.4 copy-start.3
  411.7 4.4 copy-start.4
  416.4 0.8 copy-start.5
  455.9 4.4 copy-start.3
  455.9 4.4 copy-start.4
  460.6 0.8 copy-start.5
  500.1 4.4 copy-start.3
  500.1 4.4 copy-start.4
  504.8 0.8 copy-start.5
  544.3 4.4 copy-start.3
  544.3 4.4 copy-start.4
  549.0 0.8 copy-start.5
  588.5 4.4 copy-start.3
  588.5 4.4 copy-start.4
  593.2 0.8 copy-start.5
  645.3 75.5 %copy-start.1 = (s32[64,4]{0,1:T(4,128)S(1)}, s32[64,4]{0,1:T(4,128)}, u32[]{:S(2)}) copy-start(s32[64,4]{0,1:T(4,128)} %param.18) | copy-start | bytes 3076
Sparse Core Ops, SparseCore 0:
  16.9 56.4 all-gather.3
where the time goes:
time: 730 us; the launch traced here: 728 us
  blocking collectives  474 us (65%)
  other arithmetic  125 us (17%)
  local copies, waits for them, and re-layouts  101 us (14%)
  between operations  15.6 us (2%)
  starting transfers between devices  9.43 us (1%)
    all_gather x10, blocking collectives, substep(): along_cols = lax.all_gather(own_edges, 'gy', axis=0, tiled=True)  308 us
    all_gather x1, blocking collectives, local(): lax.all_gather(column_heat.reshape(local_count, BA * BA), ('gx', 'gy'), a...  67.3 us
    all_gather x10, blocking collectives, substep(): every_edge = lax.all_gather(along_cols, 'gx', axis=0, tiled=True)  60.1 us
    add x10, other arithmetic, advance(): emitted + emission * spent  43.8 us
    mul x4, other arithmetic, cell_table(): return tuple((scales[entry] * values[entry] for entry in range(5)))  39.8 us
    psum x1, blocking collectives, local(): lax.psum((jnp.sum(burning), jnp.sum(emitted)), ('gx', 'gy'))  39.1 us
  transfers between devices with their start and end apart: 5, of which 0 were waited for; matrix products, arithmetic and copies ran while one was open for 13% of the time, Pallas kernels for 0%

commit v1 on v0

v1 whole, which is shorter than its diff:
```python
import math

import jax
import jax.numpy as jnp
from jax import lax
from jax.experimental import pallas as pl
from jax.experimental.pallas import tpu as pltpu
from jax.sharding import PartitionSpec as P


REF = 8
BA = 32
SUB = 10
PIECES = 32
LANES = 128

step_time = 0.25
smoothing = 0.15
floor_square = 0.25
viscosity = 0.1
courant = 0.25
mixing = 0.1
heating = 2.0

SIDE = 0
CORNER = 10
WIND = 12
COLS = 16
ROWS = 20
REC1 = 24
CORNER2 = 10
WINDA = 11
WINDB = 13
COLS2 = 15
ROWS2 = 19
REC2 = 24
HEAT_ROWS = 17

TOP = 8
EXT = 304
FIRST = 24

f32 = jnp.float32
i32 = jnp.int32


def lanes(shape=(8, LANES)):
    return lax.broadcasted_iota(i32, shape, len(shape) - 1)


def rolled(x, shift):
    return pltpu.roll(x, shift % LANES, x.ndim - 1)


def opposite(side):
    return (1, 0, 3, 2)[side]


def pick(table, index):
    return jnp.take_along_axis(table, index, axis=1, mode="promise_in_bounds")


def pack_kernel(pos, blocks, level, fuel_class, air_hbm, out, air, strip, edge, sem):
    load = pltpu.make_async_copy(air_hbm, air, sem)
    load.start()
    lane256 = lanes((256, LANES))
    lane16 = lanes((16, LANES))

    def place(row, first, values):
        out[pl.ds(first * REC1 + row, values.shape[0], stride=REC1), :] = values

    for q in range(2):
        fields = (level[q], fuel_class[q].astype(f32))
        turned = [
            jnp.where(lane256 < 64, field[:, :LANES], field[:, LANES:]).T for field in fields
        ]
        for side in range(4):
            for number, (field, turn) in enumerate(zip(fields, turned)):
                if side == 0:
                    rows = field[0:SUB, :]
                elif side == 1:
                    rows = field[256 - SUB : 256, :]
                elif side == 2:
                    rows = turn[0:SUB, :]
                else:
                    rows = turn[LANES - SUB : LANES, :]
                strip[side, 2 * SUB * number : 2 * SUB * number + SUB, :] = rows[:, :LANES]
                strip[side, 2 * SUB * number + SUB : 2 * SUB * (number + 1), :] = rows[:, LANES:]
            place(SIDE + q * 5 + side, 0, strip[side, 0:32, :])
            place(SIDE + q * 5 + 4, 8 * side, strip[side, 32:40, :])
        for number, field in enumerate(fields):
            half = jnp.where(
                lane16 < 16,
                field[240:256, :LANES],
                jnp.where(
                    lane16 < 32,
                    rolled(field[0:16, :LANES], 16),
                    jnp.where(
                        lane16 < 48,
                        rolled(field[0:16, LANES:], 48),
                        rolled(field[240:256, LANES:], 64),
                    ),
                ),
            )
            place(CORNER + q, 16 * number, jnp.where(lane16 < 64, half, rolled(half, 64)))

    load.wait()
    blank = jnp.zeros((PIECES, LANES), f32)
    for slot in range(4):
        place(WIND + slot, 0, blank)
    lane32 = lanes((32, LANES))
    tile_rows = 128 // BA

    def find(j, count):
        row = blocks[j, 0] - pos[0] * tile_rows
        col = blocks[j, 1] - pos[1] * tile_rows
        inside = (row >= 0) & (row < tile_rows) & (col >= 0) & (col < tile_rows)

        @pl.when(inside)
        def _():
            start = pl.multiple_of(row * BA, BA)
            u = air[pl.ds(start, BA), :]
            v = air[pl.ds(16 * 128 + start, BA), :]
            shift = LANES - col * BA
            u = pltpu.roll(u, shift, 1)
            v = pltpu.roll(v, shift, 1)
            half = jnp.where(lane32 < 32, u, rolled(v, 32))
            both = jnp.where(lane32 < 64, half, rolled(half, 64))
            out[pl.ds(WIND + count, PIECES, stride=REC1), :] = both

        return count + inside.astype(i32)

    lax.fori_loop(0, blocks.shape[0], find, jnp.int32(0))

    edge[0:48, :] = air[pl.ds(127, 48, stride=128), :]
    edge[48:96, :] = air[pl.ds(0, 48, stride=128), :]
    for group in range(3):
        place(ROWS + group, 0, edge[32 * group : 32 * group + 32, :])

    lane8 = lanes()

    def columns(chunk, carry):
        base = pl.multiple_of(chunk * 8, 8)
        total = jnp.zeros((8, LANES), f32)
        for plane in range(48):
            x = air[pl.ds(plane * 128 + base, 8), :]
            total = jnp.where(lane8 // 2 == plane, rolled(x, 1 + 2 * plane), total)
        edge[pl.ds(base, 8), :] = total
        return carry

    lax.fori_loop(0, 16, columns, 0)
    for group in range(4):
        place(COLS + group, 0, edge[32 * group : 32 * group + 32, :])
    if out.shape[0] > PIECES * REC1:
        out[PIECES * REC1 :, :] = jnp.zeros((out.shape[0] - PIECES * REC1, LANES), f32)


def select_kernel(across, down, pos, blocks, adjacency, received, out, wind_row, count):
    total = blocks.shape[0]
    devices = across * down
    relay = jnp.minimum(pos[0] * across + pos[1], PIECES - 1)
    lane1 = lanes((1, LANES))
    tile_rows = 128 // BA

    def clear(d, carry):
        count[d] = 0
        return carry

    lax.fori_loop(0, devices, clear, 0)

    def number(j, carry):
        tile = (blocks[j, 0] // tile_rows) * across + blocks[j, 1] // tile_rows
        slot = count[tile]
        count[tile] = slot + 1
        wind_row[j] = tile * REC1 + WIND + slot
        return carry

    lax.fori_loop(0, total, number, 0)

    def take(index):
        return received[pl.ds(index, 1), :]

    spare_side = relay // 8
    upper = relay >= 16
    lane_col = lane1 % 32 < 16
    first_half = lane1 < 64
    quarter = lane1 // 16

    def serve(d, carry):
        base = d * REC2

        def put(row, value):
            out[pl.ds(base + row, 1), :] = value

        corner_rows = []
        for q in range(2):
            i = 2 * d + q
            near = [adjacency[i, s] for s in range(4)]
            safe = [jnp.maximum(near[s], 0) for s in range(4)]

            def diagonal(s, t):
                by_row = adjacency[safe[s], t]
                by_col = adjacency[safe[t], s]
                return jnp.maximum(jnp.where(near[s] >= 0, by_row, jnp.where(near[t] >= 0, by_col, 0)), 0)

            nw, ne, sw, se = diagonal(0, 2), diagonal(0, 3), diagonal(1, 2), diagonal(1, 3)

            def side_row(j, s):
                return (j // 2) * REC1 + SIDE + (j % 2) * 5 + s

            def corner_row(j):
                return (j // 2) * REC1 + CORNER + j % 2

            for s in range(4):
                put(SIDE + q * 5 + s, take(side_row(safe[s], opposite(s))))
            spare = jnp.where(
                spare_side == 0,
                safe[1],
                jnp.where(spare_side == 1, safe[0], jnp.where(spare_side == 2, safe[3], safe[2])),
            )
            put(SIDE + q * 5 + 4, take(side_row(spare, 4)))
            corner_rows += [take(corner_row(j)) for j in (ne, se, sw, nw)]
            put(
                WINDA + q,
                jnp.where(
                    first_half,
                    take(wind_row[i]),
                    take(wind_row[jnp.where(upper, safe[0], safe[1])]),
                ),
            )
            east = take(wind_row[safe[3]])
            west = take(wind_row[safe[2]])
            corner_east = take(wind_row[jnp.where(upper, ne, se)])
            corner_west = take(wind_row[jnp.where(upper, nw, sw)])
            put(
                WINDB + q,
                jnp.where(
                    lane_col,
                    jnp.where(first_half, east, corner_east),
                    jnp.where(first_half, west, corner_west),
                ),
            )
        merged = corner_rows[7]
        for k in range(7):
            merged = jnp.where(quarter == k, corner_rows[k], merged)
        put(CORNER2, merged)
        a = d // across
        b = d % across
        north = jnp.where(a > 0, d - across, d)
        south = jnp.where(a < down - 1, d + across, d)
        west_tile = jnp.where(b > 0, d - 1, d)
        east_tile = jnp.where(b < across - 1, d + 1, d)
        odd = lane1 % 2 == 1
        for group in range(4):
            put(
                COLS2 + group,
                jnp.where(
                    odd,
                    take(east_tile * REC1 + COLS + group),
                    take(west_tile * REC1 + COLS + group),
                ),
            )
        put(ROWS2, take(north * REC1 + ROWS))
        put(ROWS2 + 1, take(jnp.where(relay < 16, north, south) * REC1 + ROWS + 1))
        put(ROWS2 + 2, take(south * REC1 + ROWS + 2))
        for row in range(ROWS2 + 3, REC2):
            put(row, jnp.zeros((1, LANES), f32))
        return carry

    lax.fori_loop(0, devices, serve, 0)


MAIN = (0, 1, 3, 4)


def fire_kernel(
    across,
    down,
    pos,
    adjacency,
    props,
    received,
    level,
    fuel_left,
    fuel_class,
    air_hbm,
    level_out,
    fuel_out,
    heat_out,
    air_out,
    cur,
    base_rate,
    wind_rate,
    wind,
    strips,
    turned,
    tanh_sum,
    links,
    row_heat,
    air,
    air_new,
    sem_in,
    sem_out,
):
    load = pltpu.make_async_copy(air_hbm, air.at[:, 1:17, 8:136, :], sem_in)
    load.start()
    lane = lanes()
    sub = lax.broadcasted_iota(i32, (8, LANES), 0)
    lane32 = lanes((32, LANES))
    own = 2 * (pos[0] * across + pos[1])

    def got(row, first=0, size=PIECES):
        return received[pl.ds(first * REC2 + row, size, stride=REC2), :]

    table_base = jnp.broadcast_to(0.125 * 0.3 * props[0:1, :], (8, LANES))
    table_wind = table_base * jnp.broadcast_to(0.3 * props[1:2, :], (8, LANES))
    log2e = math.log2(math.e)
    table_burn = jnp.broadcast_to((-0.5 * step_time * log2e / 4.0) / props[2:3, :], (8, LANES))
    table_heat = jnp.broadcast_to(props[3:4, :], (8, LANES))
    table_emit = jnp.broadcast_to(3.0 * props[4:5, :], (8, LANES))

    turned[...] = jnp.zeros(turned.shape, f32)
    for q in range(2):
        for s in range(4):
            strips[0:32, :] = got(SIDE + q * 5 + s)
            strips[32:40, :] = got(SIDE + q * 5 + 4, 8 * opposite(s), 8)
            for number in range(2):
                low = strips[2 * SUB * number : 2 * SUB * number + SUB, :]
                high = strips[2 * SUB * number + SUB : 2 * SUB * (number + 1), :]
                if s < 2:
                    at = FIRST - SUB if s == 0 else FIRST + 256
                    target = cur.at[0] if number == 0 else cur.at[1]
                    target[3 * q, at : at + SUB, :] = low
                    target[3 * q + 1, at : at + SUB, :] = high
                else:
                    at = (54, 118)[q] if s == 2 else (0, 64)[q]
                    turned[number, at : at + SUB, :LANES] = low
                    turned[number, at : at + SUB, LANES:] = high
    for number in range(2):
        cur[number, 2, FIRST : FIRST + 256, :] = turned[number].T
        corner = got(CORNER2, 16 * number, 16)
        cur[number, 2, TOP : TOP + 16, :] = corner
        cur[number, 2, FIRST + 256 : FIRST + 272, :] = jnp.where(
            lanes((16, LANES)) % 64 < 32, rolled(corner, -16), rolled(corner, 16)
        )
    for q in range(2):
        for half in range(2):
            cur[0, 3 * q + half, FIRST : FIRST + 256, :] = level[q, :, LANES * half : LANES * (half + 1)]
            cur[1, 3 * q + half, FIRST : FIRST + 256, :] = fuel_class[
                q, :, LANES * half : LANES * (half + 1)
            ].astype(f32)

    def rates(chunk, carry):
        at = pl.multiple_of(chunk * 8, 8)
        for t in range(5):
            kind = cur[1, t, pl.ds(at, 8), :].astype(i32) & 127
            base_rate[t, pl.ds(at, 8), :] = pick(table_base, kind)
            wind_rate[t, pl.ds(at, 8), :] = pick(table_wind, kind)
        return carry

    lax.fori_loop(1, 37, rates, 0)

    inner = lane % 64
    side_col = jnp.where(inner < 16, inner // 8, jnp.where(inner >= 48, 30 + (inner - 48) // 8, 0))
    for k in range(2):
        for t in range(5):
            for quarter in range(4):
                for outer in (0, 64):
                    if outer and quarter in (1, 2):
                        continue
                    at = outer + k * 32
                    if t == 2:
                        west = got(WINDB, 8 * quarter, 8)
                        east = got(WINDB + 1, 8 * quarter, 8)
                        index = side_col + at
                        value = jnp.where(lane < 64, pick(west, index), pick(east, index))
                    else:
                        source = got(WINDA + t // 3, 8 * quarter, 8)
                        value = pick(source, lane // 8 + (at + 16 * (t % 3)))
                    value = value * log2e
                    if not outer:
                        wind[k, t, 3 + 8 * quarter : 11 + 8 * quarter, :] = value
                    elif quarter == 3:
                        wind[k, t, 1:3, :] = value[6:8, :]
                    else:
                        wind[k, t, 35:37, :] = value[0:2, :]

    def there(j):
        return j >= 0

    across_links = []
    groups = []
    for q in range(2):
        i = own + q
        near = [adjacency[i, s] for s in range(4)]
        safe = [jnp.maximum(near[s], 0) for s in range(4)]

        def joined(s, t):
            return there(near[s]) & there(adjacency[safe[s], t])

        groups.append([(there(near[s]), joined(2, s), joined(3, s)) for s in range(2)])
        across_links.append([[joined(0, t), there(near[t]), joined(1, t)] for t in (2, 3)])

    def as_int(flag):
        return jnp.where(flag, 1, 0)

    for line in range(2):
        for q in range(2):
            mid, west, east = groups[q][line]
            row = jnp.broadcast_to(as_int(mid), (8, LANES))
            links[line, 3 * q] = row
            links[line, 3 * q + 1] = row
        w0, e0 = groups[0][line][1:]
        w1, e1 = groups[1][line][1:]
        links[line, 2] = jnp.where(
            lane < 32,
            as_int(e0),
            jnp.where(lane < 64, as_int(w0), jnp.where(lane < 96, as_int(e1), as_int(w1))),
        )

    is0 = lane == 0
    is63 = lane == 63
    is64 = lane == 64
    is127 = lane == 127
    tanh_sum[...] = jnp.zeros(tanh_sum.shape, f32)

    def make_masks(region):
        (w0, e0), (w1, e1) = [
            [as_int(across_links[q][t][region]) for t in range(2)] for q in range(2)
        ]
        on = [jnp.broadcast_to(flag, (8, LANES)) > 0 for flag in (w0, e0, w1, e1)]
        return on

    def update(source, target, chunk, masks, rows_edge, main):
        lw0, le0, lw1, le1 = masks
        at = chunk * 8
        x = [cur[source, t, pl.ds(at, 8), :] for t in range(5)]
        up = [cur[source, t, pl.ds(at - 1, 8), :] for t in range(5)]
        dn = [cur[source, t, pl.ds(at + 1, 8), :] for t in range(5)]
        if rows_edge is not None:
            kind, line, row = rows_edge
            for t in range(5):
                broken = (sub == row) & (links[line, t] == 0)
                if kind == "up":
                    up[t] = jnp.where(broken, x[t], up[t])
                else:
                    dn[t] = jnp.where(broken, x[t], dn[t])
        right = [rolled(v, 1) for v in x]
        left = [rolled(v, -1) for v in x]
        h = x[2]
        west = [
            jnp.where(is0, jnp.where(lw0, rolled(h, 65), x[0]), right[0]),
            jnp.where(is0, right[0], right[1]),
            jnp.where(
                is0,
                jnp.where(le0, right[1], h),
                jnp.where(is64, jnp.where(le1, rolled(x[4], 65), h), right[2]),
            ),
            jnp.where(is0, jnp.where(lw1, right[2], x[3]), right[3]),
            jnp.where(is0, right[3], right[4]),
        ]
        east = [
            jnp.where(is127, left[1], left[0]),
            jnp.where(is127, jnp.where(le0, left[2], x[1]), left[1]),
            jnp.where(
                is127,
                jnp.where(lw1, left[3], h),
                jnp.where(is63, jnp.where(lw0, rolled(x[0], 63), h), left[2]),
            ),
            jnp.where(is127, left[4], left[3]),
            jnp.where(is127, jnp.where(le1, rolled(h, -65), x[4]), left[4]),
        ]
        for t in range(5):
            diff_rows = dn[t] - up[t]
            diff_cols = east[t] - west[t]
            around = (dn[t] + up[t]) + (east[t] + west[t])
            square = diff_rows * diff_rows + (diff_cols * diff_cols + 4.0 * floor_square)
            inverse = lax.rsqrt(square)
            wind_r = wind[0, t, pl.ds(chunk, 1), :]
            wind_c = wind[1, t, pl.ds(chunk, 1), :]
            along = (wind_r * diff_rows + wind_c * diff_cols) * inverse
            soft = jnp.log(1.0 + jnp.exp2(along))
            power = soft * soft * lax.rsqrt(soft)
            b = base_rate[t, pl.ds(at, 8), :]
            w = wind_rate[t, pl.ds(at, 8), :]
            new = ((1.0 - 4.0 * smoothing) * x[t] + smoothing * around) - (b + w * power) * (
                square * inverse
            )
            cur[target, t, pl.ds(at, 8), :] = new
            if main and t != 2:
                m = t - t // 3
                tanh_sum[m, pl.ds(at - FIRST, 8), :] += jnp.tanh(new)

    above = make_masks(0)
    within = make_masks(1)
    below = make_masks(2)

    def substep(step, carry):
        source = step & 1
        target = 1 - source
        update(source, target, 1, above, None, False)
        update(source, target, 2, above, ("down", 0, 7), False)
        update(source, target, 3, within, ("up", 0, 0), True)

        def middle(chunk, inner_carry):
            update(source, target, chunk, within, None, True)
            return inner_carry

        lax.fori_loop(4, 34, middle, 0)
        update(source, target, 34, within, ("down", 1, 7), True)
        update(source, target, 35, below, ("up", 1, 0), False)
        update(source, target, 36, below, None, False)
        return carry

    lax.fori_loop(0, SUB, substep, 0)

    last = SUB % 2

    def finish(chunk, sums):
        burn, emit = sums
        at = pl.multiple_of(chunk * 8, 8)
        for q in range(2):
            for half in range(2):
                t = 3 * q + half
                cols = slice(LANES * half, LANES * (half + 1))
                final = cur[last, t, pl.ds(FIRST + at, 8), :]
                level_out[q, pl.ds(at, 8), cols] = final
                burn = burn + (0.5 - 0.5 * jnp.tanh(final))
                kind = fuel_class[q, pl.ds(at, 8), cols]
                fuel = fuel_left[q, pl.ds(at, 8), cols]
                power = pick(table_burn, kind) * (float(SUB) - tanh_sum[2 * q + half, pl.ds(at, 8), :])
                new_fuel = fuel * jnp.exp2(power)
                fuel_out[q, pl.ds(at, 8), cols] = new_fuel
                spent = fuel - new_fuel
                emit = emit + pick(table_emit, kind) * spent
                released = pick(table_heat, kind) * spent
                row_heat[2 * q + half, pl.ds(chunk, 1), :] = jnp.sum(released, axis=0, keepdims=True)
        return burn, emit

    blank = jnp.zeros((8, LANES), f32)
    burn, emit = lax.fori_loop(0, 32, finish, (blank, blank))
    source_lane = lax.broadcasted_iota(i32, (LANES, LANES), 0) // REF
    target_lane = lanes((LANES, LANES))
    for q in range(2):
        packed = blank
        for g in range(4):
            for half in range(2):
                gather = jnp.where(
                    target_lane == 32 * g + 16 * half + source_lane, heating / (REF * REF), 0.0
                ).astype(f32)
                packed = packed + jnp.dot(
                    row_heat[2 * q + half, 8 * g : 8 * g + 8, :],
                    gather,
                    precision=lax.Precision.HIGHEST,
                    preferred_element_type=f32,
                )
        heat_out[8 * q : 8 * q + 8, :] = packed
    burn_sum = jnp.sum(jnp.sum(burn, axis=0, keepdims=True), axis=1, keepdims=True)
    emit_sum = jnp.sum(jnp.sum(emit, axis=0, keepdims=True), axis=1, keepdims=True)
    lane1 = lanes((1, LANES))
    heat_out[16:17, :] = jnp.where(lane1 == 0, burn_sum, jnp.where(lane1 == 1, emit_sum, 0.0))

    load.wait()
    zero = jnp.zeros((128, LANES), f32)
    for f in range(3):
        air[f, 0, 8:136, :] = zero
        air[f, 17, 8:136, :] = zero
    keep_north = jnp.where(pos[0] > 0, 1.0, 0.0).astype(f32)
    keep_south = jnp.where(pos[0] < down - 1, 1.0, 0.0).astype(f32)
    keep_west = jnp.where(pos[1] > 0, 1.0, 0.0).astype(f32)
    keep_east = jnp.where(pos[1] < across - 1, 1.0, 0.0).astype(f32)
    for group in range(3):
        strips[...] = jnp.zeros(strips.shape, f32)
        rows = got(ROWS2 + group)
        for p in range(32):
            number = 32 * group + p
            plane = number % 48
            at = 7 if number < 48 else 136
            keep = keep_north if number < 48 else keep_south
            air[plane // 16, plane % 16 + 1, at : at + 1, :] = rows[p : p + 1, :] * keep
    sides = []
    for group in range(4):
        sides.append(got(COLS2 + group) * jnp.where(lane32 % 2 == 1, keep_east, keep_west))
    for group in range(4):
        turned[0, 32 * group : 32 * group + 32, :LANES] = sides[group]

    def air_level(number, carry):
        def air_rows(chunk, inner_carry):
            at = 8 + chunk * 8
            halo = turned[0, pl.ds(chunk * 8, 8), :LANES]
            u = air[0, number + 1, pl.ds(at, 8), :]
            v = air[1, number + 1, pl.ds(at, 8), :]
            for f in range(3):
                x = u if f == 0 else v if f == 1 else air[2, number + 1, pl.ds(at, 8), :]
                up = air[f, number + 1, pl.ds(at - 1, 8), :]
                dn = air[f, number + 1, pl.ds(at + 1, 8), :]
                over = air[f, number + 2, pl.ds(at, 8), :]
                under = air[f, number, pl.ds(at, 8), :]
                mine = pltpu.roll(halo, LANES - 1 - 2 * (f * 16 + number), 1)
                west = rolled(jnp.where(is127, mine, x), 1)
                east = rolled(jnp.where(is0, mine, x), -1)
                around = (up + dn) + (west + east)
                advect = u * (dn - up) + v * (east - west)
                air_new[f, number, pl.ds(chunk * 8, 8), :] = (
                    (1.0 - 4.0 * viscosity - 2.0 * mixing) * x
                    + viscosity * around
                    - (0.5 * courant) * advect
                    + mixing * (over + under)
                )
            return inner_carry

        lax.fori_loop(0, 16, air_rows, 0)
        return carry

    lax.fori_loop(0, 16, air_level, 0)
    store = pltpu.make_async_copy(air_new, air_out, sem_out)
    store.start()
    store.wait()


def heat_kernel(cells, pos, blocks, gathered, air_in, air_out, totals, plane, sem):
    load = pltpu.make_async_copy(air_in.at[2, 0], plane, sem)
    load.start()
    devices = gathered.shape[0] // HEAT_ROWS
    sums = jnp.sum(
        gathered[pl.ds(16, devices, stride=HEAT_ROWS), :], axis=0, keepdims=True
    )
    totals[...] = sums * (1.0 / cells)
    load.wait()
    lane = lanes()
    tile_rows = 128 // BA

    def place(j, carry):
        row = blocks[j, 0] - pos[0] * tile_rows
        col = blocks[j, 1] - pos[1] * tile_rows
        inside = (row >= 0) & (row < tile_rows) & (col >= 0) & (col < tile_rows)

        @pl.when(inside)
        def _():
            heat = gathered[pl.ds((j // 2) * HEAT_ROWS + 8 * (j % 2), 8), :]
            for g in range(4):
                moved = pltpu.roll(heat, (col - g + 4) * BA % LANES, 1)
                at = pl.multiple_of(row * BA + 8 * g, 8)
                plane[pl.ds(at, 8), :] += jnp.where(lane // BA == col, moved, 0.0)

        return carry

    lax.fori_loop(0, blocks.shape[0], place, 0)
    store = pltpu.make_async_copy(plane, air_out.at[2, 0], sem)
    store.start()
    store.wait()


def local(air_state, level_set, fuel_left, fuel_class, fuel_props, blocks, adjacency):
    down = lax.axis_size("gx")
    across = lax.axis_size("gy")
    devices = down * across
    both = ("gx", "gy")
    pos = jnp.stack([lax.axis_index("gx"), lax.axis_index("gy")]).astype(i32)
    smem = pl.BlockSpec(memory_space=pltpu.SMEM)
    vmem = pl.BlockSpec(memory_space=pltpu.VMEM)
    anywhere = pl.BlockSpec(memory_space=pl.ANY)
    packed = pl.pallas_call(
        pack_kernel,
        out_shape=jax.ShapeDtypeStruct((devices * REC1, LANES), f32),
        in_specs=[smem, smem, vmem, vmem, anywhere],
        out_specs=vmem,
        scratch_shapes=[
            pltpu.VMEM((48 * 128, LANES), f32),
            pltpu.VMEM((4, 40, LANES), f32),
            pltpu.VMEM((128, LANES), f32),
            pltpu.SemaphoreType.DMA(()),
        ],
        name="pack",
    )(pos, blocks, level_set, fuel_class, air_state.reshape(48 * 128, LANES))
    relayed = lax.all_to_all(packed.reshape(devices, REC1, LANES), both, 0, 0)
    chosen = pl.pallas_call(
        lambda *refs: select_kernel(across, down, *refs),
        out_shape=jax.ShapeDtypeStruct((devices * REC2, LANES), f32),
        in_specs=[smem, smem, smem, vmem],
        out_specs=vmem,
        scratch_shapes=[pltpu.SMEM((blocks.shape[0],), i32), pltpu.SMEM((devices,), i32)],
        name="select",
    )(pos, blocks, adjacency, relayed.reshape(devices * REC1, LANES))
    received = lax.all_to_all(chosen.reshape(devices, REC2, LANES), both, 0, 0)
    props = jnp.pad(fuel_props, ((0, 3), (0, LANES - fuel_props.shape[1])), constant_values=1.0)
    level_next, fuel_next, heat, air_next = pl.pallas_call(
        lambda *refs: fire_kernel(across, down, *refs),
        out_shape=(
            jax.ShapeDtypeStruct(level_set.shape, f32),
            jax.ShapeDtypeStruct(level_set.shape, f32),
            jax.ShapeDtypeStruct((HEAT_ROWS, LANES), f32),
            jax.ShapeDtypeStruct(air_state.shape, f32),
        ),
        in_specs=[smem, smem, vmem, vmem, vmem, vmem, vmem, anywhere],
        out_specs=(vmem, vmem, vmem, anywhere),
        scratch_shapes=[
            pltpu.VMEM((2, 5, EXT, LANES), f32),
            pltpu.VMEM((5, EXT, LANES), f32),
            pltpu.VMEM((5, EXT, LANES), f32),
            pltpu.VMEM((2, 5, 40, LANES), f32),
            pltpu.VMEM((40, LANES), f32),
            pltpu.VMEM((2, LANES, 256), f32),
            pltpu.VMEM((4, 256, LANES), f32),
            pltpu.VMEM((2, 5, 8, LANES), i32),
            pltpu.VMEM((4, 32, LANES), f32),
            pltpu.VMEM((3, 18, 144, LANES), f32),
            pltpu.VMEM((3, 16, 128, LANES), f32),
            pltpu.SemaphoreType.DMA(()),
            pltpu.SemaphoreType.DMA(()),
        ],
        name="fire",
    )(
        pos,
        adjacency,
        props,
        received.reshape(devices * REC2, LANES)[: PIECES * REC2],
        level_set,
        fuel_left,
        fuel_class,
        air_state,
    )
    spread = jnp.broadcast_to(
        heat.reshape(1, 1, HEAT_ROWS * LANES), (devices, 1, HEAT_ROWS * LANES)
    )
    gathered = lax.all_to_all(spread, both, 0, 0).reshape(devices * HEAT_ROWS, LANES)
    cells = blocks.shape[0] * level_set.shape[1] * level_set.shape[2]
    air_next, totals = pl.pallas_call(
        lambda *refs: heat_kernel(cells, *refs),
        out_shape=(
            jax.ShapeDtypeStruct(air_state.shape, f32),
            jax.ShapeDtypeStruct((1, LANES), f32),
        ),
        in_specs=[smem, smem, vmem, anywhere],
        out_specs=(anywhere, vmem),
        scratch_shapes=[pltpu.VMEM((128, LANES), f32), pltpu.SemaphoreType.DMA(())],
        input_output_aliases={3: 0},
        name="heat",
    )(pos, blocks, gathered, air_next)
    return (air_next, level_next, fuel_next, totals[0, 0:2])


def solution(mesh):
    in_specs = (
        P(None, None, "gx", "gy"),
        P(("gx", "gy"), None, None),
        P(("gx", "gy"), None, None),
        P(("gx", "gy"), None, None),
        P(),
        P(),
        P(),
    )
    out_specs = (
        P(None, None, "gx", "gy"),
        P(("gx", "gy"), None, None),
        P(("gx", "gy"), None, None),
        P(),
    )
    return jax.shard_map(local, mesh=mesh, in_specs=in_specs, out_specs=out_specs, check_vma=False)
```

time: 730 us -> 168 us (0.23)
  blocking collectives: 474 us -> 13.3 us
  other arithmetic: 125 us -> 0.59 us
  Pallas kernels: 0 us -> 110 us
  local copies, waits for them, and re-layouts: 101 us -> 6.11 us
  waiting for transfers between devices: 0.03 us -> 25.5 us
  between operations: 15.6 us -> 0.71 us
    all_gather x21 -> x0, blocking collectives: 435 us -> none  [the longest x10 308 us: substep(): along_cols = lax.all_gather(own_edges, 'gy', axis=0, tiled=True)]
    pallas_call x0 -> x4, Pallas kernels: none -> 110 us  [the longest x1 91.9 us: local(): pl.pallas_call(lambda *refs: fire_kernel(across, down, *refs), out_shape=...]
    add x23 -> x0, other arithmetic: 60.9 us -> none  [the longest x10 43.8 us: advance(): emitted + emission * spent]
    mul x6 -> x0, other arithmetic: 41.3 us -> none  [the longest x4 39.8 us: cell_table(): return tuple((scales[entry] * values[entry] for entry in range(5)))]
    psum x1 -> x0, blocking collectives: 39.1 us -> none  [local(): lax.psum((jnp.sum(burning), jnp.sum(emitted)), ('gx', 'gy'))]
    slice x70 -> x0, local copies, waits for them, and re-layouts: 34.9 us -> none  [the longest x30 10.7 us: advance(): south = jnp.concatenate([current[:, 1:, :], ghosts[:, 1, None, :]], axis=1)]
    all_to_all x0 -> x2, waiting for transfers between devices: none -> 25.5 us  [the longest x1 12.8 us: local(): received = lax.all_to_all(chosen.reshape(devices, REC2, LANES), both, 0, 0)]
    reshape x15 -> x0, local copies, waits for them, and re-layouts: 21.3 us -> none  [the longest x1 12.7 us: local(): jnp.broadcast_to(block_wind, (local_count, 2, BA, REF, BA, REF))]
  transfers between devices with their start and end apart: 5 -> 2, of which waited for: 0 -> 2; matrix products, arithmetic and copies ran while one was open for 13% -> 1% of each run, Pallas kernels for 0% -> 0%
where the time goes in v1:
time: 168 us; the launch traced here: 167 us
  Pallas kernels  110 us (65%)
  waiting for transfers between devices  25.5 us (15%)
  blocking collectives  13.3 us (8%)
  starting transfers between devices  10.6 us (6%)
  local copies, waits for them, and re-layouts  6.11 us (4%)
    pallas_call x1, Pallas kernels, local(): pl.pallas_call(lambda *refs: fire_kernel(across, down, *refs), out_shape=...  91.9 us
    all_to_all x1, blocking collectives, local(): lax.all_to_all(spread, both, 0, 0).reshape(devices * HEAT_ROWS, LANES)  13.3 us
    all_to_all x1, waiting for transfers between devices, local(): received = lax.all_to_all(chosen.reshape(devices, REC2, LANES), both, 0, 0)  12.8 us
    all_to_all x1, waiting for transfers between devices, local(): relayed = lax.all_to_all(packed.reshape(devices, REC1, LANES), both, 0, 0)  12.7 us
    pallas_call x1, Pallas kernels, local(): pl.pallas_call(lambda *refs: select_kernel(across, down, *refs), out_shap...  8.05 us
    all_to_all x1, starting transfers between devices, local(): relayed = lax.all_to_all(packed.reshape(devices, REC1, LANES), both, 0, 0)  7.97 us
    pallas_call x1, Pallas kernels, local(): pl.pallas_call(pack_kernel, out_shape=jax.ShapeDtypeStruct((devices * REC...  6.68 us
    pallas_call x1, Pallas kernels, local(): pl.pallas_call(lambda *refs: heat_kernel(cells, *refs), out_shape=(jax.Sh...  3.71 us
  transfers between devices with their start and end apart: 2, of which 2 were waited for; matrix products, arithmetic and copies ran while one was open for 1% of the time, Pallas kernels for 0%

profile of v1, /device:TPU:0, one launch (start us, length us, event | category | flops | bytes accessed | tf_op | source)
XLA Modules:
  0.0 167.1 jit_solution(7862770945762532090)
XLA Ops:
  0.6 0.0 copy-start.3
  0.6 1.4 copy.21.blocks.refs_1_
  2.0 0.6 pad_add_fusion.pos.refs_0_
  2.6 0.0 copy-start.2
  2.6 6.7 %pack.1 = f32[768,128]{1,0:T(8,128)} custom-call(s32[2]{0:T(128)} %pad_add_fusion.pos.refs_0_, s32[64,2]{1,0:T(8,128)} %copy.21.blocks.refs_1_, f32[2,256,256]{2,1,0:T(8,128)} %refs_4_.1, s32[2,256,256]{2,1,0:T(8,128)} %refs_6_.1, f32[6144,128]{1,0:T(8,128)} %bitcast.11), custom_call_target="tpu_custom_call" | custom-call | tf_op jit(solution)/shard_map/pack/pallas_call | solution.py:663
  9.3 8.0 %all-to-all-start = ((f32[32,24,128]{2,1,0:T(8,128)}), f32[32,24,128]{2,1,0:T(8,128)S(1)}, u32[]{:S(2)}, u32[]{:S(2)}) async-start(f32[32,24,128]{2,1,0:T(8,128)} %bitcast.15), calls=%async_computation | async-start | bytes 786432 | tf_op jit(solution)/shard_map/all_to_all | solution.py:676
  17.3 0.0 copy-done.3
  17.3 0.7 copy.20.refs_2_.refs_1_
  18.0 12.7 %all-to-all-done = f32[32,24,128]{2,1,0:T(8,128)S(1)} async-done(((f32[32,24,128]{2,1,0:T(8,128)}), f32[32,24,128]{2,1,0:T(8,128)S(1)}, u32[]{:S(2)}, u32[]{:S(2)}) %all-to-all-start) | async-done | bytes 393248 | tf_op jit(solution)/shard_map/all_to_all | solution.py:676
  30.7 0.0 copy-start.1
  30.7 0.7 copy-done.1
  31.5 8.1 %select.2 = f32[768,128]{1,0:T(8,128)} custom-call(s32[2]{0:T(128)} %pad_add_fusion.pos.refs_0_, s32[64,2]{1,0:T(8,128)} %copy.21.blocks.refs_1_, s32[64,4]{1,0:T(8,128)} %copy.20.refs_2_.refs_1_, f32[768,128]{1,0:T(8,128)} %bitcast.13), custom_call_target="tpu_custom_call" | custom-call | tf_op jit(solution)/shard_map/select/pallas_call | solution.py:677
  39.5 2.6 %all-to-all-start.1 = ((f32[32,24,128]{2,1,0:T(8,128)}), f32[32,24,128]{2,1,0:T(8,128)S(1)}, u32[]{:S(2)}, u32[]{:S(2)}) async-start(f32[32,24,128]{2,1,0:T(8,128)} %bitcast.14), calls=%async_computation.1 | async-start | bytes 786432 | tf_op jit(solution)/shard_map/all_to_all | solution.py:685
  42.1 0.0 copy-done.2
  42.1 0.6 pad.4.refs_2_
  42.7 12.8 %all-to-all-done.1 = f32[32,24,128]{2,1,0:T(8,128)S(1)} async-done(((f32[32,24,128]{2,1,0:T(8,128)}), f32[32,24,128]{2,1,0:T(8,128)S(1)}, u32[]{:S(2)}, u32[]{:S(2)}) %all-to-all-start.1) | async-done | bytes 393248 | tf_op jit(solution)/shard_map/all_to_all | solution.py:685
  55.5 0.0 copy-start
  55.5 0.7 copy-done
  56.3 91.9 %fire.1 = (f32[2,256,256]{2,1,0:T(8,128)}, f32[2,256,256]{2,1,0:T(8,128)}, f32[17,128]{1,0:T(8,128)}, f32[3,16,128,128]{3,2,1,0:T(8,128)}) custom-call(s32[2]{0:T(128)} %pad_add_fusion.pos.refs_0_, s32[64,4]{1,0:T(8,128)} %copy.20.refs_2_.refs_1_, f32[8,128]{1,0:T(8,128)} %pad.4.refs_2_, f32[768,128]{1,0:T(8,128)} %bitcast.12, f32[2,256,256]{2,1,0:T(8,128)} %refs_4_.1, ...), custom_call_target="tpu_custom_call" | custom-call | tf_op jit(solution)/shard_map/fire/pallas_call | solution.py:687
  148.1 0.9 broadcast_in_dim.8
  149.0 13.3 %all_to_all.15 = f32[32,1,2176]{2,1,0:T(1,128)} all-to-all(f32[32,1,2176]{2,1,0:T(1,128)S(1)} %broadcast_in_dim.8), channel_id=1, replica_groups=mesh['gx'=4,'gy'=8] {'gx','gy'}, dimensions={0} | all-to-all | bytes 557056 | tf_op jit(solution)/shard_map/all_to_all | solution.py:726
  162.3 3.7 %heat.1 = (f32[3,16,128,128]{3,2,1,0:T(8,128)}, f32[1,128]{1,0:T(1,128)}) custom-call(s32[2]{0:T(128)} %pad_add_fusion.pos.refs_0_, s32[64,2]{1,0:T(8,128)} %copy.21.blocks.refs_1_, f32[544,128]{1,0:T(8,128)} %bitcast.16, f32[3,16,128,128]{3,2,1,0:T(8,128)} %get-tuple-element.11.refs_3_), custom_call_target="tpu_custom_call", output_to_operand_aliasing={{0}: (3, {})} | custom-call | tf_op jit(solution)/shard_map/heat/pallas_call | solution.py:728
  166.0 1.1 slice_bitcast_fusion
Async XLA Ops:
  0.6 16.7 %copy-start.3 = (s32[64,4]{0,1:T(4,128)S(1)}, s32[64,4]{0,1:T(4,128)}, u32[]{:S(2)}) copy-start(s32[64,4]{0,1:T(4,128)} %param.13) | copy-start | bytes 3076
  2.6 39.5 %copy-start.2 = (f32[5,13]{1,0:T(8,128)S(1)}, f32[5,13]{1,0:T(8,128)}, u32[]{:S(2)}) copy-start(f32[5,13]{1,0:T(8,128)} %param.11) | copy-start | bytes 784
  9.3 21.4 %all-to-all-start = ((f32[32,24,128]{2,1,0:T(8,128)}), f32[32,24,128]{2,1,0:T(8,128)S(1)}, u32[]{:S(2)}, u32[]{:S(2)}) async-start(f32[32,24,128]{2,1,0:T(8,128)} %bitcast.15), calls=%async_computation | async-start | bytes 786432 | tf_op jit(solution)/shard_map/all_to_all | solution.py:676
  30.7 0.7 copy-start.1
  39.5 16.0 %all-to-all-start.1 = ((f32[32,24,128]{2,1,0:T(8,128)}), f32[32,24,128]{2,1,0:T(8,128)S(1)}, u32[]{:S(2)}, u32[]{:S(2)}) async-start(f32[32,24,128]{2,1,0:T(8,128)} %bitcast.14), calls=%async_computation.1 | async-start | bytes 786432 | tf_op jit(solution)/shard_map/all_to_all | solution.py:685
  55.5 0.7 copy-start

commit v2 on v1

--- a/solution.py
+++ b/solution.py
@@ -13,6 +13,10 @@
 SUB = 10
 PIECES = 32
 LANES = 128
+UNROLL = 30
+RATE_UNROLL = 12
+FINISH_UNROLL = 16
+AIR_UNROLL = 16
 
 step_time = 0.25
 smoothing = 0.15
@@ -112,8 +116,8 @@
     tile_rows = 128 // BA
 
     def find(j, count):
-        row = blocks[j, 0] - pos[0] * tile_rows
-        col = blocks[j, 1] - pos[1] * tile_rows
+        row = blocks[0, j] - pos[0] * tile_rows
+        col = blocks[1, j] - pos[1] * tile_rows
         inside = (row >= 0) & (row < tile_rows) & (col >= 0) & (col < tile_rows)
 
         @pl.when(inside)
@@ -130,7 +134,7 @@
 
         return count + inside.astype(i32)
 
-    lax.fori_loop(0, blocks.shape[0], find, jnp.int32(0))
+    lax.fori_loop(0, blocks.shape[1], find, jnp.int32(0))
 
     edge[0:48, :] = air[pl.ds(127, 48, stride=128), :]
     edge[48:96, :] = air[pl.ds(0, 48, stride=128), :]
@@ -155,11 +159,13 @@
         out[PIECES * REC1 :, :] = jnp.zeros((out.shape[0] - PIECES * REC1, LANES), f32)
 
 
-def select_kernel(across, down, pos, blocks, adjacency, received, out, wind_row, count):
-    total = blocks.shape[0]
+WORDS = 40
+
+
+def index_kernel(across, down, pos, blocks, adjacency, out, wind_row, count):
+    total = blocks.shape[1]
     devices = across * down
     relay = jnp.minimum(pos[0] * across + pos[1], PIECES - 1)
-    lane1 = lanes((1, LANES))
     tile_rows = 128 // BA
 
     def clear(d, carry):
@@ -169,38 +175,26 @@
     lax.fori_loop(0, devices, clear, 0)
 
     def number(j, carry):
-        tile = (blocks[j, 0] // tile_rows) * across + blocks[j, 1] // tile_rows
+        tile = (blocks[0, j] // tile_rows) * across + blocks[1, j] // tile_rows
         slot = count[tile]
         count[tile] = slot + 1
         wind_row[j] = tile * REC1 + WIND + slot
         return carry
 
     lax.fori_loop(0, total, number, 0)
-
-    def take(index):
-        return received[pl.ds(index, 1), :]
-
     spare_side = relay // 8
     upper = relay >= 16
-    lane_col = lane1 % 32 < 16
-    first_half = lane1 < 64
-    quarter = lane1 // 16
 
     def serve(d, carry):
-        base = d * REC2
-
-        def put(row, value):
-            out[pl.ds(base + row, 1), :] = value
-
-        corner_rows = []
+        base = d * WORDS
         for q in range(2):
             i = 2 * d + q
-            near = [adjacency[i, s] for s in range(4)]
+            near = [adjacency[s, i] for s in range(4)]
             safe = [jnp.maximum(near[s], 0) for s in range(4)]
 
             def diagonal(s, t):
-                by_row = adjacency[safe[s], t]
-                by_col = adjacency[safe[t], s]
+                by_row = adjacency[t, safe[s]]
+                by_col = adjacency[s, safe[t]]
                 return jnp.maximum(jnp.where(near[s] >= 0, by_row, jnp.where(near[t] >= 0, by_col, 0)), 0)
 
             nw, ne, sw, se = diagonal(0, 2), diagonal(0, 3), diagonal(1, 2), diagonal(1, 3)
@@ -208,30 +202,63 @@
             def side_row(j, s):
                 return (j // 2) * REC1 + SIDE + (j % 2) * 5 + s
 
-            def corner_row(j):
-                return (j // 2) * REC1 + CORNER + j % 2
-
             for s in range(4):
-                put(SIDE + q * 5 + s, take(side_row(safe[s], opposite(s))))
+                out[base + 5 * q + s] = side_row(safe[s], opposite(s))
             spare = jnp.where(
                 spare_side == 0,
                 safe[1],
                 jnp.where(spare_side == 1, safe[0], jnp.where(spare_side == 2, safe[3], safe[2])),
             )
-            put(SIDE + q * 5 + 4, take(side_row(spare, 4)))
-            corner_rows += [take(corner_row(j)) for j in (ne, se, sw, nw)]
-            put(
-                WINDA + q,
-                jnp.where(
-                    first_half,
-                    take(wind_row[i]),
-                    take(wind_row[jnp.where(upper, safe[0], safe[1])]),
-                ),
+            out[base + 5 * q + 4] = side_row(spare, 4)
+            for k, j in enumerate((ne, se, sw, nw)):
+                out[base + 10 + 4 * q + k] = (j // 2) * REC1 + CORNER + j % 2
+            winds = (
+                i,
+                jnp.where(upper, safe[0], safe[1]),
+                safe[3],
+                safe[2],
+                jnp.where(upper, ne, se),
+                jnp.where(upper, nw, sw),
             )
-            east = take(wind_row[safe[3]])
-            west = take(wind_row[safe[2]])
-            corner_east = take(wind_row[jnp.where(upper, ne, se)])
-            corner_west = take(wind_row[jnp.where(upper, nw, sw)])
+            for k, j in enumerate(winds):
+                out[base + 18 + 6 * q + k] = wind_row[j]
+        a = d // across
+        b = d % across
+        north = jnp.where(a > 0, d - across, d)
+        south = jnp.where(a < down - 1, d + across, d)
+        out[base + 30] = jnp.where(b < across - 1, d + 1, d) * REC1 + COLS
+        out[base + 31] = jnp.where(b > 0, d - 1, d) * REC1 + COLS
+        out[base + 32] = north * REC1 + ROWS
+        out[base + 33] = jnp.where(relay < 16, north, south) * REC1 + ROWS + 1
+        out[base + 34] = south * REC1 + ROWS + 2
+        return carry
+
+    lax.fori_loop(0, devices, serve, 0)
+
+
+def select_kernel(index, received, out):
+    lane1 = lanes((1, LANES))
+    lane_col = lane1 % 32 < 16
+    first_half = lane1 < 64
+    quarter = lane1 // 16
+    odd = lane1 % 2 == 1
+
+    def one(d):
+        def take(word, more=0):
+            return received[pl.ds(index[d * WORDS + word] + more, 1), :]
+
+        def put(row, value):
+            out[pl.ds(d * REC2 + row, 1), :] = value
+
+        for row in range(10):
+            put(SIDE + row, take(row))
+        merged = take(17)
+        for k in range(7):
+            merged = jnp.where(quarter == k, take(10 + k), merged)
+        put(CORNER2, merged)
+        for q in range(2):
+            own, beyond, east, west, corner_east, corner_west = [take(18 + 6 * q + k) for k in range(6)]
+            put(WINDA + q, jnp.where(first_half, own, beyond))
             put(
                 WINDB + q,
                 jnp.where(
@@ -240,37 +267,19 @@
                     jnp.where(first_half, west, corner_west),
                 ),
             )
-        merged = corner_rows[7]
-        for k in range(7):
-            merged = jnp.where(quarter == k, corner_rows[k], merged)
-        put(CORNER2, merged)
-        a = d // across
-        b = d % across
-        north = jnp.where(a > 0, d - across, d)
-        south = jnp.where(a < down - 1, d + across, d)
-        west_tile = jnp.where(b > 0, d - 1, d)
-        east_tile = jnp.where(b < across - 1, d + 1, d)
-        odd = lane1 % 2 == 1
         for group in range(4):
-            put(
-                COLS2 + group,
-                jnp.where(
-                    odd,
-                    take(east_tile * REC1 + COLS + group),
-                    take(west_tile * REC1 + COLS + group),
-                ),
-            )
-        put(ROWS2, take(north * REC1 + ROWS))
-        put(ROWS2 + 1, take(jnp.where(relay < 16, north, south) * REC1 + ROWS + 1))
-        put(ROWS2 + 2, take(south * REC1 + ROWS + 2))
+            put(COLS2 + group, jnp.where(odd, take(30, group), take(31, group)))
+        for group in range(3):
+            put(ROWS2 + group, take(32 + group))
         for row in range(ROWS2 + 3, REC2):
             put(row, jnp.zeros((1, LANES), f32))
-        return carry
-
-    lax.fori_loop(0, devices, serve, 0)
-
-
-MAIN = (0, 1, 3, 4)
+
+    def serve(pair, carry):
+        one(2 * pair)
+        one(2 * pair + 1)
+        return carry
+
+    lax.fori_loop(0, out.shape[0] // REC2 // 2, serve, 0)
 
 
 def fire_kernel(
@@ -283,12 +292,11 @@
     level,
     fuel_left,
     fuel_class,
-    air_hbm,
     level_out,
     fuel_out,
     heat_out,
-    air_out,
-    cur,
+    cur_a,
+    cur_b,
     base_rate,
     wind_rate,
     wind,
@@ -297,13 +305,8 @@
     tanh_sum,
     links,
     row_heat,
-    air,
-    air_new,
-    sem_in,
-    sem_out,
 ):
-    load = pltpu.make_async_copy(air_hbm, air.at[:, 1:17, 8:136, :], sem_in)
-    load.start()
+    cur = (cur_a, cur_b)
     lane = lanes()
     sub = lax.broadcasted_iota(i32, (8, LANES), 0)
     lane32 = lanes((32, LANES))
@@ -312,12 +315,20 @@
     def got(row, first=0, size=PIECES):
         return received[pl.ds(first * REC2 + row, size, stride=REC2), :]
 
-    table_base = jnp.broadcast_to(0.125 * 0.3 * props[0:1, :], (8, LANES))
-    table_wind = table_base * jnp.broadcast_to(0.3 * props[1:2, :], (8, LANES))
+    def table(value):
+        row = jnp.zeros((8, LANES), f32)
+        for kind in range(props.shape[1]):
+            row = jnp.where(lane == kind, value(kind), row)
+        return row
+
     log2e = math.log2(math.e)
-    table_burn = jnp.broadcast_to((-0.5 * step_time * log2e / 4.0) / props[2:3, :], (8, LANES))
-    table_heat = jnp.broadcast_to(props[3:4, :], (8, LANES))
-    table_emit = jnp.broadcast_to(3.0 * props[4:5, :], (8, LANES))
+    table_base = table(lambda c: 0.125 * 0.3 * props[0, c])
+    table_wind = table_base * table(lambda c: 0.3 * props[1, c])
+    table_burn = (-0.5 * step_time * log2e / 4.0) / jnp.where(
+        lane < props.shape[1], table(lambda c: props[2, c]), 1.0
+    )
+    table_heat = table(lambda c: props[3, c])
+    table_emit = table(lambda c: 3.0 * props[4, c])
 
     turned[...] = jnp.zeros(turned.shape, f32)
     for q in range(2):
@@ -329,7 +340,7 @@
                 high = strips[2 * SUB * number + SUB : 2 * SUB * (number + 1), :]
                 if s < 2:
                     at = FIRST - SUB if s == 0 else FIRST + 256
-                    target = cur.at[0] if number == 0 else cur.at[1]
+                    target = cur[number]
                     target[3 * q, at : at + SUB, :] = low
                     target[3 * q + 1, at : at + SUB, :] = high
                 else:
@@ -337,28 +348,29 @@
                     turned[number, at : at + SUB, :LANES] = low
                     turned[number, at : at + SUB, LANES:] = high
     for number in range(2):
-        cur[number, 2, FIRST : FIRST + 256, :] = turned[number].T
+        cur[number][2, FIRST : FIRST + 256, :] = turned[number].T
         corner = got(CORNER2, 16 * number, 16)
-        cur[number, 2, TOP : TOP + 16, :] = corner
-        cur[number, 2, FIRST + 256 : FIRST + 272, :] = jnp.where(
+        cur[number][2, TOP : TOP + 16, :] = corner
+        cur[number][2, FIRST + 256 : FIRST + 272, :] = jnp.where(
             lanes((16, LANES)) % 64 < 32, rolled(corner, -16), rolled(corner, 16)
         )
     for q in range(2):
         for half in range(2):
-            cur[0, 3 * q + half, FIRST : FIRST + 256, :] = level[q, :, LANES * half : LANES * (half + 1)]
-            cur[1, 3 * q + half, FIRST : FIRST + 256, :] = fuel_class[
+            cur_a[3 * q + half, FIRST : FIRST + 256, :] = level[q, :, LANES * half : LANES * (half + 1)]
+            cur_b[3 * q + half, FIRST : FIRST + 256, :] = fuel_class[
                 q, :, LANES * half : LANES * (half + 1)
             ].astype(f32)
 
-    def rates(chunk, carry):
-        at = pl.multiple_of(chunk * 8, 8)
-        for t in range(5):
-            kind = cur[1, t, pl.ds(at, 8), :].astype(i32) & 127
-            base_rate[t, pl.ds(at, 8), :] = pick(table_base, kind)
-            wind_rate[t, pl.ds(at, 8), :] = pick(table_wind, kind)
-        return carry
-
-    lax.fori_loop(1, 37, rates, 0)
+    def rates(group, carry):
+        for k in range(RATE_UNROLL):
+            at = pl.multiple_of((1 + group * RATE_UNROLL + k) * 8, 8)
+            for t in range(5):
+                kind = cur_b[t, pl.ds(at, 8), :].astype(i32) & 127
+                base_rate[t, pl.ds(at, 8), :] = pick(table_base, kind)
+                wind_rate[t, pl.ds(at, 8), :] = pick(table_wind, kind)
+        return carry
+
+    lax.fori_loop(0, 36 // RATE_UNROLL, rates, 0)
 
     inner = lane % 64
     side_col = jnp.where(inner < 16, inner // 8, jnp.where(inner >= 48, 30 + (inner - 48) // 8, 0))
@@ -392,11 +404,11 @@
     groups = []
     for q in range(2):
         i = own + q
-        near = [adjacency[i, s] for s in range(4)]
+        near = [adjacency[s, i] for s in range(4)]
         safe = [jnp.maximum(near[s], 0) for s in range(4)]
 
         def joined(s, t):
-            return there(near[s]) & there(adjacency[safe[s], t])
+            return there(near[s]) & there(adjacency[t, safe[s]])
 
         groups.append([(there(near[s]), joined(2, s), joined(3, s)) for s in range(2)])
         across_links.append([[joined(0, t), there(near[t]), joined(1, t)] for t in (2, 3)])
@@ -434,9 +446,9 @@
     def update(source, target, chunk, masks, rows_edge, main):
         lw0, le0, lw1, le1 = masks
         at = chunk * 8
-        x = [cur[source, t, pl.ds(at, 8), :] for t in range(5)]
-        up = [cur[source, t, pl.ds(at - 1, 8), :] for t in range(5)]
-        dn = [cur[source, t, pl.ds(at + 1, 8), :] for t in range(5)]
+        x = [source[t, pl.ds(at, 8), :] for t in range(5)]
+        up = [source[t, pl.ds(at - 1, 8), :] for t in range(5)]
+        dn = [source[t, pl.ds(at + 1, 8), :] for t in range(5)]
         if rows_edge is not None:
             kind, line, row = rows_edge
             for t in range(5):
@@ -486,7 +498,7 @@
             new = ((1.0 - 4.0 * smoothing) * x[t] + smoothing * around) - (b + w * power) * (
                 square * inverse
             )
-            cur[target, t, pl.ds(at, 8), :] = new
+            target[t, pl.ds(at, 8), :] = new
             if main and t != 2:
                 m = t - t // 3
                 tanh_sum[m, pl.ds(at - FIRST, 8), :] += jnp.tanh(new)
@@ -495,35 +507,37 @@
     within = make_masks(1)
     below = make_masks(2)
 
-    def substep(step, carry):
-        source = step & 1
-        target = 1 - source
+    def substep(source, target):
         update(source, target, 1, above, None, False)
         update(source, target, 2, above, ("down", 0, 7), False)
         update(source, target, 3, within, ("up", 0, 0), True)
 
-        def middle(chunk, inner_carry):
-            update(source, target, chunk, within, None, True)
-            return inner_carry
-
-        lax.fori_loop(4, 34, middle, 0)
+        def middle(group, carry):
+            for k in range(UNROLL):
+                update(source, target, 4 + group * UNROLL + k, within, None, True)
+            return carry
+
+        lax.fori_loop(0, 30 // UNROLL, middle, 0)
         update(source, target, 34, within, ("down", 1, 7), True)
         update(source, target, 35, below, ("up", 1, 0), False)
         update(source, target, 36, below, None, False)
-        return carry
-
-    lax.fori_loop(0, SUB, substep, 0)
+
+    def two_substeps(pair, carry):
+        substep(cur_a, cur_b)
+        substep(cur_b, cur_a)
+        return carry
+
+    lax.fori_loop(0, SUB // 2, two_substeps, 0)
 
     last = SUB % 2
 
-    def finish(chunk, sums):
-        burn, emit = sums
+    def finish(chunk, burn, emit):
         at = pl.multiple_of(chunk * 8, 8)
         for q in range(2):
             for half in range(2):
                 t = 3 * q + half
                 cols = slice(LANES * half, LANES * (half + 1))
-                final = cur[last, t, pl.ds(FIRST + at, 8), :]
+                final = cur[last][t, pl.ds(FIRST + at, 8), :]
                 level_out[q, pl.ds(at, 8), cols] = final
                 burn = burn + (0.5 - 0.5 * jnp.tanh(final))
                 kind = fuel_class[q, pl.ds(at, 8), cols]
@@ -538,7 +552,25 @@
         return burn, emit
 
     blank = jnp.zeros((8, LANES), f32)
-    burn, emit = lax.fori_loop(0, 32, finish, (blank, blank))
+    sums = [blank] * 4
+
+    def finish_group(group, totals):
+        totals = list(totals)
+        for k in range(FINISH_UNROLL):
+            pair = 2 * (k % 2)
+            totals[pair], totals[pair + 1] = finish(
+                group * FINISH_UNROLL + k, totals[pair], totals[pair + 1]
+            )
+        return tuple(totals)
+
+    sums = lax.fori_loop(0, 32 // FINISH_UNROLL, finish_group, tuple(sums))
+    burn = sums[0] + sums[2]
+    emit = sums[1] + sums[3]
+    devices = across * down
+
+    def spread(row, value):
+        heat_out[pl.ds(row, devices, stride=HEAT_ROWS), :] = jnp.broadcast_to(value, (devices, LANES))
+
     source_lane = lax.broadcasted_iota(i32, (LANES, LANES), 0) // REF
     target_lane = lanes((LANES, LANES))
     for q in range(2):
@@ -554,23 +586,42 @@
                     precision=lax.Precision.HIGHEST,
                     preferred_element_type=f32,
                 )
-        heat_out[8 * q : 8 * q + 8, :] = packed
+        for row in range(8):
+            spread(8 * q + row, packed[row : row + 1, :])
     burn_sum = jnp.sum(jnp.sum(burn, axis=0, keepdims=True), axis=1, keepdims=True)
     emit_sum = jnp.sum(jnp.sum(emit, axis=0, keepdims=True), axis=1, keepdims=True)
     lane1 = lanes((1, LANES))
-    heat_out[16:17, :] = jnp.where(lane1 == 0, burn_sum, jnp.where(lane1 == 1, emit_sum, 0.0))
-
-    load.wait()
+    spread(16, jnp.where(lane1 == 0, burn_sum, jnp.where(lane1 == 1, emit_sum, 0.0)))
+
+
+def air_kernel(across, down, pos, received, air_hbm, air_out, air, fresh, sides, sem_in, sem_out):
+    def load(number):
+        return pltpu.make_async_copy(
+            air_hbm.at[:, number], air.at[:, number + 1, 8:136, :], sem_in.at[number]
+        )
+
+    def store(number):
+        return pltpu.make_async_copy(fresh.at[:, number], air_out.at[:, number], sem_out.at[number])
+
+    levels = 16
+    for number in range(levels):
+        load(number).start()
+    lane = lanes()
+    is0 = lane == 0
+    is127 = lane == 127
     zero = jnp.zeros((128, LANES), f32)
     for f in range(3):
         air[f, 0, 8:136, :] = zero
-        air[f, 17, 8:136, :] = zero
+        air[f, levels + 1, 8:136, :] = zero
     keep_north = jnp.where(pos[0] > 0, 1.0, 0.0).astype(f32)
     keep_south = jnp.where(pos[0] < down - 1, 1.0, 0.0).astype(f32)
     keep_west = jnp.where(pos[1] > 0, 1.0, 0.0).astype(f32)
     keep_east = jnp.where(pos[1] < across - 1, 1.0, 0.0).astype(f32)
+
+    def got(row):
+        return received[pl.ds(row, PIECES, stride=REC2), :]
+
     for group in range(3):
-        strips[...] = jnp.zeros(strips.shape, f32)
         rows = got(ROWS2 + group)
         for p in range(32):
             number = 32 * group + p
@@ -578,44 +629,54 @@
             at = 7 if number < 48 else 136
             keep = keep_north if number < 48 else keep_south
             air[plane // 16, plane % 16 + 1, at : at + 1, :] = rows[p : p + 1, :] * keep
-    sides = []
+    lane32 = lanes((32, LANES))
     for group in range(4):
-        sides.append(got(COLS2 + group) * jnp.where(lane32 % 2 == 1, keep_east, keep_west))
-    for group in range(4):
-        turned[0, 32 * group : 32 * group + 32, :LANES] = sides[group]
+        sides[32 * group : 32 * group + 32, :] = got(COLS2 + group) * jnp.where(
+            lane32 % 2 == 1, keep_east, keep_west
+        )
+
+    load(0).wait()
 
     def air_level(number, carry):
-        def air_rows(chunk, inner_carry):
-            at = 8 + chunk * 8
-            halo = turned[0, pl.ds(chunk * 8, 8), :LANES]
-            u = air[0, number + 1, pl.ds(at, 8), :]
-            v = air[1, number + 1, pl.ds(at, 8), :]
-            for f in range(3):
-                x = u if f == 0 else v if f == 1 else air[2, number + 1, pl.ds(at, 8), :]
-                up = air[f, number + 1, pl.ds(at - 1, 8), :]
-                dn = air[f, number + 1, pl.ds(at + 1, 8), :]
-                over = air[f, number + 2, pl.ds(at, 8), :]
-                under = air[f, number, pl.ds(at, 8), :]
-                mine = pltpu.roll(halo, LANES - 1 - 2 * (f * 16 + number), 1)
-                west = rolled(jnp.where(is127, mine, x), 1)
-                east = rolled(jnp.where(is0, mine, x), -1)
-                around = (up + dn) + (west + east)
-                advect = u * (dn - up) + v * (east - west)
-                air_new[f, number, pl.ds(chunk * 8, 8), :] = (
-                    (1.0 - 4.0 * viscosity - 2.0 * mixing) * x
-                    + viscosity * around
-                    - (0.5 * courant) * advect
-                    + mixing * (over + under)
-                )
+        @pl.when(number < levels - 1)
+        def _():
+            load(number + 1).wait()
+
+        def air_rows(group, inner_carry):
+            for k in range(AIR_UNROLL):
+                row = group * (8 * AIR_UNROLL) + k * 8
+                at = 8 + row
+                halo = sides[pl.ds(row, 8), :]
+                x = [air[f, number + 1, pl.ds(at, 8), :] for f in range(3)]
+                for f in range(3):
+                    up = air[f, number + 1, pl.ds(at - 1, 8), :]
+                    dn = air[f, number + 1, pl.ds(at + 1, 8), :]
+                    over = air[f, number + 2, pl.ds(at, 8), :]
+                    under = air[f, number, pl.ds(at, 8), :]
+                    mine = pltpu.roll(halo, LANES - 1 - 2 * (f * 16 + number), 1)
+                    west = rolled(jnp.where(is127, mine, x[f]), 1)
+                    east = rolled(jnp.where(is0, mine, x[f]), -1)
+                    around = (up + dn) + (west + east)
+                    advect = x[0] * (dn - up) + x[1] * (east - west)
+                    fresh[f, number, pl.ds(row, 8), :] = (
+                        (1.0 - 4.0 * viscosity - 2.0 * mixing) * x[f]
+                        + viscosity * around
+                        - (0.5 * courant) * advect
+                        + mixing * (over + under)
+                    )
             return inner_carry
 
-        lax.fori_loop(0, 16, air_rows, 0)
-        return carry
-
-    lax.fori_loop(0, 16, air_level, 0)
-    store = pltpu.make_async_copy(air_new, air_out, sem_out)
-    store.start()
-    store.wait()
+        lax.fori_loop(0, 16 // AIR_UNROLL, air_rows, 0)
+        store(number).start()
+        return carry
+
+    lax.fori_loop(0, levels, air_level, 0)
+
+    def drain(number, carry):
+        store(number).wait()
+        return carry
+
+    lax.fori_loop(0, levels, drain, 0)
 
 
 def heat_kernel(cells, pos, blocks, gathered, air_in, air_out, totals, plane, sem):
@@ -625,14 +686,16 @@
     sums = jnp.sum(
         gathered[pl.ds(16, devices, stride=HEAT_ROWS), :], axis=0, keepdims=True
     )
-    totals[...] = sums * (1.0 / cells)
+    lane1 = lanes((1, LANES))
+    for k in range(2):
+        totals[k] = jnp.sum(jnp.where(lane1 == k, sums, 0.0)) * (1.0 / cells)
     load.wait()
     lane = lanes()
     tile_rows = 128 // BA
 
     def place(j, carry):
-        row = blocks[j, 0] - pos[0] * tile_rows
-        col = blocks[j, 1] - pos[1] * tile_rows
+        row = blocks[0, j] - pos[0] * tile_rows
+        col = blocks[1, j] - pos[1] * tile_rows
         inside = (row >= 0) & (row < tile_rows) & (col >= 0) & (col < tile_rows)
 
         @pl.when(inside)
@@ -645,7 +708,7 @@
 
         return carry
 
-    lax.fori_loop(0, blocks.shape[0], place, 0)
+    lax.fori_loop(0, blocks.shape[1], place, 0)
     store = pltpu.make_async_copy(plane, air_out.at[2, 0], sem)
     store.start()
     store.wait()
@@ -660,6 +723,8 @@
     smem = pl.BlockSpec(memory_space=pltpu.SMEM)
     vmem = pl.BlockSpec(memory_space=pltpu.VMEM)
     anywhere = pl.BlockSpec(memory_space=pl.ANY)
+    blocks = blocks.T
+    adjacency = adjacency.T
     packed = pl.pallas_call(
         pack_kernel,
         out_shape=jax.ShapeDtypeStruct((devices * REC1, LANES), f32),
@@ -674,28 +739,36 @@
         name="pack",
     )(pos, blocks, level_set, fuel_class, air_state.reshape(48 * 128, LANES))
     relayed = lax.all_to_all(packed.reshape(devices, REC1, LANES), both, 0, 0)
+    index = pl.pallas_call(
+        lambda *refs: index_kernel(across, down, *refs),
+        out_shape=jax.ShapeDtypeStruct((devices * WORDS,), i32),
+        in_specs=[smem, smem, smem],
+        out_specs=smem,
+        scratch_shapes=[pltpu.SMEM((blocks.shape[1],), i32), pltpu.SMEM((devices,), i32)],
+        cost_estimate=pl.CostEstimate(flops=40_000_000, transcendentals=0, bytes_accessed=10_000),
+        name="index",
+    )(pos, blocks, adjacency)
     chosen = pl.pallas_call(
-        lambda *refs: select_kernel(across, down, *refs),
+        select_kernel,
         out_shape=jax.ShapeDtypeStruct((devices * REC2, LANES), f32),
-        in_specs=[smem, smem, smem, vmem],
+        in_specs=[smem, vmem],
         out_specs=vmem,
-        scratch_shapes=[pltpu.SMEM((blocks.shape[0],), i32), pltpu.SMEM((devices,), i32)],
         name="select",
-    )(pos, blocks, adjacency, relayed.reshape(devices * REC1, LANES))
+    )(index, relayed.reshape(devices * REC1, LANES))
     received = lax.all_to_all(chosen.reshape(devices, REC2, LANES), both, 0, 0)
-    props = jnp.pad(fuel_props, ((0, 3), (0, LANES - fuel_props.shape[1])), constant_values=1.0)
-    level_next, fuel_next, heat, air_next = pl.pallas_call(
+    received = received.reshape(devices * REC2, LANES)[: PIECES * REC2]
+    level_next, fuel_next, heat = pl.pallas_call(
         lambda *refs: fire_kernel(across, down, *refs),
         out_shape=(
             jax.ShapeDtypeStruct(level_set.shape, f32),
             jax.ShapeDtypeStruct(level_set.shape, f32),
-            jax.ShapeDtypeStruct((HEAT_ROWS, LANES), f32),
-            jax.ShapeDtypeStruct(air_state.shape, f32),
+            jax.ShapeDtypeStruct((devices * HEAT_ROWS, LANES), f32),
         ),
-        in_specs=[smem, smem, vmem, vmem, vmem, vmem, vmem, anywhere],
-        out_specs=(vmem, vmem, vmem, anywhere),
+        in_specs=[smem, smem, smem, vmem, vmem, vmem, vmem],
+        out_specs=(vmem, vmem, vmem),
         scratch_shapes=[
-            pltpu.VMEM((2, 5, EXT, LANES), f32),
+            pltpu.VMEM((5, EXT, LANES), f32),
+            pltpu.VMEM((5, EXT, LANES), f32),
             pltpu.VMEM((5, EXT, LANES), f32),
             pltpu.VMEM((5, EXT, LANES), f32),
             pltpu.VMEM((2, 5, 40, LANES), f32),
@@ -704,40 +777,37 @@
             pltpu.VMEM((4, 256, LANES), f32),
             pltpu.VMEM((2, 5, 8, LANES), i32),
             pltpu.VMEM((4, 32, LANES), f32),
+        ],
+        name="fire",
+    )(pos, adjacency, fuel_props, received, level_set, fuel_left, fuel_class)
+    gathered = lax.all_to_all(heat.reshape(devices, 1, HEAT_ROWS * LANES), both, 0, 0)
+    gathered = gathered.reshape(devices * HEAT_ROWS, LANES)
+    air_next = pl.pallas_call(
+        lambda *refs: air_kernel(across, down, *refs),
+        out_shape=jax.ShapeDtypeStruct(air_state.shape, f32),
+        in_specs=[smem, vmem, anywhere],
+        out_specs=anywhere,
+        scratch_shapes=[
             pltpu.VMEM((3, 18, 144, LANES), f32),
             pltpu.VMEM((3, 16, 128, LANES), f32),
-            pltpu.SemaphoreType.DMA(()),
-            pltpu.SemaphoreType.DMA(()),
+            pltpu.VMEM((128, LANES), f32),
+            pltpu.SemaphoreType.DMA((16,)),
+            pltpu.SemaphoreType.DMA((16,)),
         ],
-        name="fire",
-    )(
-        pos,
-        adjacency,
-        props,
-        received.reshape(devices * REC2, LANES)[: PIECES * REC2],
-        level_set,
-        fuel_left,
-        fuel_class,
-        air_state,
-    )
-    spread = jnp.broadcast_to(
-        heat.reshape(1, 1, HEAT_ROWS * LANES), (devices, 1, HEAT_ROWS * LANES)
-    )
-    gathered = lax.all_to_all(spread, both, 0, 0).reshape(devices * HEAT_ROWS, LANES)
-    cells = blocks.shape[0] * level_set.shape[1] * level_set.shape[2]
+        cost_estimate=pl.CostEstimate(flops=80_000_000, transcendentals=0, bytes_accessed=6_300_000),
+        name="air",
+    )(pos, received, air_state)
+    cells = blocks.shape[1] * level_set.shape[1] * level_set.shape[2]
     air_next, totals = pl.pallas_call(
         lambda *refs: heat_kernel(cells, *refs),
-        out_shape=(
-            jax.ShapeDtypeStruct(air_state.shape, f32),
-            jax.ShapeDtypeStruct((1, LANES), f32),
-        ),
+        out_shape=(jax.ShapeDtypeStruct(air_state.shape, f32), jax.ShapeDtypeStruct((2,), f32)),
         in_specs=[smem, smem, vmem, anywhere],
-        out_specs=(anywhere, vmem),
+        out_specs=(anywhere, smem),
         scratch_shapes=[pltpu.VMEM((128, LANES), f32), pltpu.SemaphoreType.DMA(())],
         input_output_aliases={3: 0},
         name="heat",
     )(pos, blocks, gathered, air_next)
-    return (air_next, level_next, fuel_next, totals[0, 0:2])
+    return (air_next, level_next, fuel_next, totals)
 
 
 def solution(mesh):

time: 168 us -> 82.5 us (0.49)
  Pallas kernels: 110 us -> 43.7 us
  waiting for transfers between devices: 25.5 us -> 8.89 us
  local copies, waits for them, and re-layouts: 6.11 us -> 1.44 us
  blocking collectives: 13.3 us -> 16.7 us
    pallas_call x1, Pallas kernels: 91.9 us -> 14.5 us  [local(): pl.pallas_call(lambda *refs: fire_kernel(across, down, *refs), out_shape=...]
    pallas_call x1 -> x3, Pallas kernels: 8.05 us -> 18.2 us  [the longest x1 7.99 us: local(): pl.pallas_call(lambda *refs: air_kernel(across, down, *refs), out_shape=j...]
    all_to_all x1, waiting for transfers between devices: 12.8 us -> 2.87 us  [local(): lax.all_to_all(heat.reshape(devices, 1, HEAT_ROWS * LANES), both, 0, 0)]
    all_to_all x1, waiting for transfers between devices: 12.7 us -> 6.01 us  [local(): relayed = lax.all_to_all(packed.reshape(devices, REC1, LANES), both, 0, 0)]
    all_to_all x1, blocking collectives: 13.3 us -> 16.7 us  [local(): received = lax.all_to_all(chosen.reshape(devices, REC2, LANES), both, 0, 0)]
    unnamed x10 -> x4, local copies, waits for them, and re-layouts: 3.56 us -> 1.44 us
  transfers between devices with their start and end apart: 2 -> 2, of which waited for: 2 -> 2; matrix products, arithmetic and copies ran while one was open for 1% -> 0% of each run, Pallas kernels for 0% -> 19%
where the time goes in v2:
time: 82.5 us; the launch traced here: 82.3 us
  Pallas kernels  43.7 us (53%)
  blocking collectives  16.7 us (20%)
  starting transfers between devices  10.3 us (12%)
  waiting for transfers between devices  8.89 us (11%)
  local copies, waits for them, and re-layouts  1.44 us (2%)
    all_to_all x1, blocking collectives, local(): received = lax.all_to_all(chosen.reshape(devices, REC2, LANES), both, 0, 0)  16.7 us
    pallas_call x1, Pallas kernels, local(): pl.pallas_call(lambda *refs: fire_kernel(across, down, *refs), out_shape=...  14.5 us
    pallas_call x1, Pallas kernels, local(): pl.pallas_call(lambda *refs: air_kernel(across, down, *refs), out_shape=j...  7.99 us
    all_to_all x1, starting transfers between devices, local(): relayed = lax.all_to_all(packed.reshape(devices, REC1, LANES), both, 0, 0)  7.76 us
    pallas_call x1, Pallas kernels, local(): pl.pallas_call(lambda *refs: index_kernel(across, down, *refs), out_shape...  7.4 us
    pallas_call x1, Pallas kernels, local(): pl.pallas_call(pack_kernel, out_shape=jax.ShapeDtypeStruct((devices * REC...  7.03 us
    all_to_all x1, waiting for transfers between devices, local(): relayed = lax.all_to_all(packed.reshape(devices, REC1, LANES), both, 0, 0)  6.01 us
    pallas_call x1, Pallas kernels, local(): pl.pallas_call(lambda *refs: heat_kernel(cells, *refs), out_shape=(jax.Sh...  3.93 us
  transfers between devices with their start and end apart: 2, of which 2 were waited for; matrix products, arithmetic and copies ran while one was open for 0% of the time, Pallas kernels for 19%

profile of v2, /device:TPU:0, one launch (start us, length us, event | category | flops | bytes accessed | tf_op | source)
XLA Modules:
  0.0 82.3 jit_solution(679739998057690625)
XLA Ops:
  0.6 0.6 pad_add_fusion.refs_0_.pos
  1.2 7.0 %pack.1 = f32[768,128]{1,0:T(8,128)} custom-call(s32[2]{0:T(128)} %pad_add_fusion.refs_0_.pos, s32[2,64]{1,0:T(2,128)} %bitcast.19, f32[2,256,256]{2,1,0:T(8,128)} %refs_4_.1, s32[2,256,256]{2,1,0:T(8,128)} %refs_6_.1, f32[6144,128]{1,0:T(8,128)} %bitcast.11), custom_call_target="tpu_custom_call" | custom-call | tf_op jit(solution)/shard_map/pack/pallas_call | solution.py:728
  8.2 7.8 %all-to-all-start = ((f32[32,24,128]{2,1,0:T(8,128)}), f32[32,24,128]{2,1,0:T(8,128)S(1)}, u32[]{:S(2)}, u32[]{:S(2)}) async-start(f32[32,24,128]{2,1,0:T(8,128)} %bitcast.16), calls=%async_computation | async-start | bytes 786432 | tf_op jit(solution)/shard_map/all_to_all | solution.py:741
  16.0 7.4 %index.1 = s32[1280]{0:T(1024)} custom-call(s32[2]{0:T(128)} %pad_add_fusion.refs_0_.pos, s32[2,64]{1,0:T(2,128)} %bitcast.20, s32[4,64]{1,0:T(4,128)} %bitcast.22), custom_call_target="tpu_custom_call" | custom-call | flops 40000000 | bytes 10000 | tf_op jit(solution)/shard_map/index/pallas_call | solution.py:742
  23.4 6.0 %all-to-all-done = f32[32,24,128]{2,1,0:T(8,128)S(1)} async-done(((f32[32,24,128]{2,1,0:T(8,128)}), f32[32,24,128]{2,1,0:T(8,128)S(1)}, u32[]{:S(2)}, u32[]{:S(2)}) %all-to-all-start) | async-done | bytes 393248 | tf_op jit(solution)/shard_map/all_to_all | solution.py:741
  29.4 0.0 copy-start
  29.4 0.7 copy-done
  30.2 2.8 %select.1 = f32[768,128]{1,0:T(8,128)} custom-call(s32[1280]{0:T(1024)} %index.1, f32[768,128]{1,0:T(8,128)} %bitcast.14), custom_call_target="tpu_custom_call" | custom-call | tf_op jit(solution)/shard_map/select/pallas_call | solution.py:751
  33.0 16.7 %all_to_all.15 = f32[32,24,128]{2,1,0:T(8,128)} all-to-all(f32[32,24,128]{2,1,0:T(8,128)} %bitcast.15), channel_id=1, replica_groups=mesh['gx'=4,'gy'=8] {'gx','gy'}, dimensions={0} | all-to-all | bytes 786432 | tf_op jit(solution)/shard_map/all_to_all | solution.py:758
  49.7 14.5 %fire.1 = (f32[2,256,256]{2,1,0:T(8,128)}, f32[2,256,256]{2,1,0:T(8,128)}, f32[544,128]{1,0:T(8,128)}) custom-call(s32[2]{0:T(128)} %pad_add_fusion.refs_0_.pos, s32[4,64]{1,0:T(4,128)} %bitcast.23, f32[5,13]{1,0:T(8,128)} %refs_2_.2, f32[768,128]{1,0:T(8,128)} %bitcast.12, f32[2,256,256]{2,1,0:T(8,128)} %refs_4_.1, f32[2,256,256]{2,1,0:T(8,128)} %refs_5_.1, ...), custom_call_target="tpu_custom_call" | custom-call | tf_op jit(solution)/shard_map/fire/pallas_call | solution.py:760
  64.2 2.6 %all-to-all-start.2 = ((f32[32,1,2176]{2,1,0:T(1,128)}), f32[32,1,2176]{2,1,0:T(1,128)S(1)}, u32[]{:S(2)}, u32[]{:S(2)}) async-start(f32[32,1,2176]{2,1,0:T(1,128)} %bitcast.18), calls=%async_computation.2 | async-start | bytes 557056 | tf_op jit(solution)/shard_map/all_to_all | solution.py:783
  66.8 8.0 %air.1.refs_3_ = f32[3,16,128,128]{3,2,1,0:T(8,128)} custom-call(s32[2]{0:T(128)} %pad_add_fusion.refs_0_.pos, f32[768,128]{1,0:T(8,128)} %bitcast.13, f32[3,16,128,128]{3,2,1,0:T(8,128)} %refs_2_.3), custom_call_target="tpu_custom_call" | custom-call | flops 80000000 | bytes 6300000 | tf_op jit(solution)/shard_map/air/pallas_call | solution.py:785
  74.8 2.9 %all-to-all-done.2 = f32[32,1,2176]{2,1,0:T(1,128)S(1)} async-done(((f32[32,1,2176]{2,1,0:T(1,128)}), f32[32,1,2176]{2,1,0:T(1,128)S(1)}, u32[]{:S(2)}, u32[]{:S(2)}) %all-to-all-start.2) | async-done | bytes 278560 | tf_op jit(solution)/shard_map/all_to_all | solution.py:783
  77.7 0.0 copy-start.1
  77.7 0.7 copy-done.1
  78.4 3.9 %heat.1 = (f32[3,16,128,128]{3,2,1,0:T(8,128)}, f32[2]{0:T(128)}) custom-call(s32[2]{0:T(128)} %pad_add_fusion.refs_0_.pos, s32[2,64]{1,0:T(2,128)} %bitcast.21, f32[544,128]{1,0:T(8,128)} %bitcast.17, f32[3,16,128,128]{3,2,1,0:T(8,128)} %air.1.refs_3_), custom_call_target="tpu_custom_call", output_to_operand_aliasing={{0}: (3, {})} | custom-call | tf_op jit(solution)/shard_map/heat/pallas_call | solution.py:801
Async XLA Ops:
  8.2 21.2 %all-to-all-start = ((f32[32,24,128]{2,1,0:T(8,128)}), f32[32,24,128]{2,1,0:T(8,128)S(1)}, u32[]{:S(2)}, u32[]{:S(2)}) async-start(f32[32,24,128]{2,1,0:T(8,128)} %bitcast.16), calls=%async_computation | async-start | bytes 786432 | tf_op jit(solution)/shard_map/all_to_all | solution.py:741
  29.4 0.7 copy-start
  64.2 13.5 %all-to-all-start.2 = ((f32[32,1,2176]{2,1,0:T(1,128)}), f32[32,1,2176]{2,1,0:T(1,128)S(1)}, u32[]{:S(2)}, u32[]{:S(2)}) async-start(f32[32,1,2176]{2,1,0:T(1,128)} %bitcast.18), calls=%async_computation.2 | async-start | bytes 557056 | tf_op jit(solution)/shard_map/all_to_all | solution.py:783
  77.7 0.7 copy-start.1

commit v3 on v2

--- a/solution.py
+++ b/solution.py
@@ -17,6 +17,7 @@
 RATE_UNROLL = 12
 FINISH_UNROLL = 16
 AIR_UNROLL = 16
+EDGE_UNROLL = 2
 
 step_time = 0.25
 smoothing = 0.15
@@ -29,15 +30,11 @@
 SIDE = 0
 CORNER = 10
 WIND = 12
-COLS = 16
-ROWS = 20
-REC1 = 24
+REC1 = 16
 CORNER2 = 10
 WINDA = 11
 WINDB = 13
-COLS2 = 15
-ROWS2 = 19
-REC2 = 24
+REC2 = 16
 HEAT_ROWS = 17
 
 TOP = 8
@@ -64,8 +61,8 @@
     return jnp.take_along_axis(table, index, axis=1, mode="promise_in_bounds")
 
 
-def pack_kernel(pos, blocks, level, fuel_class, air_hbm, out, air, strip, edge, sem):
-    load = pltpu.make_async_copy(air_hbm, air, sem)
+def pack_kernel(pos, blocks, level, fuel_class, air_hbm, out, air, strip, sem):
+    load = pltpu.make_async_copy(air_hbm.at[0:2, 0], air, sem)
     load.start()
     lane256 = lanes((256, LANES))
     lane16 = lanes((16, LANES))
@@ -123,8 +120,8 @@
         @pl.when(inside)
         def _():
             start = pl.multiple_of(row * BA, BA)
-            u = air[pl.ds(start, BA), :]
-            v = air[pl.ds(16 * 128 + start, BA), :]
+            u = air[0, pl.ds(start, BA), :]
+            v = air[1, pl.ds(start, BA), :]
             shift = LANES - col * BA
             u = pltpu.roll(u, shift, 1)
             v = pltpu.roll(v, shift, 1)
@@ -136,128 +133,142 @@
 
     lax.fori_loop(0, blocks.shape[1], find, jnp.int32(0))
 
-    edge[0:48, :] = air[pl.ds(127, 48, stride=128), :]
-    edge[48:96, :] = air[pl.ds(0, 48, stride=128), :]
-    for group in range(3):
-        place(ROWS + group, 0, edge[32 * group : 32 * group + 32, :])
-
-    lane8 = lanes()
-
-    def columns(chunk, carry):
-        base = pl.multiple_of(chunk * 8, 8)
-        total = jnp.zeros((8, LANES), f32)
-        for plane in range(48):
-            x = air[pl.ds(plane * 128 + base, 8), :]
-            total = jnp.where(lane8 // 2 == plane, rolled(x, 1 + 2 * plane), total)
-        edge[pl.ds(base, 8), :] = total
-        return carry
-
-    lax.fori_loop(0, 16, columns, 0)
-    for group in range(4):
-        place(COLS + group, 0, edge[32 * group : 32 * group + 32, :])
     if out.shape[0] > PIECES * REC1:
         out[PIECES * REC1 :, :] = jnp.zeros((out.shape[0] - PIECES * REC1, LANES), f32)
 
 
-WORDS = 40
-
-
-def index_kernel(across, down, pos, blocks, adjacency, out, wind_row, count):
+WORDS = 15
+
+
+def edge_kernel(air_hbm, ready, first_rows, last_rows, columns, air, sem):
+    load = pltpu.make_async_copy(air_hbm, air, sem)
+    load.start()
+    load.wait()
+    first_rows[...] = air[pl.ds(0, 48, stride=128), :]
+    last_rows[...] = air[pl.ds(127, 48, stride=128), :]
+    lane = lanes()
+
+    def gather(group, carry):
+        for k in range(EDGE_UNROLL):
+            base = pl.multiple_of((group * EDGE_UNROLL + k) * 8, 8)
+            total = jnp.zeros((8, LANES), f32)
+            for plane in range(48):
+                x = air[pl.ds(plane * 128 + base, 8), :]
+                total = jnp.where(lane // 2 == plane, rolled(x, 1 + 2 * plane), total)
+            columns[pl.ds(base, 8), :] = total
+        return carry
+
+    lax.fori_loop(0, 16 // EDGE_UNROLL, gather, 0)
+
+
+def index_kernel(across, pos, blocks, adjacency, out, padded):
     total = blocks.shape[1]
-    devices = across * down
+    tiles = out.shape[1] // LANES
     relay = jnp.minimum(pos[0] * across + pos[1], PIECES - 1)
-    tile_rows = 128 // BA
-
-    def clear(d, carry):
-        count[d] = 0
-        return carry
-
-    lax.fori_loop(0, devices, clear, 0)
-
-    def number(j, carry):
-        tile = (blocks[0, j] // tile_rows) * across + blocks[1, j] // tile_rows
-        slot = count[tile]
-        count[tile] = slot + 1
-        wind_row[j] = tile * REC1 + WIND + slot
-        return carry
-
-    lax.fori_loop(0, total, number, 0)
-    spare_side = relay // 8
+    padded[...] = jnp.zeros(padded.shape, i32)
+    padded[0:2, 0:total] = blocks[...]
+    padded[8:12, 0:total] = adjacency[...]
+
+    def row(number):
+        return [
+            jnp.broadcast_to(padded[number : number + 1, LANES * u : LANES * (u + 1)], (8, LANES))
+            for u in range(tiles)
+        ]
+
+    def lookup(table, index):
+        found = []
+        for u in range(tiles):
+            value = pick(table[0], index[u] & (LANES - 1))
+            for v in range(1, tiles):
+                value = jnp.where(index[u] >> 7 == v, pick(table[v], index[u] & (LANES - 1)), value)
+            found.append(value)
+        return found
+
+    def each(f, *rows):
+        return [f(*values) for values in zip(*rows)]
+
+    lane = lanes()
+    tile_of = each(lambda r, c: (r >> 2) * across + (c >> 2), row(0), row(1))
+    before = lax.broadcasted_iota(i32, (LANES, LANES), 0)
+    here = lanes((LANES, LANES))
+    as_rows = [jnp.broadcast_to(t[0:1, :].astype(f32), (LANES, LANES)) for t in tile_of]
+    as_cols = [t.T for t in as_rows]
+    wind_row = []
+    for u in range(tiles):
+        slot = jnp.zeros((1, LANES), f32)
+        for v in range(u + 1):
+            same = (as_cols[v] == as_rows[u]) & (before + LANES * v < here + LANES * u)
+            slot = slot + jnp.sum(jnp.where(same, 1.0, 0.0), axis=0, keepdims=True)
+        wind_row.append(tile_of[u] * REC1 + WIND + jnp.broadcast_to(slot.astype(i32), (8, LANES)))
+    near = [row(8 + s) for s in range(4)]
+    safe = [each(lambda n: jnp.maximum(n, 0), near[s]) for s in range(4)]
+
+    def diagonal(s, t):
+        by_row = lookup(near[t], safe[s])
+        by_col = lookup(near[s], safe[t])
+        return each(
+            lambda n, m, r, c: jnp.maximum(jnp.where(n >= 0, r, jnp.where(m >= 0, c, 0)), 0),
+            near[s],
+            near[t],
+            by_row,
+            by_col,
+        )
+
+    nw, ne, sw, se = diagonal(0, 2), diagonal(0, 3), diagonal(1, 2), diagonal(1, 3)
+    spare_side = relay >> 3
     upper = relay >= 16
 
-    def serve(d, carry):
-        base = d * WORDS
-        for q in range(2):
-            i = 2 * d + q
-            near = [adjacency[s, i] for s in range(4)]
-            safe = [jnp.maximum(near[s], 0) for s in range(4)]
-
-            def diagonal(s, t):
-                by_row = adjacency[t, safe[s]]
-                by_col = adjacency[s, safe[t]]
-                return jnp.maximum(jnp.where(near[s] >= 0, by_row, jnp.where(near[t] >= 0, by_col, 0)), 0)
-
-            nw, ne, sw, se = diagonal(0, 2), diagonal(0, 3), diagonal(1, 2), diagonal(1, 3)
-
-            def side_row(j, s):
-                return (j // 2) * REC1 + SIDE + (j % 2) * 5 + s
-
-            for s in range(4):
-                out[base + 5 * q + s] = side_row(safe[s], opposite(s))
-            spare = jnp.where(
-                spare_side == 0,
-                safe[1],
-                jnp.where(spare_side == 1, safe[0], jnp.where(spare_side == 2, safe[3], safe[2])),
-            )
-            out[base + 5 * q + 4] = side_row(spare, 4)
-            for k, j in enumerate((ne, se, sw, nw)):
-                out[base + 10 + 4 * q + k] = (j // 2) * REC1 + CORNER + j % 2
-            winds = (
-                i,
-                jnp.where(upper, safe[0], safe[1]),
-                safe[3],
-                safe[2],
-                jnp.where(upper, ne, se),
-                jnp.where(upper, nw, sw),
-            )
-            for k, j in enumerate(winds):
-                out[base + 18 + 6 * q + k] = wind_row[j]
-        a = d // across
-        b = d % across
-        north = jnp.where(a > 0, d - across, d)
-        south = jnp.where(a < down - 1, d + across, d)
-        out[base + 30] = jnp.where(b < across - 1, d + 1, d) * REC1 + COLS
-        out[base + 31] = jnp.where(b > 0, d - 1, d) * REC1 + COLS
-        out[base + 32] = north * REC1 + ROWS
-        out[base + 33] = jnp.where(relay < 16, north, south) * REC1 + ROWS + 1
-        out[base + 34] = south * REC1 + ROWS + 2
-        return carry
-
-    lax.fori_loop(0, devices, serve, 0)
-
-
-def select_kernel(index, received, out):
+    def side_row(j, s):
+        return each(lambda b: (b >> 1) * REC1 + SIDE + (b & 1) * 5 + s, j)
+
+    def choose(flag, yes, no):
+        return each(lambda a, b: jnp.where(flag, a, b), yes, no)
+
+    words = [side_row(safe[s], opposite(s)) for s in range(4)]
+    spare = choose(
+        spare_side == 0,
+        safe[1],
+        choose(spare_side == 1, safe[0], choose(spare_side == 2, safe[3], safe[2])),
+    )
+    words.append(side_row(spare, 4))
+    for j in (ne, se, sw, nw):
+        words.append(each(lambda b: (b >> 1) * REC1 + CORNER + (b & 1), j))
+    words.append(wind_row)
+    for j in (
+        choose(upper, safe[0], safe[1]),
+        safe[3],
+        safe[2],
+        choose(upper, ne, se),
+        choose(upper, nw, sw),
+    ):
+        words.append(lookup(wind_row, j))
+    for number, word in enumerate(words):
+        for u in range(tiles):
+            out[number : number + 1, LANES * u : LANES * (u + 1)] = word[u][0:1, :]
+    out[WORDS : WORDS + 1, :] = jnp.zeros((1, out.shape[1]), i32)
+
+
+def select_kernel(index, received, north, south, out):
     lane1 = lanes((1, LANES))
     lane_col = lane1 % 32 < 16
     first_half = lane1 < 64
     quarter = lane1 // 16
-    odd = lane1 % 2 == 1
 
     def one(d):
-        def take(word, more=0):
-            return received[pl.ds(index[d * WORDS + word] + more, 1), :]
+        def take(word, q):
+            return received[pl.ds(index[word, 2 * d + q], 1), :]
 
         def put(row, value):
             out[pl.ds(d * REC2 + row, 1), :] = value
 
         for row in range(10):
-            put(SIDE + row, take(row))
-        merged = take(17)
+            put(SIDE + row, take(row % 5, row // 5))
+        merged = take(8, 1)
         for k in range(7):
-            merged = jnp.where(quarter == k, take(10 + k), merged)
+            merged = jnp.where(quarter == k, take(5 + k % 4, k // 4), merged)
         put(CORNER2, merged)
         for q in range(2):
-            own, beyond, east, west, corner_east, corner_west = [take(18 + 6 * q + k) for k in range(6)]
+            own, beyond, east, west, corner_east, corner_west = [take(9 + k, q) for k in range(6)]
             put(WINDA + q, jnp.where(first_half, own, beyond))
             put(
                 WINDB + q,
@@ -267,12 +278,7 @@
                     jnp.where(first_half, west, corner_west),
                 ),
             )
-        for group in range(4):
-            put(COLS2 + group, jnp.where(odd, take(30, group), take(31, group)))
-        for group in range(3):
-            put(ROWS2 + group, take(32 + group))
-        for row in range(ROWS2 + 3, REC2):
-            put(row, jnp.zeros((1, LANES), f32))
+        put(REC2 - 1, jnp.zeros((1, LANES), f32))
 
     def serve(pair, carry):
         one(2 * pair)
@@ -292,6 +298,8 @@
     level,
     fuel_left,
     fuel_class,
+    west_side,
+    east_side,
     level_out,
     fuel_out,
     heat_out,
@@ -594,7 +602,7 @@
     spread(16, jnp.where(lane1 == 0, burn_sum, jnp.where(lane1 == 1, emit_sum, 0.0)))
 
 
-def air_kernel(across, down, pos, received, air_hbm, air_out, air, fresh, sides, sem_in, sem_out):
+def air_kernel(north, south, west_side, east_side, air_hbm, air_out, air, fresh, sides, sem_in, sem_out):
     def load(number):
         return pltpu.make_async_copy(
             air_hbm.at[:, number], air.at[:, number + 1, 8:136, :], sem_in.at[number]
@@ -613,27 +621,11 @@
     for f in range(3):
         air[f, 0, 8:136, :] = zero
         air[f, levels + 1, 8:136, :] = zero
-    keep_north = jnp.where(pos[0] > 0, 1.0, 0.0).astype(f32)
-    keep_south = jnp.where(pos[0] < down - 1, 1.0, 0.0).astype(f32)
-    keep_west = jnp.where(pos[1] > 0, 1.0, 0.0).astype(f32)
-    keep_east = jnp.where(pos[1] < across - 1, 1.0, 0.0).astype(f32)
-
-    def got(row):
-        return received[pl.ds(row, PIECES, stride=REC2), :]
-
-    for group in range(3):
-        rows = got(ROWS2 + group)
-        for p in range(32):
-            number = 32 * group + p
-            plane = number % 48
-            at = 7 if number < 48 else 136
-            keep = keep_north if number < 48 else keep_south
-            air[plane // 16, plane % 16 + 1, at : at + 1, :] = rows[p : p + 1, :] * keep
-    lane32 = lanes((32, LANES))
-    for group in range(4):
-        sides[32 * group : 32 * group + 32, :] = got(COLS2 + group) * jnp.where(
-            lane32 % 2 == 1, keep_east, keep_west
-        )
+    for plane in range(48):
+        at = (plane // 16, plane % 16 + 1)
+        air[at[0], at[1], 7:8, :] = north[plane : plane + 1, :]
+        air[at[0], at[1], 136:137, :] = south[plane : plane + 1, :]
+    sides[...] = jnp.where(lanes((128, LANES)) % 2 == 1, east_side[...], west_side[...])
 
     load(0).wait()
 
@@ -727,44 +719,63 @@
     adjacency = adjacency.T
     packed = pl.pallas_call(
         pack_kernel,
-        out_shape=jax.ShapeDtypeStruct((devices * REC1, LANES), f32),
+        out_shape=pltpu.VMEM((devices * REC1, LANES), f32),
         in_specs=[smem, smem, vmem, vmem, anywhere],
         out_specs=vmem,
         scratch_shapes=[
-            pltpu.VMEM((48 * 128, LANES), f32),
+            pltpu.VMEM((2, 128, LANES), f32),
             pltpu.VMEM((4, 40, LANES), f32),
-            pltpu.VMEM((128, LANES), f32),
             pltpu.SemaphoreType.DMA(()),
         ],
         name="pack",
-    )(pos, blocks, level_set, fuel_class, air_state.reshape(48 * 128, LANES))
+    )(pos, blocks, level_set, fuel_class, air_state)
     relayed = lax.all_to_all(packed.reshape(devices, REC1, LANES), both, 0, 0)
+    lanes_used = -(-blocks.shape[1] // LANES) * LANES
     index = pl.pallas_call(
-        lambda *refs: index_kernel(across, down, *refs),
-        out_shape=jax.ShapeDtypeStruct((devices * WORDS,), i32),
-        in_specs=[smem, smem, smem],
-        out_specs=smem,
-        scratch_shapes=[pltpu.SMEM((blocks.shape[1],), i32), pltpu.SMEM((devices,), i32)],
-        cost_estimate=pl.CostEstimate(flops=40_000_000, transcendentals=0, bytes_accessed=10_000),
+        lambda *refs: index_kernel(across, *refs),
+        out_shape=jax.ShapeDtypeStruct((WORDS + 1, lanes_used), i32),
+        in_specs=[smem, vmem, vmem],
+        out_specs=vmem,
+        scratch_shapes=[pltpu.VMEM((16, lanes_used), i32)],
+        cost_estimate=pl.CostEstimate(flops=20_000_000, transcendentals=0, bytes_accessed=10_000),
         name="index",
     )(pos, blocks, adjacency)
+    first_rows, last_rows, columns = pl.pallas_call(
+        edge_kernel,
+        out_shape=(
+            pltpu.VMEM((48, LANES), f32),
+            pltpu.VMEM((48, LANES), f32),
+            pltpu.VMEM((128, LANES), f32),
+        ),
+        in_specs=[anywhere, anywhere],
+        out_specs=(vmem, vmem, vmem),
+        scratch_shapes=[pltpu.VMEM((48 * 128, LANES), f32), pltpu.SemaphoreType.DMA(())],
+        cost_estimate=pl.CostEstimate(flops=30_000_000, transcendentals=0, bytes_accessed=3_200_000),
+        name="edge",
+    )(air_state.reshape(48 * 128, LANES), index)
+    north = near(lax.ppermute(last_rows, "gx", [(k, k + 1) for k in range(down - 1)]))
+    south = near(lax.ppermute(first_rows, "gx", [(k + 1, k) for k in range(down - 1)]))
     chosen = pl.pallas_call(
         select_kernel,
-        out_shape=jax.ShapeDtypeStruct((devices * REC2, LANES), f32),
-        in_specs=[smem, vmem],
+        out_shape=pltpu.VMEM((devices * REC2, LANES), f32),
+        in_specs=[smem, vmem, vmem, vmem],
         out_specs=vmem,
         name="select",
-    )(index, relayed.reshape(devices * REC1, LANES))
+    )(index, near(relayed.reshape(devices * REC1, LANES)), north, south)
+    columns, chosen = lax.optimization_barrier((columns, chosen))
+    west_side = near(lax.ppermute(columns, "gy", [(k, k + 1) for k in range(across - 1)]))
+    east_side = near(lax.ppermute(columns, "gy", [(k + 1, k) for k in range(across - 1)]))
     received = lax.all_to_all(chosen.reshape(devices, REC2, LANES), both, 0, 0)
     received = received.reshape(devices * REC2, LANES)[: PIECES * REC2]
+    received = near(received)
     level_next, fuel_next, heat = pl.pallas_call(
         lambda *refs: fire_kernel(across, down, *refs),
         out_shape=(
             jax.ShapeDtypeStruct(level_set.shape, f32),
             jax.ShapeDtypeStruct(level_set.shape, f32),
-            jax.ShapeDtypeStruct((devices * HEAT_ROWS, LANES), f32),
+            pltpu.VMEM((devices * HEAT_ROWS, LANES), f32),
         ),
-        in_specs=[smem, smem, smem, vmem, vmem, vmem, vmem],
+        in_specs=[smem, smem, smem, vmem, vmem, vmem, vmem] + [vmem] * 2,
         out_specs=(vmem, vmem, vmem),
         scratch_shapes=[
             pltpu.VMEM((5, EXT, LANES), f32),
@@ -779,13 +790,23 @@
             pltpu.VMEM((4, 32, LANES), f32),
         ],
         name="fire",
-    )(pos, adjacency, fuel_props, received, level_set, fuel_left, fuel_class)
+    )(
+        pos,
+        adjacency,
+        fuel_props,
+        received,
+        near(level_set),
+        near(fuel_left),
+        near(fuel_class),
+        west_side,
+        east_side,
+    )
     gathered = lax.all_to_all(heat.reshape(devices, 1, HEAT_ROWS * LANES), both, 0, 0)
-    gathered = gathered.reshape(devices * HEAT_ROWS, LANES)
+    gathered = near(gathered.reshape(devices * HEAT_ROWS, LANES))
     air_next = pl.pallas_call(
-        lambda *refs: air_kernel(across, down, *refs),
+        air_kernel,
         out_shape=jax.ShapeDtypeStruct(air_state.shape, f32),
-        in_specs=[smem, vmem, anywhere],
+        in_specs=[vmem, vmem, vmem, vmem, anywhere],
         out_specs=anywhere,
         scratch_shapes=[
             pltpu.VMEM((3, 18, 144, LANES), f32),
@@ -796,7 +817,7 @@
         ],
         cost_estimate=pl.CostEstimate(flops=80_000_000, transcendentals=0, bytes_accessed=6_300_000),
         name="air",
-    )(pos, received, air_state)
+    )(north, south, west_side, east_side, air_state)
     cells = blocks.shape[1] * level_set.shape[1] * level_set.shape[2]
     air_next, totals = pl.pallas_call(
         lambda *refs: heat_kernel(cells, *refs),
@@ -808,6 +829,10 @@
         name="heat",
     )(pos, blocks, gathered, air_next)
     return (air_next, level_next, fuel_next, totals)
+
+
+def near(x):
+    return pltpu.with_memory_space_constraint(x, pltpu.VMEM)
 
 
 def solution(mesh):

time: 82.5 us -> 77.8 us (0.943)
  starting transfers between devices: 10.3 us -> 28.4 us
  blocking collectives: 16.7 us -> 0 us
  Pallas kernels: 43.7 us -> 35.9 us
  waiting for transfers between devices: 8.89 us -> 11.4 us
  local copies, waits for them, and re-layouts: 1.44 us -> 0.02 us
    all_to_all x1 -> x0, blocking collectives: 16.7 us -> none  [local(): received = lax.all_to_all(chosen.reshape(devices, REC2, LANES), both, 0, 0)]
    ppermute x0 -> x4, starting transfers between devices: none -> 9.29 us  [the longest x1 4.55 us: local(): lax.ppermute(columns, 'gy', [(k, k + 1) for k in range(across - 1)])]
    all_to_all x0 -> x1, starting transfers between devices: none -> 6.79 us  [local(): received = lax.all_to_all(chosen.reshape(devices, REC2, LANES), both, 0, 0)]
    pallas_call x4 -> x5, Pallas kernels: 25.3 us -> 18.7 us  [the longest x1 6.99 us: local(): pl.pallas_call(air_kernel, out_shape=jax.ShapeDtypeStruct(air_state.shape...]
    all_to_all x1, waiting for transfers between devices: 6.01 us -> 0.01 us  [local(): relayed = lax.all_to_all(packed.reshape(devices, REC1, LANES), both, 0, 0)]
    ppermute x0 -> x4, waiting for transfers between devices: none -> 5.76 us  [the longest x1 2.92 us: local(): lax.ppermute(first_rows, 'gx', [(k + 1, k) for k in range(down - 1)])]
    all_to_all x1, starting transfers between devices: 2.59 us -> 4.87 us  [local(): lax.all_to_all(heat.reshape(devices, 1, HEAT_ROWS * LANES), both, 0, 0)]
    all_to_all x0 -> x1, waiting for transfers between devices: none -> 1.74 us  [local(): received = lax.all_to_all(chosen.reshape(devices, REC2, LANES), both, 0, 0)]
  transfers between devices with their start and end apart: 2 -> 7, of which waited for: 2 -> 5; matrix products, arithmetic and copies ran while one was open for 0% -> 0% of each run, Pallas kernels for 19% -> 15%
where the time goes in v3:
time: 77.8 us; the launch traced here: 77 us
  Pallas kernels  35.9 us (46%)
  starting transfers between devices  28.4 us (37%)
  waiting for transfers between devices  11.4 us (15%)
    pallas_call x1, Pallas kernels, local(): pl.pallas_call(lambda *refs: fire_kernel(across, down, *refs), out_shape=...  13.8 us
    all_to_all x1, starting transfers between devices, local(): relayed = lax.all_to_all(packed.reshape(devices, REC1, LANES), both, 0, 0)  7.47 us
    pallas_call x1, Pallas kernels, local(): pl.pallas_call(air_kernel, out_shape=jax.ShapeDtypeStruct(air_state.shape...  6.99 us
    all_to_all x1, starting transfers between devices, local(): received = lax.all_to_all(chosen.reshape(devices, REC2, LANES), both, 0, 0)  6.79 us
    all_to_all x1, starting transfers between devices, local(): lax.all_to_all(heat.reshape(devices, 1, HEAT_ROWS * LANES), both, 0, 0)  4.87 us
    ppermute x1, starting transfers between devices, local(): lax.ppermute(columns, 'gy', [(k, k + 1) for k in range(across - 1)])  4.55 us
    pallas_call x1, Pallas kernels, local(): pl.pallas_call(pack_kernel, out_shape=pltpu.VMEM((devices * REC1, LANES),...  4.29 us
    all_to_all x1, waiting for transfers between devices, local(): lax.all_to_all(heat.reshape(devices, 1, HEAT_ROWS * LANES), both, 0, 0)  3.88 us
  transfers between devices with their start and end apart: 7, of which 5 were waited for; matrix products, arithmetic and copies ran while one was open for 0% of the time, Pallas kernels for 15%

profile of v3, /device:TPU:0, one launch (start us, length us, event | category | flops | bytes accessed | tf_op | source)
XLA Modules:
  0.0 77.0 jit_solution(1411783283694234531)
XLA Ops:
  0.6 0.6 pad_add_fusion.refs_0_.pos
  1.2 4.3 %pack.1 = f32[512,128]{1,0:T(8,128)} custom-call(s32[2]{0:T(128)} %pad_add_fusion.refs_0_.pos, s32[2,64]{1,0:T(2,128)} %bitcast.15, f32[2,256,256]{2,1,0:T(8,128)} %refs_4_.1, s32[2,256,256]{2,1,0:T(8,128)} %refs_6_.1, f32[3,16,128,128]{3,2,1,0:T(8,128)} %air_hbm.3), custom_call_target="tpu_custom_call" | custom-call | tf_op jit(solution)/shard_map/pack/pallas_call | solution.py:720
  5.5 0.0 copy-start
  5.5 0.0 copy-start.1
  5.5 0.0 copy-start.2
  5.5 7.5 %all-to-all-start = ((f32[32,16,128]{2,1,0:T(8,128)}), f32[32,16,128]{2,1,0:T(8,128)S(1)}, u32[]{:S(2)}, u32[]{:S(2)}) async-start(f32[32,16,128]{2,1,0:T(8,128)} %bitcast.5), calls=%async_computation | async-start | bytes 524288 | tf_op jit(solution)/shard_map/all_to_all | solution.py:732
  13.0 1.5 %index.1.ready = s32[16,128]{1,0:T(8,128)} custom-call(s32[2]{0:T(128)} %pad_add_fusion.refs_0_.pos, s32[2,64]{1,0:T(2,128)} %bitcast.16, s32[4,64]{1,0:T(4,128)} %bitcast.18), custom_call_target="tpu_custom_call" | custom-call | flops 20000000 | bytes 10000 | tf_op jit(solution)/shard_map/index/pallas_call | solution.py:734
  14.5 3.3 %edge.1 = (f32[48,128]{1,0:T(8,128)S(1)}, f32[48,128]{1,0:T(8,128)S(1)}, f32[128,128]{1,0:T(8,128)S(1)}) custom-call(f32[6144,128]{1,0:T(8,128)} %bitcast.14, s32[16,128]{1,0:T(8,128)} %index.1.ready), custom_call_target="tpu_custom_call" | custom-call | flops 30000000 | bytes 3200000 | tf_op jit(solution)/shard_map/edge/pallas_call | solution.py:743
  17.8 2.2 %collective-permute-start = (f32[48,128]{1,0:T(8,128)S(1)}, f32[48,128]{1,0:T(8,128)S(1)}, u32[]{:S(2)}, u32[]{:S(2)}) collective-permute-start(f32[48,128]{1,0:T(8,128)S(1)} %get-tuple-element.15), channel_id=1, source_target_pairs={{0,8},{8,16},{16,24},{1,9},{9,17},{17,25},{2,10},{10,18},{18,26},{... | collective-permute-start | bytes 73736 | tf_op jit(solution)/shard_map/ppermute | solution.py:756
  20.0 1.3 %collective-permute-start.1 = (f32[48,128]{1,0:T(8,128)S(1)}, f32[48,128]{1,0:T(8,128)S(1)}, u32[]{:S(2)}, u32[]{:S(2)}) collective-permute-start(f32[48,128]{1,0:T(8,128)S(1)} %get-tuple-element.16), channel_id=1, source_target_pairs={{8,0},{16,8},{24,16},{9,1},{17,9},{25,17},{10,2},{18,10},{26,18},{... | collective-permute-start | bytes 73736 | tf_op jit(solution)/shard_map/ppermute | solution.py:757
  21.3 0.0 collective-permute-done.north
  21.3 2.9 %collective-permute-done.1.south = f32[48,128]{1,0:T(8,128)S(1)} collective-permute-done((f32[48,128]{1,0:T(8,128)S(1)}, f32[48,128]{1,0:T(8,128)S(1)}, u32[]{:S(2)}, u32[]{:S(2)}) %collective-permute-start.1) | collective-permute-done | bytes 24608 | tf_op jit(solution)/shard_map/ppermute | solution.py:757
  24.2 0.0 all-to-all-done
  24.2 2.6 %select.1 = f32[512,128]{1,0:T(8,128)} custom-call(s32[16,128]{1,0:T(8,128)} %index.1.ready, f32[512,128]{1,0:T(8,128)S(1)} %bitcast.13, f32[48,128]{1,0:T(8,128)S(1)} %collective-permute-done.north, f32[48,128]{1,0:T(8,128)S(1)} %collective-permute-done.1.south), custom_call_target="tpu_custom_call" | custom-call | tf_op jit(solution)/shard_map/select/pallas_call | solution.py:758
  26.9 6.8 %all-to-all-start.1 = ((f32[32,16,128]{2,1,0:T(8,128)}), f32[32,16,128]{2,1,0:T(8,128)S(1)}, u32[]{:S(2)}, u32[]{:S(2)}) async-start(f32[32,16,128]{2,1,0:T(8,128)} %bitcast.7), calls=%async_computation.1 | async-start | bytes 524288 | tf_op jit(solution)/shard_map/all_to_all | solution.py:768
  33.7 1.3 %collective-permute-start.3 = (f32[128,128]{1,0:T(8,128)S(1)}, f32[128,128]{1,0:T(8,128)S(1)}, u32[]{:S(2)}, u32[]{:S(2)}) collective-permute-start(f32[128,128]{1,0:T(8,128)S(1)} %get-tuple-element.18), channel_id=1, source_target_pairs={{1,0},{2,1},{3,2},{4,3},{5,4},{6,5},{7,6},{9,8},{10,9},{11,10},{12... | collective-permute-start | bytes 196616 | tf_op jit(solution)/shard_map/ppermute | solution.py:767
  35.0 4.5 %collective-permute-start.2 = (f32[128,128]{1,0:T(8,128)S(1)}, f32[128,128]{1,0:T(8,128)S(1)}, u32[]{:S(2)}, u32[]{:S(2)}) collective-permute-start(f32[128,128]{1,0:T(8,128)S(1)} %get-tuple-element.18), channel_id=1, source_target_pairs={{0,1},{1,2},{2,3},{3,4},{4,5},{5,6},{6,7},{8,9},{9,10},{10,11},{11... | collective-permute-start | bytes 196616 | tf_op jit(solution)/shard_map/ppermute | solution.py:766
  39.5 1.7 %collective-permute-done.3.refs_8_.east_side = f32[128,128]{1,0:T(8,128)S(1)} collective-permute-done((f32[128,128]{1,0:T(8,128)S(1)}, f32[128,128]{1,0:T(8,128)S(1)}, u32[]{:S(2)}, u32[]{:S(2)}) %collective-permute-start.3) | collective-permute-done | bytes 65568 | tf_op jit(solution)/shard_map/ppermute | solution.py:767
  41.2 1.2 %collective-permute-done.2.refs_7_.west_side = f32[128,128]{1,0:T(8,128)S(1)} collective-permute-done((f32[128,128]{1,0:T(8,128)S(1)}, f32[128,128]{1,0:T(8,128)S(1)}, u32[]{:S(2)}, u32[]{:S(2)}) %collective-permute-start.2) | collective-permute-done | bytes 65568 | tf_op jit(solution)/shard_map/ppermute | solution.py:766
  42.4 1.7 %all-to-all-done.1 = f32[32,16,128]{2,1,0:T(8,128)S(1)} async-done(((f32[32,16,128]{2,1,0:T(8,128)}), f32[32,16,128]{2,1,0:T(8,128)S(1)}, u32[]{:S(2)}, u32[]{:S(2)}) %all-to-all-start.1) | async-done | bytes 262176 | tf_op jit(solution)/shard_map/all_to_all | solution.py:768
  44.1 0.0 copy-done
  44.1 0.0 copy-done.1
  44.1 0.0 copy-done.2
  44.1 13.8 %fire.1 = (f32[2,256,256]{2,1,0:T(8,128)}, f32[2,256,256]{2,1,0:T(8,128)}, f32[544,128]{1,0:T(8,128)}) custom-call(s32[2]{0:T(128)} %pad_add_fusion.refs_0_.pos, s32[4,64]{1,0:T(4,128)} %bitcast.19, f32[5,13]{1,0:T(8,128)} %refs_2_.1, f32[512,128]{1,0:T(8,128)S(1)} %bitcast.12, f32[2,256,256]{2,1,0:T(8,128)S(1)} %copy-done, f32[2,256,256]{2,1,0:T(8,128)S(1)} %copy-done.2, ...), custom_call_target="tpu_custom_call" | custom-call | tf_op jit(solution)/shard_map/fire/pallas_call | solution.py:771
  57.9 4.9 %all-to-all-start.2 = ((f32[32,1,2176]{2,1,0:T(1,128)}), f32[32,1,2176]{2,1,0:T(1,128)S(1)}, u32[]{:S(2)}, u32[]{:S(2)}) async-start(f32[32,1,2176]{2,1,0:T(1,128)} %bitcast.9), calls=%async_computation.2 | async-start | bytes 557056 | tf_op jit(solution)/shard_map/all_to_all | solution.py:804
  62.8 7.0 %air.1.refs_3_ = f32[3,16,128,128]{3,2,1,0:T(8,128)} custom-call(f32[48,128]{1,0:T(8,128)S(1)} %collective-permute-done.north, f32[48,128]{1,0:T(8,128)S(1)} %collective-permute-done.1.south, f32[128,128]{1,0:T(8,128)S(1)} %collective-permute-done.2.refs_7_.west_side, f32[128,128]{1,0:T(8,128)S(1)} %collective-permute-done.3.refs_8_.east_side, ...), custom_call_target="tpu_custom_call" | custom-call | flops 80000000 | bytes 6300000 | tf_op jit(solution)/shard_map/air/pallas_call | solution.py:806
  69.8 3.9 %all-to-all-done.2 = f32[32,1,2176]{2,1,0:T(1,128)S(1)} async-done(((f32[32,1,2176]{2,1,0:T(1,128)}), f32[32,1,2176]{2,1,0:T(1,128)S(1)}, u32[]{:S(2)}, u32[]{:S(2)}) %all-to-all-start.2) | async-done | bytes 278560 | tf_op jit(solution)/shard_map/all_to_all | solution.py:804
  73.7 3.3 %heat.1 = (f32[3,16,128,128]{3,2,1,0:T(8,128)}, f32[2]{0:T(128)}) custom-call(s32[2]{0:T(128)} %pad_add_fusion.refs_0_.pos, s32[2,64]{1,0:T(2,128)} %bitcast.17, f32[544,128]{1,0:T(8,128)S(1)} %bitcast.11, f32[3,16,128,128]{3,2,1,0:T(8,128)} %air.1.refs_3_), custom_call_target="tpu_custom_call", output_to_operand_aliasing={{0}: (3, {})} | custom-call | tf_op jit(solution)/shard_map/heat/pallas_call | solution.py:822
Async XLA Ops:
  5.5 38.6 %copy-start = (f32[2,256,256]{2,1,0:T(8,128)S(1)}, f32[2,256,256]{2,1,0:T(8,128)}, u32[]{:S(2)}) copy-start(f32[2,256,256]{2,1,0:T(8,128)} %refs_4_.1) | copy-start | bytes 1572868
  5.5 38.6 %copy-start.1 = (s32[2,256,256]{2,1,0:T(8,128)S(1)}, s32[2,256,256]{2,1,0:T(8,128)}, u32[]{:S(2)}) copy-start(s32[2,256,256]{2,1,0:T(8,128)} %refs_6_.1) | copy-start | bytes 1572868
  5.5 38.6 %copy-start.2 = (f32[2,256,256]{2,1,0:T(8,128)S(1)}, f32[2,256,256]{2,1,0:T(8,128)}, u32[]{:S(2)}) copy-start(f32[2,256,256]{2,1,0:T(8,128)} %refs_5_.1) | copy-start | bytes 1572868
  5.5 18.7 %all-to-all-start = ((f32[32,16,128]{2,1,0:T(8,128)}), f32[32,16,128]{2,1,0:T(8,128)S(1)}, u32[]{:S(2)}, u32[]{:S(2)}) async-start(f32[32,16,128]{2,1,0:T(8,128)} %bitcast.5), calls=%async_computation | async-start | bytes 524288 | tf_op jit(solution)/shard_map/all_to_all | solution.py:732
  17.8 3.5 %collective-permute-start = (f32[48,128]{1,0:T(8,128)S(1)}, f32[48,128]{1,0:T(8,128)S(1)}, u32[]{:S(2)}, u32[]{:S(2)}) collective-permute-start(f32[48,128]{1,0:T(8,128)S(1)} %get-tuple-element.15), channel_id=1, source_target_pairs={{0,8},{8,16},{16,24},{1,9},{9,17},{17,25},{2,10},{10,18},{18,26},{... | collective-permute-start | bytes 73736 | tf_op jit(solution)/shard_map/ppermute | solution.py:756
  20.0 4.2 %collective-permute-start.1 = (f32[48,128]{1,0:T(8,128)S(1)}, f32[48,128]{1,0:T(8,128)S(1)}, u32[]{:S(2)}, u32[]{:S(2)}) collective-permute-start(f32[48,128]{1,0:T(8,128)S(1)} %get-tuple-element.16), channel_id=1, source_target_pairs={{8,0},{16,8},{24,16},{9,1},{17,9},{25,17},{10,2},{18,10},{26,18},{... | collective-permute-start | bytes 73736 | tf_op jit(solution)/shard_map/ppermute | solution.py:757
  26.9 17.2 %all-to-all-start.1 = ((f32[32,16,128]{2,1,0:T(8,128)}), f32[32,16,128]{2,1,0:T(8,128)S(1)}, u32[]{:S(2)}, u32[]{:S(2)}) async-start(f32[32,16,128]{2,1,0:T(8,128)} %bitcast.7), calls=%async_computation.1 | async-start | bytes 524288 | tf_op jit(solution)/shard_map/all_to_all | solution.py:768
  33.7 7.5 %collective-permute-start.3 = (f32[128,128]{1,0:T(8,128)S(1)}, f32[128,128]{1,0:T(8,128)S(1)}, u32[]{:S(2)}, u32[]{:S(2)}) collective-permute-start(f32[128,128]{1,0:T(8,128)S(1)} %get-tuple-element.18), channel_id=1, source_target_pairs={{1,0},{2,1},{3,2},{4,3},{5,4},{6,5},{7,6},{9,8},{10,9},{11,10},{12... | collective-permute-start | bytes 196616 | tf_op jit(solution)/shard_map/ppermute | solution.py:767
  35.0 7.4 %collective-permute-start.2 = (f32[128,128]{1,0:T(8,128)S(1)}, f32[128,128]{1,0:T(8,128)S(1)}, u32[]{:S(2)}, u32[]{:S(2)}) collective-permute-start(f32[128,128]{1,0:T(8,128)S(1)} %get-tuple-element.18), channel_id=1, source_target_pairs={{0,1},{1,2},{2,3},{3,4},{4,5},{5,6},{6,7},{8,9},{9,10},{10,11},{11... | collective-permute-start | bytes 196616 | tf_op jit(solution)/shard_map/ppermute | solution.py:766
  57.9 15.8 %all-to-all-start.2 = ((f32[32,1,2176]{2,1,0:T(1,128)}), f32[32,1,2176]{2,1,0:T(1,128)S(1)}, u32[]{:S(2)}, u32[]{:S(2)}) async-start(f32[32,1,2176]{2,1,0:T(1,128)} %bitcast.9), calls=%async_computation.2 | async-start | bytes 557056 | tf_op jit(solution)/shard_map/all_to_all | solution.py:804

commit v4 on v3

--- a/solution.py
+++ b/solution.py
@@ -61,9 +61,37 @@
     return jnp.take_along_axis(table, index, axis=1, mode="promise_in_bounds")
 
 
-def pack_kernel(pos, blocks, level, fuel_class, air_hbm, out, air, strip, sem):
-    load = pltpu.make_async_copy(air_hbm.at[0:2, 0], air, sem)
-    load.start()
+def position():
+    return lax.axis_index("gx"), lax.axis_index("gy")
+
+
+def pack_kernel(blocks, level_hbm, class_hbm, air_hbm, out, level, fuel_class, air, strip, mine, sem):
+    loads = [
+        pltpu.make_async_copy(level_hbm, level, sem.at[0]),
+        pltpu.make_async_copy(class_hbm, fuel_class, sem.at[1]),
+        pltpu.make_async_copy(air_hbm.at[0:2, 0], air, sem.at[2]),
+    ]
+    for load in loads:
+        load.start()
+    pos = position()
+    tile_rows = 128 // BA
+    for slot in range(4):
+        mine[slot] = -1
+
+    def find(j, count):
+        row = blocks[0, j] - pos[0] * tile_rows
+        col = blocks[1, j] - pos[1] * tile_rows
+        inside = (row >= 0) & (row < tile_rows) & (col >= 0) & (col < tile_rows)
+
+        @pl.when(inside)
+        def _():
+            mine[count] = row * tile_rows + col
+
+        return count + inside.astype(i32)
+
+    lax.fori_loop(0, blocks.shape[1], find, jnp.int32(0))
+    loads[0].wait()
+    loads[1].wait()
     lane256 = lanes((256, LANES))
     lane16 = lanes((16, LANES))
 
@@ -105,34 +133,16 @@
             )
             place(CORNER + q, 16 * number, jnp.where(lane16 < 64, half, rolled(half, 64)))
 
-    load.wait()
-    blank = jnp.zeros((PIECES, LANES), f32)
+    loads[2].wait()
+    lane32 = lanes((32, LANES))
     for slot in range(4):
-        place(WIND + slot, 0, blank)
-    lane32 = lanes((32, LANES))
-    tile_rows = 128 // BA
-
-    def find(j, count):
-        row = blocks[0, j] - pos[0] * tile_rows
-        col = blocks[1, j] - pos[1] * tile_rows
-        inside = (row >= 0) & (row < tile_rows) & (col >= 0) & (col < tile_rows)
-
-        @pl.when(inside)
-        def _():
-            start = pl.multiple_of(row * BA, BA)
-            u = air[0, pl.ds(start, BA), :]
-            v = air[1, pl.ds(start, BA), :]
-            shift = LANES - col * BA
-            u = pltpu.roll(u, shift, 1)
-            v = pltpu.roll(v, shift, 1)
-            half = jnp.where(lane32 < 32, u, rolled(v, 32))
-            both = jnp.where(lane32 < 64, half, rolled(half, 64))
-            out[pl.ds(WIND + count, PIECES, stride=REC1), :] = both
-
-        return count + inside.astype(i32)
-
-    lax.fori_loop(0, blocks.shape[1], find, jnp.int32(0))
-
+        at = jnp.maximum(mine[slot], 0)
+        start = pl.multiple_of((at // tile_rows) * BA, BA)
+        shift = LANES - (at % tile_rows) * BA
+        u = pltpu.roll(air[0, pl.ds(start, BA), :], shift, 1)
+        v = pltpu.roll(air[1, pl.ds(start, BA), :], shift, 1)
+        half = jnp.where(lane32 < 32, u, rolled(v, 32))
+        place(WIND + slot, 0, jnp.where(lane32 < 64, half, rolled(half, 64)))
     if out.shape[0] > PIECES * REC1:
         out[PIECES * REC1 :, :] = jnp.zeros((out.shape[0] - PIECES * REC1, LANES), f32)
 
@@ -161,7 +171,8 @@
     lax.fori_loop(0, 16 // EDGE_UNROLL, gather, 0)
 
 
-def index_kernel(across, pos, blocks, adjacency, out, padded):
+def index_kernel(across, blocks, adjacency, out, padded):
+    pos = position()
     total = blocks.shape[1]
     tiles = out.shape[1] // LANES
     relay = jnp.minimum(pos[0] * across + pos[1], PIECES - 1)
@@ -194,11 +205,19 @@
     as_rows = [jnp.broadcast_to(t[0:1, :].astype(f32), (LANES, LANES)) for t in tile_of]
     as_cols = [t.T for t in as_rows]
     wind_row = []
+    placed = [jnp.zeros((8, 1), f32)] * 4
+    own = (pos[0] * across + pos[1]).astype(f32)
+    lane = lanes()
     for u in range(tiles):
         slot = jnp.zeros((1, LANES), f32)
         for v in range(u + 1):
             same = (as_cols[v] == as_rows[u]) & (before + LANES * v < here + LANES * u)
             slot = slot + jnp.sum(jnp.where(same, 1.0, 0.0), axis=0, keepdims=True)
+        number = (lane + (LANES * u + 1)).astype(f32)
+        own_tile = (jnp.broadcast_to(as_rows[u][0:1, :], (8, LANES)) == own) & (number <= total)
+        for c in range(4):
+            at_slot = own_tile & (jnp.broadcast_to(slot, (8, LANES)) == c)
+            placed[c] = placed[c] + jnp.sum(jnp.where(at_slot, number, 0.0), axis=1, keepdims=True)
         wind_row.append(tile_of[u] * REC1 + WIND + jnp.broadcast_to(slot.astype(i32), (8, LANES)))
     near = [row(8 + s) for s in range(4)]
     safe = [each(lambda n: jnp.maximum(n, 0), near[s]) for s in range(4)]
@@ -245,7 +264,12 @@
     for number, word in enumerate(words):
         for u in range(tiles):
             out[number : number + 1, LANES * u : LANES * (u + 1)] = word[u][0:1, :]
-    out[WORDS : WORDS + 1, :] = jnp.zeros((1, out.shape[1]), i32)
+    listed = jnp.zeros((8, LANES), f32)
+    for c in range(4):
+        listed = jnp.where(lane == c, placed[c], listed)
+    out[WORDS : WORDS + 1, 0:LANES] = listed[0:1, :].astype(i32)
+    if tiles > 1:
+        out[WORDS : WORDS + 1, LANES:] = jnp.zeros((1, out.shape[1] - LANES), i32)
 
 
 def select_kernel(index, received, north, south, out):
@@ -291,7 +315,6 @@
 def fire_kernel(
     across,
     down,
-    pos,
     adjacency,
     props,
     received,
@@ -300,9 +323,11 @@
     fuel_class,
     west_side,
     east_side,
+    level_hbm,
+    fuel_hbm,
+    heat_out,
     level_out,
     fuel_out,
-    heat_out,
     cur_a,
     cur_b,
     base_rate,
@@ -313,8 +338,10 @@
     tanh_sum,
     links,
     row_heat,
+    sem,
 ):
     cur = (cur_a, cur_b)
+    pos = position()
     lane = lanes()
     sub = lax.broadcasted_iota(i32, (8, LANES), 0)
     lane32 = lanes((32, LANES))
@@ -515,8 +542,11 @@
     within = make_masks(1)
     below = make_masks(2)
 
+    def outer(source, target):
+        update(source, target, 1, above, None, False)
+        update(source, target, 36, below, None, False)
+
     def substep(source, target):
-        update(source, target, 1, above, None, False)
         update(source, target, 2, above, ("down", 0, 7), False)
         update(source, target, 3, within, ("up", 0, 0), True)
 
@@ -528,13 +558,13 @@
         lax.fori_loop(0, 30 // UNROLL, middle, 0)
         update(source, target, 34, within, ("down", 1, 7), True)
         update(source, target, 35, below, ("up", 1, 0), False)
-        update(source, target, 36, below, None, False)
 
     def two_substeps(pair, carry):
         substep(cur_a, cur_b)
         substep(cur_b, cur_a)
         return carry
 
+    outer(cur_a, cur_b)
     lax.fori_loop(0, SUB // 2, two_substeps, 0)
 
     last = SUB % 2
@@ -562,6 +592,13 @@
     blank = jnp.zeros((8, LANES), f32)
     sums = [blank] * 4
 
+    def stores(group):
+        rows = pl.ds(group * (8 * FINISH_UNROLL), 8 * FINISH_UNROLL)
+        return [
+            pltpu.make_async_copy(level_out.at[:, rows, :], level_hbm.at[:, rows, :], sem.at[0, group]),
+            pltpu.make_async_copy(fuel_out.at[:, rows, :], fuel_hbm.at[:, rows, :], sem.at[1, group]),
+        ]
+
     def finish_group(group, totals):
         totals = list(totals)
         for k in range(FINISH_UNROLL):
@@ -569,6 +606,8 @@
             totals[pair], totals[pair + 1] = finish(
                 group * FINISH_UNROLL + k, totals[pair], totals[pair + 1]
             )
+        for copy in stores(group):
+            copy.start()
         return tuple(totals)
 
     sums = lax.fori_loop(0, 32 // FINISH_UNROLL, finish_group, tuple(sums))
@@ -600,9 +639,12 @@
     emit_sum = jnp.sum(jnp.sum(emit, axis=0, keepdims=True), axis=1, keepdims=True)
     lane1 = lanes((1, LANES))
     spread(16, jnp.where(lane1 == 0, burn_sum, jnp.where(lane1 == 1, emit_sum, 0.0)))
-
-
-def air_kernel(north, south, west_side, east_side, air_hbm, air_out, air, fresh, sides, sem_in, sem_out):
+    for group in range(32 // FINISH_UNROLL):
+        for copy in stores(group):
+            copy.wait()
+
+
+def air_kernel(north, south, west_side, east_side, air_hbm, air_out, surface, air, fresh, sides, sem_in, sem_out):
     def load(number):
         return pltpu.make_async_copy(
             air_hbm.at[:, number], air.at[:, number + 1, 8:136, :], sem_in.at[number]
@@ -664,6 +706,8 @@
 
     lax.fori_loop(0, levels, air_level, 0)
 
+    surface[...] = fresh[2, 0]
+
     def drain(number, carry):
         store(number).wait()
         return carry
@@ -671,38 +715,31 @@
     lax.fori_loop(0, levels, drain, 0)
 
 
-def heat_kernel(cells, pos, blocks, gathered, air_in, air_out, totals, plane, sem):
-    load = pltpu.make_async_copy(air_in.at[2, 0], plane, sem)
-    load.start()
-    devices = gathered.shape[0] // HEAT_ROWS
-    sums = jnp.sum(
-        gathered[pl.ds(16, devices, stride=HEAT_ROWS), :], axis=0, keepdims=True
-    )
-    lane1 = lanes((1, LANES))
-    for k in range(2):
-        totals[k] = jnp.sum(jnp.where(lane1 == k, sums, 0.0)) * (1.0 / cells)
-    load.wait()
+def heat_kernel(cells, blocks, index, gathered, plane, air_in, air_out, totals, warm, sem):
+    pos = position()
+    tile_rows = 128 // BA
     lane = lanes()
-    tile_rows = 128 // BA
-
-    def place(j, carry):
-        row = blocks[0, j] - pos[0] * tile_rows
-        col = blocks[1, j] - pos[1] * tile_rows
-        inside = (row >= 0) & (row < tile_rows) & (col >= 0) & (col < tile_rows)
-
-        @pl.when(inside)
+    warm[...] = plane[...]
+    for slot in range(4):
+        j = index[WORDS, slot] - 1
+
+        @pl.when(j >= 0)
         def _():
+            row = blocks[0, j] - pos[0] * tile_rows
+            col = blocks[1, j] - pos[1] * tile_rows
             heat = gathered[pl.ds((j // 2) * HEAT_ROWS + 8 * (j % 2), 8), :]
             for g in range(4):
                 moved = pltpu.roll(heat, (col - g + 4) * BA % LANES, 1)
                 at = pl.multiple_of(row * BA + 8 * g, 8)
-                plane[pl.ds(at, 8), :] += jnp.where(lane // BA == col, moved, 0.0)
-
-        return carry
-
-    lax.fori_loop(0, blocks.shape[1], place, 0)
-    store = pltpu.make_async_copy(plane, air_out.at[2, 0], sem)
+                warm[pl.ds(at, 8), :] += jnp.where(lane // BA == col, moved, 0.0)
+
+    store = pltpu.make_async_copy(warm, air_out.at[2, 0], sem)
     store.start()
+    devices = gathered.shape[0] // HEAT_ROWS
+    sums = jnp.sum(gathered[pl.ds(16, devices, stride=HEAT_ROWS), :], axis=0, keepdims=True)
+    lane1 = lanes((1, LANES))
+    for k in range(2):
+        totals[k] = jnp.sum(jnp.where(lane1 == k, sums, 0.0)) * (1.0 / cells)
     store.wait()
 
 
@@ -711,7 +748,6 @@
     across = lax.axis_size("gy")
     devices = down * across
     both = ("gx", "gy")
-    pos = jnp.stack([lax.axis_index("gx"), lax.axis_index("gy")]).astype(i32)
     smem = pl.BlockSpec(memory_space=pltpu.SMEM)
     vmem = pl.BlockSpec(memory_space=pltpu.VMEM)
     anywhere = pl.BlockSpec(memory_space=pl.ANY)
@@ -720,26 +756,29 @@
     packed = pl.pallas_call(
         pack_kernel,
         out_shape=pltpu.VMEM((devices * REC1, LANES), f32),
-        in_specs=[smem, smem, vmem, vmem, anywhere],
+        in_specs=[smem, anywhere, anywhere, anywhere],
         out_specs=vmem,
         scratch_shapes=[
+            pltpu.VMEM(level_set.shape, f32),
+            pltpu.VMEM(level_set.shape, i32),
             pltpu.VMEM((2, 128, LANES), f32),
             pltpu.VMEM((4, 40, LANES), f32),
-            pltpu.SemaphoreType.DMA(()),
+            pltpu.SMEM((8,), i32),
+            pltpu.SemaphoreType.DMA((3,)),
         ],
         name="pack",
-    )(pos, blocks, level_set, fuel_class, air_state)
+    )(blocks, level_set, fuel_class, air_state)
     relayed = lax.all_to_all(packed.reshape(devices, REC1, LANES), both, 0, 0)
     lanes_used = -(-blocks.shape[1] // LANES) * LANES
     index = pl.pallas_call(
         lambda *refs: index_kernel(across, *refs),
         out_shape=jax.ShapeDtypeStruct((WORDS + 1, lanes_used), i32),
-        in_specs=[smem, vmem, vmem],
+        in_specs=[vmem, vmem],
         out_specs=vmem,
         scratch_shapes=[pltpu.VMEM((16, lanes_used), i32)],
         cost_estimate=pl.CostEstimate(flops=20_000_000, transcendentals=0, bytes_accessed=10_000),
         name="index",
-    )(pos, blocks, adjacency)
+    )(blocks, adjacency)
     first_rows, last_rows, columns = pl.pallas_call(
         edge_kernel,
         out_shape=(
@@ -775,9 +814,11 @@
             jax.ShapeDtypeStruct(level_set.shape, f32),
             pltpu.VMEM((devices * HEAT_ROWS, LANES), f32),
         ),
-        in_specs=[smem, smem, smem, vmem, vmem, vmem, vmem] + [vmem] * 2,
-        out_specs=(vmem, vmem, vmem),
+        in_specs=[smem, smem, vmem, vmem, vmem, vmem] + [vmem] * 2,
+        out_specs=(anywhere, anywhere, vmem),
         scratch_shapes=[
+            pltpu.VMEM(level_set.shape, f32),
+            pltpu.VMEM(level_set.shape, f32),
             pltpu.VMEM((5, EXT, LANES), f32),
             pltpu.VMEM((5, EXT, LANES), f32),
             pltpu.VMEM((5, EXT, LANES), f32),
@@ -788,10 +829,10 @@
             pltpu.VMEM((4, 256, LANES), f32),
             pltpu.VMEM((2, 5, 8, LANES), i32),
             pltpu.VMEM((4, 32, LANES), f32),
+            pltpu.SemaphoreType.DMA((2, 32 // FINISH_UNROLL)),
         ],
         name="fire",
     )(
-        pos,
         adjacency,
         fuel_props,
         received,
@@ -803,11 +844,11 @@
     )
     gathered = lax.all_to_all(heat.reshape(devices, 1, HEAT_ROWS * LANES), both, 0, 0)
     gathered = near(gathered.reshape(devices * HEAT_ROWS, LANES))
-    air_next = pl.pallas_call(
+    air_next, plane = pl.pallas_call(
         air_kernel,
-        out_shape=jax.ShapeDtypeStruct(air_state.shape, f32),
+        out_shape=(jax.ShapeDtypeStruct(air_state.shape, f32), pltpu.VMEM((128, LANES), f32)),
         in_specs=[vmem, vmem, vmem, vmem, anywhere],
-        out_specs=anywhere,
+        out_specs=(anywhere, vmem),
         scratch_shapes=[
             pltpu.VMEM((3, 18, 144, LANES), f32),
             pltpu.VMEM((3, 16, 128, LANES), f32),
@@ -822,12 +863,12 @@
     air_next, totals = pl.pallas_call(
         lambda *refs: heat_kernel(cells, *refs),
         out_shape=(jax.ShapeDtypeStruct(air_state.shape, f32), jax.ShapeDtypeStruct((2,), f32)),
-        in_specs=[smem, smem, vmem, anywhere],
+        in_specs=[smem, smem, vmem, vmem, anywhere],
         out_specs=(anywhere, smem),
         scratch_shapes=[pltpu.VMEM((128, LANES), f32), pltpu.SemaphoreType.DMA(())],
-        input_output_aliases={3: 0},
+        input_output_aliases={4: 0},
         name="heat",
-    )(pos, blocks, gathered, air_next)
+    )(blocks, index, gathered, plane, air_next)
     return (air_next, level_next, fuel_next, totals)
 
 

time: 77.8 us -> 74.3 us (0.955)
  Pallas kernels: 35.9 us -> 33.2 us
    pallas_call x1, Pallas kernels: 3.32 us -> 2.1 us  [local(): pl.pallas_call(lambda *refs: heat_kernel(cells, *refs), out_shape=(jax.Sh...]
    pallas_call x1, Pallas kernels: 4.29 us -> 3.2 us  [local(): pl.pallas_call(pack_kernel, out_shape=pltpu.VMEM((devices * REC1, LANES),...]
  transfers between devices with their start and end apart: 7 -> 7, of which waited for: 5 -> 5; matrix products, arithmetic and copies ran while one was open for 0% -> 0% of each run, Pallas kernels for 15% -> 16%
where the time goes in v4:
time: 74.3 us; the launch traced here: 73.7 us
  Pallas kernels  33.2 us (45%)
  starting transfers between devices  28.3 us (38%)
  waiting for transfers between devices  10.8 us (15%)
  between operations  0.77 us (1%)
    pallas_call x1, Pallas kernels, local(): pl.pallas_call(lambda *refs: fire_kernel(across, down, *refs), out_shape=...  13.5 us
    all_to_all x1, starting transfers between devices, local(): relayed = lax.all_to_all(packed.reshape(devices, REC1, LANES), both, 0, 0)  7.33 us
    pallas_call x1, Pallas kernels, local(): pl.pallas_call(air_kernel, out_shape=(jax.ShapeDtypeStruct(air_state.shap...  6.99 us
    all_to_all x1, starting transfers between devices, local(): received = lax.all_to_all(chosen.reshape(devices, REC2, LANES), both, 0, 0)  6.79 us
    all_to_all x1, starting transfers between devices, local(): lax.all_to_all(heat.reshape(devices, 1, HEAT_ROWS * LANES), both, 0, 0)  4.88 us
    ppermute x1, starting transfers between devices, local(): lax.ppermute(columns, 'gy', [(k, k + 1) for k in range(across - 1)])  4.55 us
    pallas_call x1, Pallas kernels, local(): pl.pallas_call(edge_kernel, out_shape=(pltpu.VMEM((48, LANES), f32), pltp...  3.29 us
    all_to_all x1, waiting for transfers between devices, local(): lax.all_to_all(heat.reshape(devices, 1, HEAT_ROWS * LANES), both, 0, 0)  3.25 us
  transfers between devices with their start and end apart: 7, of which 5 were waited for; matrix products, arithmetic and copies ran while one was open for 0% of the time, Pallas kernels for 16%

profile of v4, /device:TPU:0, one launch (start us, length us, event | category | flops | bytes accessed | tf_op | source)
XLA Modules:
  0.0 73.7 jit_solution(6715268205325716532)
XLA Ops:
  0.6 3.2 %pack.1 = f32[512,128]{1,0:T(8,128)} custom-call(s32[2,64]{1,0:T(2,128)} %bitcast.13, f32[2,256,256]{2,1,0:T(8,128)} %refs_3_.1, s32[2,256,256]{2,1,0:T(8,128)} %refs_5_.1, f32[3,16,128,128]{3,2,1,0:T(8,128)} %air_hbm.3), custom_call_target="tpu_custom_call" | custom-call | tf_op jit(solution)/shard_map/pack/pallas_call | solution.py:756
  3.8 0.0 copy-start
  3.8 0.0 copy-start.1
  3.9 0.0 copy-start.2
  3.9 7.3 %all-to-all-start = ((f32[32,16,128]{2,1,0:T(8,128)}), f32[32,16,128]{2,1,0:T(8,128)S(1)}, u32[]{:S(2)}, u32[]{:S(2)}) async-start(f32[32,16,128]{2,1,0:T(8,128)} %bitcast.3), calls=%async_computation | async-start | bytes 524288 | tf_op jit(solution)/shard_map/all_to_all | solution.py:771
  11.2 1.5 %index.1.ready.refs_1_ = s32[16,128]{1,0:T(8,128)} custom-call(s32[2,64]{1,0:T(2,128)} %bitcast.14, s32[4,64]{1,0:T(4,128)} %bitcast.16), custom_call_target="tpu_custom_call" | custom-call | flops 20000000 | bytes 10000 | tf_op jit(solution)/shard_map/index/pallas_call | solution.py:773
  12.7 3.3 %edge.1 = (f32[48,128]{1,0:T(8,128)S(1)}, f32[48,128]{1,0:T(8,128)S(1)}, f32[128,128]{1,0:T(8,128)S(1)}) custom-call(f32[6144,128]{1,0:T(8,128)} %bitcast.12, s32[16,128]{1,0:T(8,128)} %index.1.ready.refs_1_), custom_call_target="tpu_custom_call" | custom-call | flops 30000000 | bytes 3200000 | tf_op jit(solution)/shard_map/edge/pallas_call | solution.py:782
  16.0 2.2 %collective-permute-start = (f32[48,128]{1,0:T(8,128)S(1)}, f32[48,128]{1,0:T(8,128)S(1)}, u32[]{:S(2)}, u32[]{:S(2)}) collective-permute-start(f32[48,128]{1,0:T(8,128)S(1)} %get-tuple-element.17), channel_id=1, source_target_pairs={{0,8},{8,16},{16,24},{1,9},{9,17},{17,25},{2,10},{10,18},{18,26},{... | collective-permute-start | bytes 73736 | tf_op jit(solution)/shard_map/ppermute | solution.py:795
  18.2 1.3 %collective-permute-start.1 = (f32[48,128]{1,0:T(8,128)S(1)}, f32[48,128]{1,0:T(8,128)S(1)}, u32[]{:S(2)}, u32[]{:S(2)}) collective-permute-start(f32[48,128]{1,0:T(8,128)S(1)} %get-tuple-element.18), channel_id=1, source_target_pairs={{8,0},{16,8},{24,16},{9,1},{17,9},{25,17},{10,2},{18,10},{26,18},{... | collective-permute-start | bytes 73736 | tf_op jit(solution)/shard_map/ppermute | solution.py:796
  19.5 0.0 collective-permute-done.north
  19.5 2.9 %collective-permute-done.1.south = f32[48,128]{1,0:T(8,128)S(1)} collective-permute-done((f32[48,128]{1,0:T(8,128)S(1)}, f32[48,128]{1,0:T(8,128)S(1)}, u32[]{:S(2)}, u32[]{:S(2)}) %collective-permute-start.1) | collective-permute-done | bytes 24608 | tf_op jit(solution)/shard_map/ppermute | solution.py:796
  22.4 0.0 all-to-all-done
  22.4 2.6 %select.1 = f32[512,128]{1,0:T(8,128)} custom-call(s32[16,128]{1,0:T(8,128)} %index.1.ready.refs_1_, f32[512,128]{1,0:T(8,128)S(1)} %bitcast.11, f32[48,128]{1,0:T(8,128)S(1)} %collective-permute-done.north, f32[48,128]{1,0:T(8,128)S(1)} %collective-permute-done.1.south), custom_call_target="tpu_custom_call" | custom-call | tf_op jit(solution)/shard_map/select/pallas_call | solution.py:797
  25.0 6.8 %all-to-all-start.1 = ((f32[32,16,128]{2,1,0:T(8,128)}), f32[32,16,128]{2,1,0:T(8,128)S(1)}, u32[]{:S(2)}, u32[]{:S(2)}) async-start(f32[32,16,128]{2,1,0:T(8,128)} %bitcast.5), calls=%async_computation.1 | async-start | bytes 524288 | tf_op jit(solution)/shard_map/all_to_all | solution.py:807
  31.8 1.3 %collective-permute-start.3 = (f32[128,128]{1,0:T(8,128)S(1)}, f32[128,128]{1,0:T(8,128)S(1)}, u32[]{:S(2)}, u32[]{:S(2)}) collective-permute-start(f32[128,128]{1,0:T(8,128)S(1)} %get-tuple-element.20), channel_id=1, source_target_pairs={{1,0},{2,1},{3,2},{4,3},{5,4},{6,5},{7,6},{9,8},{10,9},{11,10},{12... | collective-permute-start | bytes 196616 | tf_op jit(solution)/shard_map/ppermute | solution.py:806
  33.1 4.5 %collective-permute-start.2 = (f32[128,128]{1,0:T(8,128)S(1)}, f32[128,128]{1,0:T(8,128)S(1)}, u32[]{:S(2)}, u32[]{:S(2)}) collective-permute-start(f32[128,128]{1,0:T(8,128)S(1)} %get-tuple-element.20), channel_id=1, source_target_pairs={{0,1},{1,2},{2,3},{3,4},{4,5},{5,6},{6,7},{8,9},{9,10},{10,11},{11... | collective-permute-start | bytes 196616 | tf_op jit(solution)/shard_map/ppermute | solution.py:805
  37.7 1.7 %collective-permute-done.3.refs_7_.east_side = f32[128,128]{1,0:T(8,128)S(1)} collective-permute-done((f32[128,128]{1,0:T(8,128)S(1)}, f32[128,128]{1,0:T(8,128)S(1)}, u32[]{:S(2)}, u32[]{:S(2)}) %collective-permute-start.3) | collective-permute-done | bytes 65568 | tf_op jit(solution)/shard_map/ppermute | solution.py:806
  39.4 1.2 %collective-permute-done.2.refs_6_.west_side = f32[128,128]{1,0:T(8,128)S(1)} collective-permute-done((f32[128,128]{1,0:T(8,128)S(1)}, f32[128,128]{1,0:T(8,128)S(1)}, u32[]{:S(2)}, u32[]{:S(2)}) %collective-permute-start.2) | collective-permute-done | bytes 65568 | tf_op jit(solution)/shard_map/ppermute | solution.py:805
  40.5 1.7 %all-to-all-done.1 = f32[32,16,128]{2,1,0:T(8,128)S(1)} async-done(((f32[32,16,128]{2,1,0:T(8,128)}), f32[32,16,128]{2,1,0:T(8,128)S(1)}, u32[]{:S(2)}, u32[]{:S(2)}) %all-to-all-start.1) | async-done | bytes 262176 | tf_op jit(solution)/shard_map/all_to_all | solution.py:807
  42.3 0.0 copy-done
  42.3 0.0 copy-done.1
  42.3 0.0 copy-done.2
  42.3 13.5 %fire.1 = (f32[2,256,256]{2,1,0:T(8,128)}, f32[2,256,256]{2,1,0:T(8,128)}, f32[544,128]{1,0:T(8,128)}) custom-call(s32[4,64]{1,0:T(4,128)} %bitcast.17, f32[5,13]{1,0:T(8,128)} %refs_1_.1, f32[512,128]{1,0:T(8,128)S(1)} %bitcast.10, f32[2,256,256]{2,1,0:T(8,128)S(1)} %copy-done, f32[2,256,256]{2,1,0:T(8,128)S(1)} %copy-done.2, s32[2,256,256]{2,1,0:T(8,128)S(1)} %copy-done.1, ...), custom_call_target="tpu_custom_call" | custom-call | tf_op jit(solution)/shard_map/fire/pallas_call | solution.py:810
  55.8 4.9 %all-to-all-start.2 = ((f32[32,1,2176]{2,1,0:T(1,128)}), f32[32,1,2176]{2,1,0:T(1,128)S(1)}, u32[]{:S(2)}, u32[]{:S(2)}) async-start(f32[32,1,2176]{2,1,0:T(1,128)} %bitcast.7), calls=%async_computation.2 | async-start | bytes 557056 | tf_op jit(solution)/shard_map/all_to_all | solution.py:845
  60.7 7.0 %air.1 = (f32[3,16,128,128]{3,2,1,0:T(8,128)}, f32[128,128]{1,0:T(8,128)S(1)}) custom-call(f32[48,128]{1,0:T(8,128)S(1)} %collective-permute-done.north, f32[48,128]{1,0:T(8,128)S(1)} %collective-permute-done.1.south, f32[128,128]{1,0:T(8,128)S(1)} %collective-permute-done.2.refs_6_.west_side, f32[128,128]{1,0:T(8,128)S(1)} %collective-permute-done.3.refs_7_.east_side, ...), custom_call_target="tpu_custom_call" | custom-call | flops 80000000 | bytes 6300000 | tf_op jit(solution)/shard_map/air/pallas_call | solution.py:847
  67.7 0.0 copy-start.3
  67.7 0.6 copy-done.3
  68.3 3.3 %all-to-all-done.2 = f32[32,1,2176]{2,1,0:T(1,128)S(1)} async-done(((f32[32,1,2176]{2,1,0:T(1,128)}), f32[32,1,2176]{2,1,0:T(1,128)S(1)}, u32[]{:S(2)}, u32[]{:S(2)}) %all-to-all-start.2) | async-done | bytes 278560 | tf_op jit(solution)/shard_map/all_to_all | solution.py:845
  71.6 2.1 %heat.1 = (f32[3,16,128,128]{3,2,1,0:T(8,128)}, f32[2]{0:T(128)}) custom-call(s32[2,64]{1,0:T(2,128)} %bitcast.15, s32[16,128]{1,0:T(8,128)} %index.1.ready.refs_1_, f32[544,128]{1,0:T(8,128)S(1)} %bitcast.9, f32[128,128]{1,0:T(8,128)} %copy-done.3, f32[3,16,128,128]{3,2,1,0:T(8,128)} %get-tuple-element.23.refs_4_), custom_call_target="tpu_custom_call", output_to_operand_aliasing={{0}: (4, {})} | custom-call | tf_op jit(solution)/shard_map/heat/pallas_call | solution.py:863
Async XLA Ops:
  3.8 38.5 %copy-start = (f32[2,256,256]{2,1,0:T(8,128)S(1)}, f32[2,256,256]{2,1,0:T(8,128)}, u32[]{:S(2)}) copy-start(f32[2,256,256]{2,1,0:T(8,128)} %refs_3_.1) | copy-start | bytes 1572868
  3.8 38.4 %copy-start.1 = (s32[2,256,256]{2,1,0:T(8,128)S(1)}, s32[2,256,256]{2,1,0:T(8,128)}, u32[]{:S(2)}) copy-start(s32[2,256,256]{2,1,0:T(8,128)} %refs_5_.1) | copy-start | bytes 1572868
  3.9 38.4 %copy-start.2 = (f32[2,256,256]{2,1,0:T(8,128)S(1)}, f32[2,256,256]{2,1,0:T(8,128)}, u32[]{:S(2)}) copy-start(f32[2,256,256]{2,1,0:T(8,128)} %refs_4_.1) | copy-start | bytes 1572868
  3.9 18.5 %all-to-all-start = ((f32[32,16,128]{2,1,0:T(8,128)}), f32[32,16,128]{2,1,0:T(8,128)S(1)}, u32[]{:S(2)}, u32[]{:S(2)}) async-start(f32[32,16,128]{2,1,0:T(8,128)} %bitcast.3), calls=%async_computation | async-start | bytes 524288 | tf_op jit(solution)/shard_map/all_to_all | solution.py:771
  16.0 3.5 %collective-permute-start = (f32[48,128]{1,0:T(8,128)S(1)}, f32[48,128]{1,0:T(8,128)S(1)}, u32[]{:S(2)}, u32[]{:S(2)}) collective-permute-start(f32[48,128]{1,0:T(8,128)S(1)} %get-tuple-element.17), channel_id=1, source_target_pairs={{0,8},{8,16},{16,24},{1,9},{9,17},{17,25},{2,10},{10,18},{18,26},{... | collective-permute-start | bytes 73736 | tf_op jit(solution)/shard_map/ppermute | solution.py:795
  18.2 4.2 %collective-permute-start.1 = (f32[48,128]{1,0:T(8,128)S(1)}, f32[48,128]{1,0:T(8,128)S(1)}, u32[]{:S(2)}, u32[]{:S(2)}) collective-permute-start(f32[48,128]{1,0:T(8,128)S(1)} %get-tuple-element.18), channel_id=1, source_target_pairs={{8,0},{16,8},{24,16},{9,1},{17,9},{25,17},{10,2},{18,10},{26,18},{... | collective-permute-start | bytes 73736 | tf_op jit(solution)/shard_map/ppermute | solution.py:796
  25.0 17.2 %all-to-all-start.1 = ((f32[32,16,128]{2,1,0:T(8,128)}), f32[32,16,128]{2,1,0:T(8,128)S(1)}, u32[]{:S(2)}, u32[]{:S(2)}) async-start(f32[32,16,128]{2,1,0:T(8,128)} %bitcast.5), calls=%async_computation.1 | async-start | bytes 524288 | tf_op jit(solution)/shard_map/all_to_all | solution.py:807
  31.8 7.5 %collective-permute-start.3 = (f32[128,128]{1,0:T(8,128)S(1)}, f32[128,128]{1,0:T(8,128)S(1)}, u32[]{:S(2)}, u32[]{:S(2)}) collective-permute-start(f32[128,128]{1,0:T(8,128)S(1)} %get-tuple-element.20), channel_id=1, source_target_pairs={{1,0},{2,1},{3,2},{4,3},{5,4},{6,5},{7,6},{9,8},{10,9},{11,10},{12... | collective-permute-start | bytes 196616 | tf_op jit(solution)/shard_map/ppermute | solution.py:806
  33.1 7.4 %collective-permute-start.2 = (f32[128,128]{1,0:T(8,128)S(1)}, f32[128,128]{1,0:T(8,128)S(1)}, u32[]{:S(2)}, u32[]{:S(2)}) collective-permute-start(f32[128,128]{1,0:T(8,128)S(1)} %get-tuple-element.20), channel_id=1, source_target_pairs={{0,1},{1,2},{2,3},{3,4},{4,5},{5,6},{6,7},{8,9},{9,10},{10,11},{11... | collective-permute-start | bytes 196616 | tf_op jit(solution)/shard_map/ppermute | solution.py:805
  55.8 15.8 %all-to-all-start.2 = ((f32[32,1,2176]{2,1,0:T(1,128)}), f32[32,1,2176]{2,1,0:T(1,128)S(1)}, u32[]{:S(2)}, u32[]{:S(2)}) async-start(f32[32,1,2176]{2,1,0:T(1,128)} %bitcast.7), calls=%async_computation.2 | async-start | bytes 557056 | tf_op jit(solution)/shard_map/all_to_all | solution.py:845
  67.7 0.6 copy-start.3

commit v5 on v4

--- a/solution.py
+++ b/solution.py
@@ -171,7 +171,7 @@
     lax.fori_loop(0, 16 // EDGE_UNROLL, gather, 0)
 
 
-def index_kernel(across, blocks, adjacency, out, padded):
+def index_kernel(across, blocks, adjacency, near_own, props, out, tables, flags, padded):
     pos = position()
     total = blocks.shape[1]
     tiles = out.shape[1] // LANES
@@ -264,6 +264,62 @@
     for number, word in enumerate(words):
         for u in range(tiles):
             out[number : number + 1, LANES * u : LANES * (u + 1)] = word[u][0:1, :]
+    device = pos[0] * across + pos[1]
+
+    def table(value):
+        row = jnp.zeros((8, LANES), f32)
+        for kind in range(props.shape[1]):
+            row = jnp.where(lane == kind, value(kind), row)
+        return row
+
+    log2e = math.log2(math.e)
+    table_base = table(lambda c: 0.125 * 0.3 * props[0, c])
+    table_wind = table_base * table(lambda c: 0.3 * props[1, c])
+    table_burn = (-0.5 * step_time * log2e / 4.0) / jnp.where(
+        lane < props.shape[1], table(lambda c: props[2, c]), 1.0
+    )
+    table_heat = table(lambda c: props[3, c])
+    table_emit = table(lambda c: 3.0 * props[4, c])
+    for k, values in enumerate((table_base, table_wind, table_burn, table_heat, table_emit)):
+        tables[k] = values
+
+    def there(j):
+        return j >= 0
+
+    across_links = []
+    groups = []
+    for q in range(2):
+        i = 2 * device + q
+        near = [near_own[s, i] for s in range(4)]
+        safe = [jnp.maximum(near[s], 0) for s in range(4)]
+
+        def joined(s, t):
+            return there(near[s]) & there(near_own[t, safe[s]])
+
+        groups.append([(there(near[s]), joined(2, s), joined(3, s)) for s in range(2)])
+        across_links.append([[joined(0, t), there(near[t]), joined(1, t)] for t in (2, 3)])
+
+    def as_int(flag):
+        return jnp.where(flag, 1, 0)
+
+    for line in range(2):
+        for q in range(2):
+            mid, west, east = groups[q][line]
+            row = jnp.broadcast_to(as_int(mid), (8, LANES))
+            flags[12 + 5 * line + 3 * q] = row
+            flags[12 + 5 * line + 3 * q + 1] = row
+        w0, e0 = groups[0][line][1:]
+        w1, e1 = groups[1][line][1:]
+        flags[12 + 5 * line + 2] = jnp.where(
+            lane < 32,
+            as_int(e0),
+            jnp.where(lane < 64, as_int(w0), jnp.where(lane < 96, as_int(e1), as_int(w1))),
+        )
+
+    for region in range(3):
+        for k in range(4):
+            flag = as_int(across_links[k // 2][k % 2][region])
+            flags[4 * region + k] = jnp.broadcast_to(flag, (8, LANES))
     listed = jnp.zeros((8, LANES), f32)
     for c in range(4):
         listed = jnp.where(lane == c, placed[c], listed)
@@ -272,7 +328,7 @@
         out[WORDS : WORDS + 1, LANES:] = jnp.zeros((1, out.shape[1] - LANES), i32)
 
 
-def select_kernel(index, received, north, south, out):
+def select_kernel(index, received, out):
     lane1 = lanes((1, LANES))
     lane_col = lane1 % 32 < 16
     first_half = lane1 < 64
@@ -315,14 +371,16 @@
 def fire_kernel(
     across,
     down,
-    adjacency,
-    props,
+    tables,
+    flags,
     received,
     level,
     fuel_left,
     fuel_class,
     west_side,
     east_side,
+    north,
+    south,
     level_hbm,
     fuel_hbm,
     heat_out,
@@ -336,7 +394,6 @@
     strips,
     turned,
     tanh_sum,
-    links,
     row_heat,
     sem,
 ):
@@ -345,25 +402,12 @@
     lane = lanes()
     sub = lax.broadcasted_iota(i32, (8, LANES), 0)
     lane32 = lanes((32, LANES))
-    own = 2 * (pos[0] * across + pos[1])
 
     def got(row, first=0, size=PIECES):
         return received[pl.ds(first * REC2 + row, size, stride=REC2), :]
 
-    def table(value):
-        row = jnp.zeros((8, LANES), f32)
-        for kind in range(props.shape[1]):
-            row = jnp.where(lane == kind, value(kind), row)
-        return row
-
+    table_base, table_wind, table_burn, table_heat, table_emit = [tables[k] for k in range(5)]
     log2e = math.log2(math.e)
-    table_base = table(lambda c: 0.125 * 0.3 * props[0, c])
-    table_wind = table_base * table(lambda c: 0.3 * props[1, c])
-    table_burn = (-0.5 * step_time * log2e / 4.0) / jnp.where(
-        lane < props.shape[1], table(lambda c: props[2, c]), 1.0
-    )
-    table_heat = table(lambda c: props[3, c])
-    table_emit = table(lambda c: 3.0 * props[4, c])
 
     turned[...] = jnp.zeros(turned.shape, f32)
     for q in range(2):
@@ -432,39 +476,6 @@
                     else:
                         wind[k, t, 35:37, :] = value[0:2, :]
 
-    def there(j):
-        return j >= 0
-
-    across_links = []
-    groups = []
-    for q in range(2):
-        i = own + q
-        near = [adjacency[s, i] for s in range(4)]
-        safe = [jnp.maximum(near[s], 0) for s in range(4)]
-
-        def joined(s, t):
-            return there(near[s]) & there(adjacency[t, safe[s]])
-
-        groups.append([(there(near[s]), joined(2, s), joined(3, s)) for s in range(2)])
-        across_links.append([[joined(0, t), there(near[t]), joined(1, t)] for t in (2, 3)])
-
-    def as_int(flag):
-        return jnp.where(flag, 1, 0)
-
-    for line in range(2):
-        for q in range(2):
-            mid, west, east = groups[q][line]
-            row = jnp.broadcast_to(as_int(mid), (8, LANES))
-            links[line, 3 * q] = row
-            links[line, 3 * q + 1] = row
-        w0, e0 = groups[0][line][1:]
-        w1, e1 = groups[1][line][1:]
-        links[line, 2] = jnp.where(
-            lane < 32,
-            as_int(e0),
-            jnp.where(lane < 64, as_int(w0), jnp.where(lane < 96, as_int(e1), as_int(w1))),
-        )
-
     is0 = lane == 0
     is63 = lane == 63
     is64 = lane == 64
@@ -472,11 +483,7 @@
     tanh_sum[...] = jnp.zeros(tanh_sum.shape, f32)
 
     def make_masks(region):
-        (w0, e0), (w1, e1) = [
-            [as_int(across_links[q][t][region]) for t in range(2)] for q in range(2)
-        ]
-        on = [jnp.broadcast_to(flag, (8, LANES)) > 0 for flag in (w0, e0, w1, e1)]
-        return on
+        return [flags[4 * region + k] > 0 for k in range(4)]
 
     def update(source, target, chunk, masks, rows_edge, main):
         lw0, le0, lw1, le1 = masks
@@ -487,7 +494,7 @@
         if rows_edge is not None:
             kind, line, row = rows_edge
             for t in range(5):
-                broken = (sub == row) & (links[line, t] == 0)
+                broken = (sub == row) & (flags[12 + 5 * line + t] == 0)
                 if kind == "up":
                     up[t] = jnp.where(broken, x[t], up[t])
                 else:
@@ -770,15 +777,19 @@
     )(blocks, level_set, fuel_class, air_state)
     relayed = lax.all_to_all(packed.reshape(devices, REC1, LANES), both, 0, 0)
     lanes_used = -(-blocks.shape[1] // LANES) * LANES
-    index = pl.pallas_call(
+    index, tables, flags = pl.pallas_call(
         lambda *refs: index_kernel(across, *refs),
-        out_shape=jax.ShapeDtypeStruct((WORDS + 1, lanes_used), i32),
-        in_specs=[vmem, vmem],
-        out_specs=vmem,
+        out_shape=(
+            jax.ShapeDtypeStruct((WORDS + 1, lanes_used), i32),
+            pltpu.VMEM((5, 8, LANES), f32),
+            pltpu.VMEM((22, 8, LANES), i32),
+        ),
+        in_specs=[vmem, vmem, smem, smem],
+        out_specs=(vmem, vmem, vmem),
         scratch_shapes=[pltpu.VMEM((16, lanes_used), i32)],
         cost_estimate=pl.CostEstimate(flops=20_000_000, transcendentals=0, bytes_accessed=10_000),
         name="index",
-    )(blocks, adjacency)
+    )(blocks, adjacency, adjacency, fuel_props)
     first_rows, last_rows, columns = pl.pallas_call(
         edge_kernel,
         out_shape=(
@@ -797,10 +808,10 @@
     chosen = pl.pallas_call(
         select_kernel,
         out_shape=pltpu.VMEM((devices * REC2, LANES), f32),
-        in_specs=[smem, vmem, vmem, vmem],
+        in_specs=[smem, vmem],
         out_specs=vmem,
         name="select",
-    )(index, near(relayed.reshape(devices * REC1, LANES)), north, south)
+    )(index, near(relayed.reshape(devices * REC1, LANES)))
     columns, chosen = lax.optimization_barrier((columns, chosen))
     west_side = near(lax.ppermute(columns, "gy", [(k, k + 1) for k in range(across - 1)]))
     east_side = near(lax.ppermute(columns, "gy", [(k + 1, k) for k in range(across - 1)]))
@@ -814,7 +825,7 @@
             jax.ShapeDtypeStruct(level_set.shape, f32),
             pltpu.VMEM((devices * HEAT_ROWS, LANES), f32),
         ),
-        in_specs=[smem, smem, vmem, vmem, vmem, vmem] + [vmem] * 2,
+        in_specs=[vmem] * 10,
         out_specs=(anywhere, anywhere, vmem),
         scratch_shapes=[
             pltpu.VMEM(level_set.shape, f32),
@@ -827,20 +838,21 @@
             pltpu.VMEM((40, LANES), f32),
             pltpu.VMEM((2, LANES, 256), f32),
             pltpu.VMEM((4, 256, LANES), f32),
-            pltpu.VMEM((2, 5, 8, LANES), i32),
             pltpu.VMEM((4, 32, LANES), f32),
             pltpu.SemaphoreType.DMA((2, 32 // FINISH_UNROLL)),
         ],
         name="fire",
     )(
-        adjacency,
-        fuel_props,
+        near(tables),
+        near(flags),
         received,
         near(level_set),
         near(fuel_left),
         near(fuel_class),
         west_side,
         east_side,
+        north,
+        south,
     )
     gathered = lax.all_to_all(heat.reshape(devices, 1, HEAT_ROWS * LANES), both, 0, 0)
     gathered = near(gathered.reshape(devices * HEAT_ROWS, LANES))
@@ -868,7 +880,7 @@
         scratch_shapes=[pltpu.VMEM((128, LANES), f32), pltpu.SemaphoreType.DMA(())],
         input_output_aliases={4: 0},
         name="heat",
-    )(blocks, index, gathered, plane, air_next)
+    )(blocks, index, gathered, near(plane), air_next)
     return (air_next, level_next, fuel_next, totals)
 
 

time: 74.3 us -> 72.3 us (0.973)
  starting transfers between devices: 28.3 us -> 25.4 us
  waiting for transfers between devices: 10.8 us -> 12.8 us
    all_to_all x1, waiting for transfers between devices: 0.01 us -> 5.43 us  [local(): relayed = lax.all_to_all(packed.reshape(devices, REC1, LANES), both, 0, 0)]
    all_to_all x1, starting transfers between devices: 6.79 us -> 2.59 us  [local(): received = lax.all_to_all(chosen.reshape(devices, REC2, LANES), both, 0, 0)]
    all_to_all x1, starting transfers between devices: 4.88 us -> 6.78 us  [local(): lax.all_to_all(heat.reshape(devices, 1, HEAT_ROWS * LANES), both, 0, 0)]
    all_to_all x1, waiting for transfers between devices: 1.74 us -> 0.01 us  [local(): received = lax.all_to_all(chosen.reshape(devices, REC2, LANES), both, 0, 0)]
    ppermute x1, waiting for transfers between devices: 1.69 us -> 0.01 us  [local(): lax.ppermute(columns, 'gy', [(k + 1, k) for k in range(across - 1)])]
    ppermute x1, waiting for transfers between devices: 1.15 us -> 0.01 us  [local(): lax.ppermute(columns, 'gy', [(k, k + 1) for k in range(across - 1)])]
    pallas_call x1, Pallas kernels: 13.5 us -> 12.8 us  [local(): pl.pallas_call(lambda *refs: fire_kernel(across, down, *refs), out_shape=...]
  transfers between devices with their start and end apart: 7 -> 7, of which waited for: 5 -> 3; matrix products, arithmetic and copies ran while one was open for 0% -> 0% of each run, Pallas kernels for 16% -> 17%
where the time goes in v5:
time: 72.3 us; the launch traced here: 71.8 us
  Pallas kernels  32.8 us (45%)
  starting transfers between devices  25.4 us (35%)
  waiting for transfers between devices  12.8 us (18%)
  between operations  0.78 us (1%)
    pallas_call x1, Pallas kernels, local(): pl.pallas_call(lambda *refs: fire_kernel(across, down, *refs), out_shape=...  12.8 us
    all_to_all x1, starting transfers between devices, local(): relayed = lax.all_to_all(packed.reshape(devices, REC1, LANES), both, 0, 0)  7.33 us
    pallas_call x1, Pallas kernels, local(): pl.pallas_call(air_kernel, out_shape=(jax.ShapeDtypeStruct(air_state.shap...  6.99 us
    all_to_all x1, starting transfers between devices, local(): lax.all_to_all(heat.reshape(devices, 1, HEAT_ROWS * LANES), both, 0, 0)  6.78 us
    all_to_all x1, waiting for transfers between devices, local(): relayed = lax.all_to_all(packed.reshape(devices, REC1, LANES), both, 0, 0)  5.43 us
    ppermute x1, starting transfers between devices, local(): lax.ppermute(columns, 'gy', [(k, k + 1) for k in range(across - 1)])  4.55 us
    all_to_all x1, waiting for transfers between devices, local(): lax.all_to_all(heat.reshape(devices, 1, HEAT_ROWS * LANES), both, 0, 0)  3.88 us
    ppermute x1, waiting for transfers between devices, local(): lax.ppermute(first_rows, 'gx', [(k + 1, k) for k in range(down - 1)])  3.48 us
  transfers between devices with their start and end apart: 7, of which 3 were waited for; matrix products, arithmetic and copies ran while one was open for 0% of the time, Pallas kernels for 17%

profile of v5, /device:TPU:0, one launch (start us, length us, event | category | flops | bytes accessed | tf_op | source)
XLA Modules:
  0.0 71.8 jit_solution(9328745021736797246)
XLA Ops:
  0.6 3.2 %pack.1 = f32[512,128]{1,0:T(8,128)} custom-call(s32[2,64]{1,0:T(2,128)} %bitcast.13, f32[2,256,256]{2,1,0:T(8,128)} %refs_3_.3, s32[2,256,256]{2,1,0:T(8,128)} %refs_5_.1, f32[3,16,128,128]{3,2,1,0:T(8,128)} %air_hbm.3), custom_call_target="tpu_custom_call" | custom-call | tf_op jit(solution)/shard_map/pack/pallas_call | solution.py:763
  3.8 0.0 copy-start
  3.8 0.0 copy-start.1
  3.9 0.0 copy-start.2
  3.9 7.3 %all-to-all-start = ((f32[32,16,128]{2,1,0:T(8,128)}), f32[32,16,128]{2,1,0:T(8,128)S(1)}, u32[]{:S(2)}, u32[]{:S(2)}) async-start(f32[32,16,128]{2,1,0:T(8,128)} %bitcast.3), calls=%async_computation | async-start | bytes 524288 | tf_op jit(solution)/shard_map/all_to_all | solution.py:778
  11.2 1.7 %index.1 = (s32[16,128]{1,0:T(8,128)}, f32[5,8,128]{2,1,0:T(8,128)S(1)}, s32[22,8,128]{2,1,0:T(8,128)S(1)}) custom-call(s32[2,64]{1,0:T(2,128)} %bitcast.14, s32[4,64]{1,0:T(4,128)} %bitcast.16, s32[4,64]{1,0:T(4,128)} %bitcast.17, f32[5,13]{1,0:T(8,128)} %refs_3_.2), custom_call_target="tpu_custom_call" | custom-call | flops 20000000 | bytes 10000 | tf_op jit(solution)/shard_map/index/pallas_call | solution.py:780
  12.9 3.3 %edge.1 = (f32[48,128]{1,0:T(8,128)S(1)}, f32[48,128]{1,0:T(8,128)S(1)}, f32[128,128]{1,0:T(8,128)S(1)}) custom-call(f32[6144,128]{1,0:T(8,128)} %bitcast.12, s32[16,128]{1,0:T(8,128)} %get-tuple-element.19.ready.index.refs_1_), custom_call_target="tpu_custom_call" | custom-call | flops 30000000 | bytes 3200000 | tf_op jit(solution)/shard_map/edge/pallas_call | solution.py:793
  16.2 5.4 %all-to-all-done = f32[32,16,128]{2,1,0:T(8,128)S(1)} async-done(((f32[32,16,128]{2,1,0:T(8,128)}), f32[32,16,128]{2,1,0:T(8,128)S(1)}, u32[]{:S(2)}, u32[]{:S(2)}) %all-to-all-start) | async-done | bytes 262176 | tf_op jit(solution)/shard_map/all_to_all | solution.py:778
  21.7 2.6 %select.1 = f32[512,128]{1,0:T(8,128)} custom-call(s32[16,128]{1,0:T(8,128)} %get-tuple-element.19.ready.index.refs_1_, f32[512,128]{1,0:T(8,128)S(1)} %bitcast.10), custom_call_target="tpu_custom_call" | custom-call | tf_op jit(solution)/shard_map/select/pallas_call | solution.py:808
  24.3 2.6 %all-to-all-start.1 = ((f32[32,16,128]{2,1,0:T(8,128)}), f32[32,16,128]{2,1,0:T(8,128)S(1)}, u32[]{:S(2)}, u32[]{:S(2)}) async-start(f32[32,16,128]{2,1,0:T(8,128)} %bitcast.5), calls=%async_computation.1 | async-start | bytes 524288 | tf_op jit(solution)/shard_map/all_to_all | solution.py:818
  26.9 1.3 %collective-permute-start.1 = (f32[128,128]{1,0:T(8,128)S(1)}, f32[128,128]{1,0:T(8,128)S(1)}, u32[]{:S(2)}, u32[]{:S(2)}) collective-permute-start(f32[128,128]{1,0:T(8,128)S(1)} %get-tuple-element.24), channel_id=1, source_target_pairs={{1,0},{2,1},{3,2},{4,3},{5,4},{6,5},{7,6},{9,8},{10,9},{11,10},{12... | collective-permute-start | bytes 196616 | tf_op jit(solution)/shard_map/ppermute | solution.py:817
  28.2 4.5 %collective-permute-start = (f32[128,128]{1,0:T(8,128)S(1)}, f32[128,128]{1,0:T(8,128)S(1)}, u32[]{:S(2)}, u32[]{:S(2)}) collective-permute-start(f32[128,128]{1,0:T(8,128)S(1)} %get-tuple-element.24), channel_id=1, source_target_pairs={{0,1},{1,2},{2,3},{3,4},{4,5},{5,6},{6,7},{8,9},{9,10},{10,11},{11... | collective-permute-start | bytes 196616 | tf_op jit(solution)/shard_map/ppermute | solution.py:816
  32.7 1.5 %collective-permute-start.2 = (f32[48,128]{1,0:T(8,128)S(1)}, f32[48,128]{1,0:T(8,128)S(1)}, u32[]{:S(2)}, u32[]{:S(2)}) collective-permute-start(f32[48,128]{1,0:T(8,128)S(1)} %get-tuple-element.25), channel_id=1, source_target_pairs={{0,8},{8,16},{16,24},{1,9},{9,17},{17,25},{2,10},{10,18},{18,26},{... | collective-permute-start | bytes 73736 | tf_op jit(solution)/shard_map/ppermute | solution.py:806
  34.3 1.3 %collective-permute-start.3 = (f32[48,128]{1,0:T(8,128)S(1)}, f32[48,128]{1,0:T(8,128)S(1)}, u32[]{:S(2)}, u32[]{:S(2)}) collective-permute-start(f32[48,128]{1,0:T(8,128)S(1)} %get-tuple-element.26), channel_id=1, source_target_pairs={{8,0},{16,8},{24,16},{9,1},{17,9},{25,17},{10,2},{18,10},{26,18},{... | collective-permute-start | bytes 73736 | tf_op jit(solution)/shard_map/ppermute | solution.py:807
  35.6 0.0 collective-permute-done.2.refs_8_.north
  35.6 3.5 %collective-permute-done.3.refs_9_.south = f32[48,128]{1,0:T(8,128)S(1)} collective-permute-done((f32[48,128]{1,0:T(8,128)S(1)}, f32[48,128]{1,0:T(8,128)S(1)}, u32[]{:S(2)}, u32[]{:S(2)}) %collective-permute-start.3) | collective-permute-done | bytes 24608 | tf_op jit(solution)/shard_map/ppermute | solution.py:807
  39.1 0.0 collective-permute-done.1.refs_7_.east_side
  39.1 0.0 collective-permute-done.refs_6_.west_side
  39.1 0.0 all-to-all-done.1
  39.1 0.0 copy-done
  39.1 0.0 copy-done.1
  39.1 0.0 copy-done.2
  39.1 12.8 %fire.1 = (f32[2,256,256]{2,1,0:T(8,128)}, f32[2,256,256]{2,1,0:T(8,128)}, f32[544,128]{1,0:T(8,128)}) custom-call(f32[5,8,128]{2,1,0:T(8,128)S(1)} %get-tuple-element.20.refs_0_, s32[22,8,128]{2,1,0:T(8,128)S(1)} %get-tuple-element.21.refs_1_, f32[512,128]{1,0:T(8,128)S(1)} %bitcast.11, f32[2,256,256]{2,1,0:T(8,128)S(1)} %copy-done, ...), custom_call_target="tpu_custom_call" | custom-call | tf_op jit(solution)/shard_map/fire/pallas_call | solution.py:821
  51.9 6.8 %all-to-all-start.2 = ((f32[32,1,2176]{2,1,0:T(1,128)}), f32[32,1,2176]{2,1,0:T(1,128)S(1)}, u32[]{:S(2)}, u32[]{:S(2)}) async-start(f32[32,1,2176]{2,1,0:T(1,128)} %bitcast.7), calls=%async_computation.2 | async-start | bytes 557056 | tf_op jit(solution)/shard_map/all_to_all | solution.py:857
  58.7 7.0 %air.1 = (f32[3,16,128,128]{3,2,1,0:T(8,128)}, f32[128,128]{1,0:T(8,128)S(1)}) custom-call(f32[48,128]{1,0:T(8,128)S(1)} %collective-permute-done.2.refs_8_.north, f32[48,128]{1,0:T(8,128)S(1)} %collective-permute-done.3.refs_9_.south, f32[128,128]{1,0:T(8,128)S(1)} %collective-permute-done.refs_6_.west_side, ...), custom_call_target="tpu_custom_call" | custom-call | flops 80000000 | bytes 6300000 | tf_op jit(solution)/shard_map/air/pallas_call | solution.py:859
  65.7 3.9 %all-to-all-done.2 = f32[32,1,2176]{2,1,0:T(1,128)S(1)} async-done(((f32[32,1,2176]{2,1,0:T(1,128)}), f32[32,1,2176]{2,1,0:T(1,128)S(1)}, u32[]{:S(2)}, u32[]{:S(2)}) %all-to-all-start.2) | async-done | bytes 278560 | tf_op jit(solution)/shard_map/all_to_all | solution.py:857
  69.5 2.2 %heat.1 = (f32[3,16,128,128]{3,2,1,0:T(8,128)}, f32[2]{0:T(128)}) custom-call(s32[2,64]{1,0:T(2,128)} %bitcast.15, s32[16,128]{1,0:T(8,128)} %get-tuple-element.19.ready.index.refs_1_, f32[544,128]{1,0:T(8,128)S(1)} %bitcast.9, f32[128,128]{1,0:T(8,128)S(1)} %get-tuple-element.28.refs_3_, ...), custom_call_target="tpu_custom_call", output_to_operand_aliasing={{0}: (4, {})} | custom-call | tf_op jit(solution)/shard_map/heat/pallas_call | solution.py:875
Async XLA Ops:
  3.8 35.2 %copy-start = (f32[2,256,256]{2,1,0:T(8,128)S(1)}, f32[2,256,256]{2,1,0:T(8,128)}, u32[]{:S(2)}) copy-start(f32[2,256,256]{2,1,0:T(8,128)} %refs_3_.3) | copy-start | bytes 1572868
  3.8 35.2 %copy-start.1 = (s32[2,256,256]{2,1,0:T(8,128)S(1)}, s32[2,256,256]{2,1,0:T(8,128)}, u32[]{:S(2)}) copy-start(s32[2,256,256]{2,1,0:T(8,128)} %refs_5_.1) | copy-start | bytes 1572868
  3.9 35.2 %copy-start.2 = (f32[2,256,256]{2,1,0:T(8,128)S(1)}, f32[2,256,256]{2,1,0:T(8,128)}, u32[]{:S(2)}) copy-start(f32[2,256,256]{2,1,0:T(8,128)} %refs_4_.1) | copy-start | bytes 1572868
  3.9 17.8 %all-to-all-start = ((f32[32,16,128]{2,1,0:T(8,128)}), f32[32,16,128]{2,1,0:T(8,128)S(1)}, u32[]{:S(2)}, u32[]{:S(2)}) async-start(f32[32,16,128]{2,1,0:T(8,128)} %bitcast.3), calls=%async_computation | async-start | bytes 524288 | tf_op jit(solution)/shard_map/all_to_all | solution.py:778
  24.3 14.8 %all-to-all-start.1 = ((f32[32,16,128]{2,1,0:T(8,128)}), f32[32,16,128]{2,1,0:T(8,128)S(1)}, u32[]{:S(2)}, u32[]{:S(2)}) async-start(f32[32,16,128]{2,1,0:T(8,128)} %bitcast.5), calls=%async_computation.1 | async-start | bytes 524288 | tf_op jit(solution)/shard_map/all_to_all | solution.py:818
  26.9 12.2 %collective-permute-start.1 = (f32[128,128]{1,0:T(8,128)S(1)}, f32[128,128]{1,0:T(8,128)S(1)}, u32[]{:S(2)}, u32[]{:S(2)}) collective-permute-start(f32[128,128]{1,0:T(8,128)S(1)} %get-tuple-element.24), channel_id=1, source_target_pairs={{1,0},{2,1},{3,2},{4,3},{5,4},{6,5},{7,6},{9,8},{10,9},{11,10},{12... | collective-permute-start | bytes 196616 | tf_op jit(solution)/shard_map/ppermute | solution.py:817
  28.2 10.9 %collective-permute-start = (f32[128,128]{1,0:T(8,128)S(1)}, f32[128,128]{1,0:T(8,128)S(1)}, u32[]{:S(2)}, u32[]{:S(2)}) collective-permute-start(f32[128,128]{1,0:T(8,128)S(1)} %get-tuple-element.24), channel_id=1, source_target_pairs={{0,1},{1,2},{2,3},{3,4},{4,5},{5,6},{6,7},{8,9},{9,10},{10,11},{11... | collective-permute-start | bytes 196616 | tf_op jit(solution)/shard_map/ppermute | solution.py:816
  32.7 2.9 %collective-permute-start.2 = (f32[48,128]{1,0:T(8,128)S(1)}, f32[48,128]{1,0:T(8,128)S(1)}, u32[]{:S(2)}, u32[]{:S(2)}) collective-permute-start(f32[48,128]{1,0:T(8,128)S(1)} %get-tuple-element.25), channel_id=1, source_target_pairs={{0,8},{8,16},{16,24},{1,9},{9,17},{17,25},{2,10},{10,18},{18,26},{... | collective-permute-start | bytes 73736 | tf_op jit(solution)/shard_map/ppermute | solution.py:806
  34.3 4.8 %collective-permute-start.3 = (f32[48,128]{1,0:T(8,128)S(1)}, f32[48,128]{1,0:T(8,128)S(1)}, u32[]{:S(2)}, u32[]{:S(2)}) collective-permute-start(f32[48,128]{1,0:T(8,128)S(1)} %get-tuple-element.26), channel_id=1, source_target_pairs={{8,0},{16,8},{24,16},{9,1},{17,9},{25,17},{10,2},{18,10},{26,18},{... | collective-permute-start | bytes 73736 | tf_op jit(solution)/shard_map/ppermute | solution.py:807
  51.9 17.7 %all-to-all-start.2 = ((f32[32,1,2176]{2,1,0:T(1,128)}), f32[32,1,2176]{2,1,0:T(1,128)S(1)}, u32[]{:S(2)}, u32[]{:S(2)}) async-start(f32[32,1,2176]{2,1,0:T(1,128)} %bitcast.7), calls=%async_computation.2 | async-start | bytes 557056 | tf_op jit(solution)/shard_map/all_to_all | solution.py:857

commit v6 on v5

--- a/solution.py
+++ b/solution.py
@@ -304,7 +304,7 @@
 
     for line in range(2):
         for q in range(2):
-            mid, west, east = groups[q][line]
+            mid, _, _ = groups[q][line]
             row = jnp.broadcast_to(as_int(mid), (8, LANES))
             flags[12 + 5 * line + 3 * q] = row
             flags[12 + 5 * line + 3 * q + 1] = row
@@ -398,7 +398,6 @@
     sem,
 ):
     cur = (cur_a, cur_b)
-    pos = position()
     lane = lanes()
     sub = lax.broadcasted_iota(i32, (8, LANES), 0)
     lane32 = lanes((32, LANES))
@@ -750,7 +749,7 @@
     store.wait()
 
 
-def local(air_state, level_set, fuel_left, fuel_class, fuel_props, blocks, adjacency):
+def step(air_state, level_set, fuel_left, fuel_class, fuel_props, blocks, adjacency):
     down = lax.axis_size("gx")
     across = lax.axis_size("gy")
     devices = down * across
@@ -803,8 +802,10 @@
         cost_estimate=pl.CostEstimate(flops=30_000_000, transcendentals=0, bytes_accessed=3_200_000),
         name="edge",
     )(air_state.reshape(48 * 128, LANES), index)
-    north = near(lax.ppermute(last_rows, "gx", [(k, k + 1) for k in range(down - 1)]))
-    south = near(lax.ppermute(first_rows, "gx", [(k + 1, k) for k in range(down - 1)]))
+    north = lax.ppermute(last_rows, "gx", [(k, k + 1) for k in range(down - 1)])
+    south = lax.ppermute(first_rows, "gx", [(k + 1, k) for k in range(down - 1)])
+    north = near(north)
+    south = near(south)
     chosen = pl.pallas_call(
         select_kernel,
         out_shape=pltpu.VMEM((devices * REC2, LANES), f32),
@@ -812,9 +813,10 @@
         out_specs=vmem,
         name="select",
     )(index, near(relayed.reshape(devices * REC1, LANES)))
-    columns, chosen = lax.optimization_barrier((columns, chosen))
-    west_side = near(lax.ppermute(columns, "gy", [(k, k + 1) for k in range(across - 1)]))
-    east_side = near(lax.ppermute(columns, "gy", [(k + 1, k) for k in range(across - 1)]))
+    west_side = lax.ppermute(columns, "gy", [(k, k + 1) for k in range(across - 1)])
+    east_side = lax.ppermute(columns, "gy", [(k + 1, k) for k in range(across - 1)])
+    west_side = near(west_side)
+    east_side = near(east_side)
     received = lax.all_to_all(chosen.reshape(devices, REC2, LANES), both, 0, 0)
     received = received.reshape(devices * REC2, LANES)[: PIECES * REC2]
     received = near(received)
@@ -904,4 +906,4 @@
         P(("gx", "gy"), None, None),
         P(),
     )
-    return jax.shard_map(local, mesh=mesh, in_specs=in_specs, out_specs=out_specs, check_vma=False)
+    return jax.shard_map(step, mesh=mesh, in_specs=in_specs, out_specs=out_specs, check_vma=False)

time: 72.3 us -> 75.7 us (1.047)
  waiting for transfers between devices: 12.8 us -> 16.1 us
    all_to_all x3, waiting for transfers between devices: 9.31 us -> 12.6 us  [the longest x1 8.73 us: step(): relayed = lax.all_to_all(packed.reshape(devices, REC1, LANES), both, 0, 0)]
  transfers between devices with their start and end apart: 7 -> 7, of which waited for: 3 -> 3; matrix products, arithmetic and copies ran while one was open for 0% -> 0% of each run, Pallas kernels for 17% -> 16%
where the time goes in v6:
time: 75.7 us; the launch traced here: 75.1 us
  Pallas kernels  32.9 us (43%)
  starting transfers between devices  25.4 us (34%)
  waiting for transfers between devices  16.1 us (21%)
  between operations  0.78 us (1%)
    pallas_call x1, Pallas kernels, step(): pl.pallas_call(lambda *refs: fire_kernel(across, down, *refs), out_shape=...  12.7 us
    all_to_all x1, waiting for transfers between devices, step(): relayed = lax.all_to_all(packed.reshape(devices, REC1, LANES), both, 0, 0)  8.73 us
    all_to_all x1, starting transfers between devices, step(): relayed = lax.all_to_all(packed.reshape(devices, REC1, LANES), both, 0, 0)  7.33 us
    pallas_call x1, Pallas kernels, step(): pl.pallas_call(air_kernel, out_shape=(jax.ShapeDtypeStruct(air_state.shap...  6.99 us
    all_to_all x1, starting transfers between devices, step(): lax.all_to_all(heat.reshape(devices, 1, HEAT_ROWS * LANES), both, 0, 0)  6.78 us
    ppermute x1, starting transfers between devices, step(): lax.ppermute(columns, 'gy', [(k, k + 1) for k in range(across - 1)])  4.55 us
    all_to_all x1, waiting for transfers between devices, step(): lax.all_to_all(heat.reshape(devices, 1, HEAT_ROWS * LANES), both, 0, 0)  3.88 us
    ppermute x1, waiting for transfers between devices, step(): lax.ppermute(first_rows, 'gx', [(k + 1, k) for k in range(down - 1)])  3.48 us
  transfers between devices with their start and end apart: 7, of which 3 were waited for; matrix products, arithmetic and copies ran while one was open for 0% of the time, Pallas kernels for 16%

profile of v6, /device:TPU:0, one launch (start us, length us, event | category | flops | bytes accessed | tf_op | source)
XLA Modules:
  0.0 75.1 jit_solution(4046598686923165477)
XLA Ops:
  0.6 3.2 %pack.1 = f32[512,128]{1,0:T(8,128)} custom-call(s32[2,64]{1,0:T(2,128)} %bitcast.13, f32[2,256,256]{2,1,0:T(8,128)} %refs_3_.3, s32[2,256,256]{2,1,0:T(8,128)} %refs_5_.1, f32[3,16,128,128]{3,2,1,0:T(8,128)} %air_hbm.3), custom_call_target="tpu_custom_call" | custom-call | tf_op jit(solution)/shard_map/pack/pallas_call | solution.py:762
  3.8 0.0 copy-start
  3.8 0.0 copy-start.1
  3.9 0.0 copy-start.2
  3.9 7.3 %all-to-all-start = ((f32[32,16,128]{2,1,0:T(8,128)}), f32[32,16,128]{2,1,0:T(8,128)S(1)}, u32[]{:S(2)}, u32[]{:S(2)}) async-start(f32[32,16,128]{2,1,0:T(8,128)} %bitcast.2), calls=%async_computation | async-start | bytes 524288 | tf_op jit(solution)/shard_map/all_to_all | solution.py:777
  11.2 1.7 %index.1 = (s32[16,128]{1,0:T(8,128)}, f32[5,8,128]{2,1,0:T(8,128)S(1)}, s32[22,8,128]{2,1,0:T(8,128)S(1)}) custom-call(s32[2,64]{1,0:T(2,128)} %bitcast.14, s32[4,64]{1,0:T(4,128)} %bitcast.16, s32[4,64]{1,0:T(4,128)} %bitcast.17, f32[5,13]{1,0:T(8,128)} %refs_3_.2), custom_call_target="tpu_custom_call" | custom-call | flops 20000000 | bytes 10000 | tf_op jit(solution)/shard_map/index/pallas_call | solution.py:779
  12.9 8.7 %all-to-all-done = f32[32,16,128]{2,1,0:T(8,128)S(1)} async-done(((f32[32,16,128]{2,1,0:T(8,128)}), f32[32,16,128]{2,1,0:T(8,128)S(1)}, u32[]{:S(2)}, u32[]{:S(2)}) %all-to-all-start) | async-done | bytes 262176 | tf_op jit(solution)/shard_map/all_to_all | solution.py:777
  21.7 2.6 %select.1 = f32[512,128]{1,0:T(8,128)} custom-call(s32[16,128]{1,0:T(8,128)} %get-tuple-element.17.index.ready.refs_1_, f32[512,128]{1,0:T(8,128)S(1)} %bitcast.10), custom_call_target="tpu_custom_call" | custom-call | tf_op jit(solution)/shard_map/select/pallas_call | solution.py:809
  24.3 2.6 %all-to-all-start.1 = ((f32[32,16,128]{2,1,0:T(8,128)}), f32[32,16,128]{2,1,0:T(8,128)S(1)}, u32[]{:S(2)}, u32[]{:S(2)}) async-start(f32[32,16,128]{2,1,0:T(8,128)} %bitcast.4), calls=%async_computation.1 | async-start | bytes 524288 | tf_op jit(solution)/shard_map/all_to_all | solution.py:820
  26.9 3.3 %edge.1 = (f32[48,128]{1,0:T(8,128)S(1)}, f32[48,128]{1,0:T(8,128)S(1)}, f32[128,128]{1,0:T(8,128)S(1)}) custom-call(f32[6144,128]{1,0:T(8,128)} %bitcast.12, s32[16,128]{1,0:T(8,128)} %get-tuple-element.17.index.ready.refs_1_), custom_call_target="tpu_custom_call" | custom-call | flops 30000000 | bytes 3200000 | tf_op jit(solution)/shard_map/edge/pallas_call | solution.py:792
  30.2 1.3 %collective-permute-start.1 = (f32[128,128]{1,0:T(8,128)S(1)}, f32[128,128]{1,0:T(8,128)S(1)}, u32[]{:S(2)}, u32[]{:S(2)}) collective-permute-start(f32[128,128]{1,0:T(8,128)S(1)} %get-tuple-element.20), channel_id=1, source_target_pairs={{1,0},{2,1},{3,2},{4,3},{5,4},{6,5},{7,6},{9,8},{10,9},{11,10},{12... | collective-permute-start | bytes 196616 | tf_op jit(solution)/shard_map/ppermute | solution.py:817
  31.5 4.5 %collective-permute-start = (f32[128,128]{1,0:T(8,128)S(1)}, f32[128,128]{1,0:T(8,128)S(1)}, u32[]{:S(2)}, u32[]{:S(2)}) collective-permute-start(f32[128,128]{1,0:T(8,128)S(1)} %get-tuple-element.20), channel_id=1, source_target_pairs={{0,1},{1,2},{2,3},{3,4},{4,5},{5,6},{6,7},{8,9},{9,10},{10,11},{11... | collective-permute-start | bytes 196616 | tf_op jit(solution)/shard_map/ppermute | solution.py:816
  36.0 1.5 %collective-permute-start.2 = (f32[48,128]{1,0:T(8,128)S(1)}, f32[48,128]{1,0:T(8,128)S(1)}, u32[]{:S(2)}, u32[]{:S(2)}) collective-permute-start(f32[48,128]{1,0:T(8,128)S(1)} %get-tuple-element.21), channel_id=1, source_target_pairs={{0,8},{8,16},{16,24},{1,9},{9,17},{17,25},{2,10},{10,18},{18,26},{... | collective-permute-start | bytes 73736 | tf_op jit(solution)/shard_map/ppermute | solution.py:805
  37.6 1.3 %collective-permute-start.3 = (f32[48,128]{1,0:T(8,128)S(1)}, f32[48,128]{1,0:T(8,128)S(1)}, u32[]{:S(2)}, u32[]{:S(2)}) collective-permute-start(f32[48,128]{1,0:T(8,128)S(1)} %get-tuple-element.22), channel_id=1, source_target_pairs={{8,0},{16,8},{24,16},{9,1},{17,9},{25,17},{10,2},{18,10},{26,18},{... | collective-permute-start | bytes 73736 | tf_op jit(solution)/shard_map/ppermute | solution.py:806
  38.9 0.0 collective-permute-done.2.refs_8_.north
  38.9 3.5 %collective-permute-done.3.refs_9_.south = f32[48,128]{1,0:T(8,128)S(1)} collective-permute-done((f32[48,128]{1,0:T(8,128)S(1)}, f32[48,128]{1,0:T(8,128)S(1)}, u32[]{:S(2)}, u32[]{:S(2)}) %collective-permute-start.3) | collective-permute-done | bytes 24608 | tf_op jit(solution)/shard_map/ppermute | solution.py:806
  42.4 0.0 collective-permute-done.1.refs_7_.east_side
  42.4 0.0 collective-permute-done.refs_6_.west_side
  42.4 0.0 all-to-all-done.1
  42.4 0.0 copy-done
  42.4 0.0 copy-done.1
  42.4 0.0 copy-done.2
  42.4 12.7 %fire.1 = (f32[2,256,256]{2,1,0:T(8,128)}, f32[2,256,256]{2,1,0:T(8,128)}, f32[544,128]{1,0:T(8,128)}) custom-call(f32[5,8,128]{2,1,0:T(8,128)S(1)} %get-tuple-element.18.refs_0_, s32[22,8,128]{2,1,0:T(8,128)S(1)} %get-tuple-element.19.refs_1_, f32[512,128]{1,0:T(8,128)S(1)} %bitcast.11, f32[2,256,256]{2,1,0:T(8,128)S(1)} %copy-done, ...), custom_call_target="tpu_custom_call" | custom-call | tf_op jit(solution)/shard_map/fire/pallas_call | solution.py:823
  55.2 6.8 %all-to-all-start.2 = ((f32[32,1,2176]{2,1,0:T(1,128)}), f32[32,1,2176]{2,1,0:T(1,128)S(1)}, u32[]{:S(2)}, u32[]{:S(2)}) async-start(f32[32,1,2176]{2,1,0:T(1,128)} %bitcast.7), calls=%async_computation.2 | async-start | bytes 557056 | tf_op jit(solution)/shard_map/all_to_all | solution.py:859
  62.0 7.0 %air.1 = (f32[3,16,128,128]{3,2,1,0:T(8,128)}, f32[128,128]{1,0:T(8,128)S(1)}) custom-call(f32[48,128]{1,0:T(8,128)S(1)} %collective-permute-done.2.refs_8_.north, f32[48,128]{1,0:T(8,128)S(1)} %collective-permute-done.3.refs_9_.south, f32[128,128]{1,0:T(8,128)S(1)} %collective-permute-done.refs_6_.west_side, ...), custom_call_target="tpu_custom_call" | custom-call | flops 80000000 | bytes 6300000 | tf_op jit(solution)/shard_map/air/pallas_call | solution.py:861
  69.0 3.9 %all-to-all-done.2 = f32[32,1,2176]{2,1,0:T(1,128)S(1)} async-done(((f32[32,1,2176]{2,1,0:T(1,128)}), f32[32,1,2176]{2,1,0:T(1,128)S(1)}, u32[]{:S(2)}, u32[]{:S(2)}) %all-to-all-start.2) | async-done | bytes 278560 | tf_op jit(solution)/shard_map/all_to_all | solution.py:859
  72.8 2.3 %heat.1 = (f32[3,16,128,128]{3,2,1,0:T(8,128)}, f32[2]{0:T(128)}) custom-call(s32[2,64]{1,0:T(2,128)} %bitcast.15, s32[16,128]{1,0:T(8,128)} %get-tuple-element.17.index.ready.refs_1_, f32[544,128]{1,0:T(8,128)S(1)} %bitcast.9, f32[128,128]{1,0:T(8,128)S(1)} %get-tuple-element.24.refs_3_, ...), custom_call_target="tpu_custom_call", output_to_operand_aliasing={{0}: (4, {})} | custom-call | tf_op jit(solution)/shard_map/heat/pallas_call | solution.py:877
Async XLA Ops:
  3.8 38.5 %copy-start = (f32[2,256,256]{2,1,0:T(8,128)S(1)}, f32[2,256,256]{2,1,0:T(8,128)}, u32[]{:S(2)}) copy-start(f32[2,256,256]{2,1,0:T(8,128)} %refs_3_.3) | copy-start | bytes 1572868
  3.8 38.5 %copy-start.1 = (s32[2,256,256]{2,1,0:T(8,128)S(1)}, s32[2,256,256]{2,1,0:T(8,128)}, u32[]{:S(2)}) copy-start(s32[2,256,256]{2,1,0:T(8,128)} %refs_5_.1) | copy-start | bytes 1572868
  3.9 38.5 %copy-start.2 = (f32[2,256,256]{2,1,0:T(8,128)S(1)}, f32[2,256,256]{2,1,0:T(8,128)}, u32[]{:S(2)}) copy-start(f32[2,256,256]{2,1,0:T(8,128)} %refs_4_.1) | copy-start | bytes 1572868
  3.9 17.8 %all-to-all-start = ((f32[32,16,128]{2,1,0:T(8,128)}), f32[32,16,128]{2,1,0:T(8,128)S(1)}, u32[]{:S(2)}, u32[]{:S(2)}) async-start(f32[32,16,128]{2,1,0:T(8,128)} %bitcast.2), calls=%async_computation | async-start | bytes 524288 | tf_op jit(solution)/shard_map/all_to_all | solution.py:777
  24.3 18.1 %all-to-all-start.1 = ((f32[32,16,128]{2,1,0:T(8,128)}), f32[32,16,128]{2,1,0:T(8,128)S(1)}, u32[]{:S(2)}, u32[]{:S(2)}) async-start(f32[32,16,128]{2,1,0:T(8,128)} %bitcast.4), calls=%async_computation.1 | async-start | bytes 524288 | tf_op jit(solution)/shard_map/all_to_all | solution.py:820
  30.2 12.2 %collective-permute-start.1 = (f32[128,128]{1,0:T(8,128)S(1)}, f32[128,128]{1,0:T(8,128)S(1)}, u32[]{:S(2)}, u32[]{:S(2)}) collective-permute-start(f32[128,128]{1,0:T(8,128)S(1)} %get-tuple-element.20), channel_id=1, source_target_pairs={{1,0},{2,1},{3,2},{4,3},{5,4},{6,5},{7,6},{9,8},{10,9},{11,10},{12... | collective-permute-start | bytes 196616 | tf_op jit(solution)/shard_map/ppermute | solution.py:817
  31.5 10.9 %collective-permute-start = (f32[128,128]{1,0:T(8,128)S(1)}, f32[128,128]{1,0:T(8,128)S(1)}, u32[]{:S(2)}, u32[]{:S(2)}) collective-permute-start(f32[128,128]{1,0:T(8,128)S(1)} %get-tuple-element.20), channel_id=1, source_target_pairs={{0,1},{1,2},{2,3},{3,4},{4,5},{5,6},{6,7},{8,9},{9,10},{10,11},{11... | collective-permute-start | bytes 196616 | tf_op jit(solution)/shard_map/ppermute | solution.py:816
  36.0 2.9 %collective-permute-start.2 = (f32[48,128]{1,0:T(8,128)S(1)}, f32[48,128]{1,0:T(8,128)S(1)}, u32[]{:S(2)}, u32[]{:S(2)}) collective-permute-start(f32[48,128]{1,0:T(8,128)S(1)} %get-tuple-element.21), channel_id=1, source_target_pairs={{0,8},{8,16},{16,24},{1,9},{9,17},{17,25},{2,10},{10,18},{18,26},{... | collective-permute-start | bytes 73736 | tf_op jit(solution)/shard_map/ppermute | solution.py:805
  37.6 4.8 %collective-permute-start.3 = (f32[48,128]{1,0:T(8,128)S(1)}, f32[48,128]{1,0:T(8,128)S(1)}, u32[]{:S(2)}, u32[]{:S(2)}) collective-permute-start(f32[48,128]{1,0:T(8,128)S(1)} %get-tuple-element.22), channel_id=1, source_target_pairs={{8,0},{16,8},{24,16},{9,1},{17,9},{25,17},{10,2},{18,10},{26,18},{... | collective-permute-start | bytes 73736 | tf_op jit(solution)/shard_map/ppermute | solution.py:806
  55.2 17.7 %all-to-all-start.2 = ((f32[32,1,2176]{2,1,0:T(1,128)}), f32[32,1,2176]{2,1,0:T(1,128)S(1)}, u32[]{:S(2)}, u32[]{:S(2)}) async-start(f32[32,1,2176]{2,1,0:T(1,128)} %bitcast.7), calls=%async_computation.2 | async-start | bytes 557056 | tf_op jit(solution)/shard_map/all_to_all | solution.py:859
